TPU v7x, 32 devices: a whole 2x2x4 slice. The times are simulated.
32 devices in a mesh: gx: 2 (over x), gy: 4 (over y, core), gz: 4 (over z).
Axes of the slice: x: 2, y: 2, z: 4, core: 2. Of those that a mesh axis runs over, the one named last changes fastest.
Arguments:
- charges: bfloat16 [8, 16, 16, 32, 128], P('gx', 'gy', 'gz'), may hold values from -6 to 6
- counts: int32 [8, 16, 16], P('gx', 'gy', 'gz'), may hold values from 32 to 128, as said below
- near_offsets: int32 [27, 3], replicated, may hold values from -1 to 1, as said below
- near_blocks: bfloat16 [27, 128, 128], replicated, may hold values from -0.109375 to 0.109375
- leaf_basis: bfloat16 [48, 128], replicated, may hold values from -0.5 to 0.5
- transfer: bfloat16 [8, 48, 48], replicated, may hold values from -0.625 to 0.625
- far_offsets: int32 [2, 32, 3], replicated, may hold values from -2 to 2, as said below
- coupling: bfloat16 [2, 32, 48, 48], replicated, may hold values from -0.15625 to 0.15625
- coarse_coupling: bfloat16 [2, 4, 4, 48, 48], replicated, may hold values from -0.3125 to 0.3125
Outputs:
- potentials: float32 [8, 16, 16, 32, 128], P('gx', 'gy', 'gz')
Inputs may be any that keep to these rules, and one draw needn't show every extreme that they name: `counts`: in each device's block of 4 x 4 x 4 leaf boxes some box holds 128 points. `near_offsets`: each of the 27 offsets with components in -1, 0, 1 appears once. `far_offsets`: each level lists 32 distinct offsets whose largest component in magnitude is 2.
All inputs are finite; a program needn't handle non-finite values.
Results may differ from a plain program's by a relative error of at most 0.008.
Values may be sent and summed in bfloat16 or wider, within the bound.
No kernel may reach another device: no remote copies, remote signals or barrier semaphores. Data moves between devices by JAX's collectives and lax.ppermute only.
A program may use at most 128 MiB of HBM per device.

v0:
```python
import functools

import jax
import jax.numpy as jnp
from jax import lax
from jax.experimental import pallas as pl
from jax.experimental.pallas import tpu as pltpu
from jax.sharding import PartitionSpec as P


F32 = jnp.float32
BF16 = jnp.bfloat16


def from_shift(value, axis, size, shift):
    return lax.ppermute(value, axis, [(i, (i - shift) % size) for i in range(size)])


def spec_vmem():
    return pl.BlockSpec(memory_space=pltpu.VMEM)


def spec_smem():
    return pl.BlockSpec(memory_space=pltpu.SMEM)


def run(kernel, out_shape, args, smem=(), hbm=(), scratch=(), flops=None, limit=8):
    def spec(i):
        if i in hbm:
            return pl.BlockSpec(memory_space=pltpu.HBM)
        return spec_smem() if i in smem else spec_vmem()

    cost = None
    if flops is not None:
        cost = pl.CostEstimate(flops=flops, transcendentals=0, bytes_accessed=0)
    return pl.pallas_call(
        kernel,
        out_shape=out_shape,
        in_specs=[spec(i) for i in range(len(args))],
        out_specs=jax.tree.map(lambda _: spec_vmem(), out_shape),
        scratch_shapes=scratch,
        compiler_params=pltpu.CompilerParams(vmem_limit_bytes=limit * 1024 * 1024),
        cost_estimate=cost,
    )(*args)


def lane_blocks(rows, width):
    return lax.broadcasted_iota(jnp.int32, (rows, 128), 1) // width


def roll(value, shift):
    shift = shift % 128
    return value if shift == 0 else pltpu.roll(value, shift, 1)


def dot(a, b, dims=((1,), (0,))):
    return lax.dot_general(a, b, (dims, ((), ())), preferred_element_type=F32)


def assemble(sources, width, load):
    per = 128 // width
    out = []
    for start in range(0, len(sources), per):
        total = None
        for d, (key, b) in enumerate(sources[start : start + per]):
            moved = roll(load(key).astype(F32), width * (d - b))
            if total is None:
                total = moved
                blocks = lane_blocks(moved.shape[0], width)
            else:
                total = jnp.where(blocks == d, moved, total)
        out.append(total.astype(BF16))
    return out


def tile_at(ref, start, rank):
    return ref[start : start + rank, :]


def first_kernel(counts_in, charges_in, basis_in, transfer_in, own, z_high, z_low, mom, y_high, y_low, counts, charges, basis, transfer, sems):
    bx, by, bz, rhs, pts = charges.shape
    rank = basis.shape[0]
    width = rhs
    copies = [
        pltpu.make_async_copy(counts_in, counts, sems.at[0]),
        pltpu.make_async_copy(basis_in, basis, sems.at[1]),
        pltpu.make_async_copy(transfer_in, transfer, sems.at[2]),
    ]
    parts = [pltpu.make_async_copy(charges_in.at[x], charges.at[x], sems.at[3 + x]) for x in range(bx)]
    for c in copies[:1] + parts + copies[1:]:
        c.start()
    lane = lax.broadcasted_iota(jnp.int32, (rhs, pts), 1)
    copies[0].wait()
    for x in range(bx):
        parts[x].wait()
        for y in range(by):
            for z in range(bz):
                keep = lane < counts[x, y, z]
                value = jnp.where(keep, charges[x, y, z].astype(F32), 0.0).astype(BF16)
                own[z, y, x] = value
                if z == 0:
                    z_low[y, x] = value
                if z == bz - 1:
                    z_high[y, x] = value
                at = (z * bx + x) * rhs
                if y == 0:
                    y_low[at : at + rhs] = value
                if y == by - 1:
                    y_high[at : at + rhs] = value
    copies[1].wait()
    copies[2].wait()
    base = bz * bx * rhs
    leaf = {}
    for z in range(bz):
        for y in range(0, by, 2):
            rows = own[z, y : y + 2].reshape(2 * bx * rhs, pts)
            value = dot(basis[...], rows, ((1,), (1,))).astype(BF16)
            for k in range(2):
                leaf[z, y + k] = value[:, 128 * k : 128 * (k + 1)]
                mom[z * by + y + k] = leaf[z, y + k]
                at = base + (z * 2 + k) * rank
                (y_low if y == 0 else y_high)[at : at + rank] = leaf[z, y + k]
    sums = [None, None]
    for i in range(2):
        for j in range(2):
            for l in range(2):
                cols = jnp.concatenate([leaf[2 * z + l, 2 * y + j] for z in range(2) for y in range(2)], axis=1)
                part = dot(transfer[4 * i + 2 * j + l], cols)
                sums[i] = part if sums[i] is None else sums[i] + part
    blocks = lane_blocks(rank, width)
    first = bz * by
    one = []
    for z in range(2):
        whole = []
        for y in range(2):
            at = 128 * (z * 2 + y)
            whole.append(sums[0][:, at : at + 128] + roll(sums[1][:, at : at + 128], -width))
        packed = jnp.where(
            blocks == 0,
            whole[0],
            jnp.where(
                blocks == 1,
                roll(whole[0], -width),
                jnp.where(blocks == 2, roll(whole[1], 2 * width), roll(whole[1], width)),
            ),
        ).astype(BF16)
        one.append(packed)
        mom[first + z] = packed
        at = base + (2 * bz + z) * rank
        y_high[at : at + rank] = packed
        y_low[at : at + rank] = packed
    two = None
    for j in range(2):
        for i in range(2):
            part = dot(transfer[4 * i + 2 * j], one[0]) + dot(transfer[4 * i + 2 * j + 1], one[1])
            part = roll(part, -width * (2 * j + i))
            two = part if two is None else two + part
    mom[first + 2] = two.astype(BF16)


def second_kernel(geo, *refs):
    nx, xs, bx, by, bz, rhs, rank = (geo[k] for k in ("nx", "xs", "bx", "by", "bz", "rhs", "rank"))
    it = iter(refs)

    def take(count):
        return [next(it) for _ in range(count)]

    own, prev, nxt = take(3)
    sources = take(xs)
    far = take(geo["extra_x"])
    x_high, x_low, z_high, z_low, y_high, y_low, two = take(7)
    leaf = bz * by
    at = 0
    for s in sources:
        for z in range(2):
            for y in range(by):
                z_high[at] = s[(bz - 2 + z) * by + y]
                z_low[at] = s[z * by + y]
                at += 1
    for s in sources:
        for z in range(2):
            z_high[at] = s[leaf + z]
            z_low[at] = s[leaf + z]
            at += 1

    def load(key):
        if key == 0:
            return sources[0][leaf + 2]
        if key == 1:
            return sources[xs - 1][leaf + 2]
        if key == nx - 1:
            return sources[1][leaf + 2]
        return far[key - 2][...]

    for t, tile in enumerate(assemble([(k, 0) for k in range(nx)], rhs, load)):
        z_high[at + t] = tile
        z_low[at + t] = tile
        two[t] = tile
    for y in range(by):
        for out, x in ((x_high, bx - 1), (x_low, 0)):
            out[0, y] = prev[y, x]
            out[bz + 1, y] = nxt[y, x]
            for z in range(bz):
                out[z + 1, y] = own[z, y, x]
    for out, y in ((y_high, by - 1), (y_low, 0)):
        for k, s in enumerate((prev, nxt)):
            for x in range(bx):
                at = (k * bx + x) * rhs
                out[at : at + rhs] = s[y, x]
    base = 2 * bx * rhs
    for out, start in ((y_high, by - 2), (y_low, 0)):
        for k in range(1, xs):
            for z in range(bz):
                for y in range(2):
                    at = base + (((k - 1) * bz + z) * 2 + y) * rank
                    out[at : at + rank] = sources[k][z * by + start + y]
            for z in range(2):
                at = base + ((xs - 1) * bz * 2 + (k - 1) * 2 + z) * rank
                out[at : at + rank] = sources[k][leaf + z]


def third_kernel(geo, *refs):
    nx, nz, xs, _, by, bz, rhs, rank = (geo[k] for k in ("nx", "nz", "xs", "bx", "by", "bz", "rhs", "rank"))
    it = iter(refs)

    def take(count):
        return [next(it) for _ in range(count)]

    before, after, prev, nxt, mine = take(5)
    far = take(geo["extra_z"])
    y_high, y_low, two = take(3)
    for out, y in ((y_high, by - 1), (y_low, 0)):
        for k, s in enumerate((before, after)):
            for z in range(bz + 2):
                at = (k * (bz + 2) + z) * rhs
                out[at : at + rhs] = s[z, y]
    base = 2 * (bz + 2) * rhs
    for out, start in ((y_high, by - 2), (y_low, 0)):
        for k in range(xs):
            for zh in range(4):
                s = prev if zh < 2 else nxt
                for y in range(2):
                    at = base + ((k * 4 + zh) * 2 + y) * rank
                    out[at : at + rank] = s[(k * 2 + zh % 2) * by + start + y]
            for side, s in enumerate((prev, nxt)):
                for z in range(2):
                    at = base + (xs * 8 + (k * 2 + side) * 2 + z) * rank
                    out[at : at + rank] = s[xs * 2 * by + k * 2 + z]
    first = xs * 2 * by + xs * 2
    per = 128 // rhs
    order = [((s, b // per), b % per) for s in range(nz) for b in range(nx)]

    def load(key):
        s, t = key
        if s == 0:
            return mine[t]
        if s == 1:
            return nxt[first + t]
        if s == nz - 1:
            return prev[first + t]
        return far[s - 2][t]

    for t, tile in enumerate(assemble(order, rhs, load)):
        at = base + (xs * 12 + t) * rank
        y_high[at : at + rank] = tile
        y_low[at : at + rank] = tile
        two[t] = tile


def near_weights(inverse, near_blocks, codes):
    return jnp.concatenate([near_blocks[inverse[c]] for c in codes], axis=1)


def find_inverse(table, inverse, count):
    for s in range(count):
        ox, oy, oz = (table[d, s] + 1 for d in range(3))
        inverse[(ox * 3 + oy) * 3 + oz] = s


def near_kernel(geo, table, near_blocks, own, cz_prev, cz_next, cx_prev, cx_next, *refs):
    bx, by, bz, rhs = (geo[k] for k in ("bx", "by", "bz", "rhs"))
    y1, y2, (out, wide, inverse) = refs[0:2], refs[2:4], refs[4:]
    pts = wide.shape[3]
    stencil = near_blocks.shape[0]
    find_inverse(table, inverse, stencil)
    zero = jnp.zeros((rhs, pts), BF16)
    for z in range(bz + 2):
        for y in (0, by + 1):
            k = 0 if y == 0 else 1
            if z == 0:
                middle = y2[k][0 : bx * rhs]
            elif z == bz + 1:
                middle = y2[k][bx * rhs : 2 * bx * rhs]
            else:
                middle = y1[k][(z - 1) * bx * rhs : z * bx * rhs]
            wide[z, y, 0:rhs] = zero
            wide[z, y, rhs : (bx + 1) * rhs] = middle
            wide[z, y, (bx + 1) * rhs :] = zero
        for y in range(1, by + 1):
            if z == 0:
                middle = cz_prev[y - 1]
            elif z == bz + 1:
                middle = cz_next[y - 1]
            else:
                middle = own[z - 1, y - 1]
            wide[z, y, 0:rhs] = cx_prev[z, y - 1]
            wide[z, y, rhs : (bx + 1) * rhs] = middle.reshape(bx * rhs, pts)
            wide[z, y, (bx + 1) * rhs :] = cx_next[z, y - 1]
    weights = near_weights(inverse, near_blocks, range(stencil))

    def step(number, carry):
        z = number // (by // 2)
        y = number % (by // 2) * 2
        windows = []
        for ox in range(3):
            for oy in range(3):
                for oz in range(3):
                    window = wide[z + oz, pl.ds(y + oy, 2), ox * rhs : (ox + bx) * rhs, :]
                    windows.append(window.reshape(2 * bx * rhs, pts))
        out[number] = dot(jnp.concatenate(windows, axis=1), weights, ((1,), (1,)))
        return carry

    lax.fori_loop(0, bz * by // 2, step, 0)


def weight_kernel(coupling_in, coarse_in, transfer, coupling, coarse, down_one, down_zero):
    entries, rank = coupling_in.shape[1:3]
    for level in range(2):
        coupling[level] = jnp.concatenate([coupling_in[level, e] for e in range(entries)], axis=1)
    nx, ny, nz = coarse_in.shape[:3]
    coarse[...] = jnp.concatenate(
        [coarse_in[x, y, z] for y in range(ny) for z in range(nz) for x in range(nx)], axis=1
    )
    turned = [transfer[c].astype(F32).T.astype(BF16) for c in range(8)]
    for c in range(8):
        down_one[c * rank : (c + 1) * rank] = turned[c]
    for k in range(4):
        down_zero[k] = jnp.concatenate([turned[k], turned[4 + k]], axis=1)


def final_kernel(geo, *refs):
    nx, ny, nz, xs, bx, by, bz, rhs, rank = (
        geo[k] for k in ("nx", "ny", "nz", "xs", "bx", "by", "bz", "rhs", "rank")
    )
    width = rhs
    it = iter(refs)

    def take(count):
        return [next(it) for _ in range(count)]

    counts, near_table, far_table = take(3)
    near, near_blocks, basis, coupling, coarse, down_one, down_zero = take(7)
    sources = take(xs)
    mz_prev, mz_next = take(2)
    y1, y2, y3 = take(2), take(2), take(2)
    (mine_two,) = take(1)
    far_two = take(geo["extra_y"])
    (out,) = take(1)
    shifts, ones, columns, local, corners, inverse = take(6)
    pts = basis.shape[1]
    leaf = bz * by
    blocks = lane_blocks(rank, width)
    stencil = near_blocks.shape[0]
    entries = coupling.shape[2] // rank
    base1 = bz * bx * rhs
    base2 = 2 * bx * rhs
    base3 = 2 * (bz + 2) * rhs

    def far_offset(level, e):
        return [far_table[d, level, e] + 2 for d in range(3)]

    find_inverse(near_table, inverse, stencil)
    for oy, yk in ((0, 0), (2, 1)):
        for ox, xk in ((0, 0), (2, 1)):
            weights = near_weights(inverse, near_blocks, [(ox * 3 + oy) * 3 + oz for oz in range(3)])
            windows = []
            for oz in range(3):
                at = (xk * (bz + 2) + oz) * rhs
                windows.append(y3[yk][at : at + bz * rhs])
            corners[yk, xk] = dot(jnp.concatenate(windows, axis=1), weights, ((1,), (1,)))

    def leaf_tile(k, z, y):
        if 0 <= y < by:
            if z < 0:
                return mz_prev[k * 2 * by + (z + 2) * by + y]
            if z >= bz:
                return mz_next[k * 2 * by + (z - bz) * by + y]
            return sources[k][z * by + y]
        side, yy = (0, y + 2) if y < 0 else (1, y - by)
        if not 0 <= z < bz:
            zh = z + 2 if z < 0 else z - bz + 2
            return tile_at(y3[side], base3 + ((k * 4 + zh) * 2 + yy) * rank, rank)
        if k == 0:
            return tile_at(y1[side], base1 + (z * 2 + yy) * rank, rank)
        return tile_at(y2[side], base2 + (((k - 1) * bz + z) * 2 + yy) * rank, rank)

    for z in range(-2, bz + 2):
        for y in range(-2, by + 2):
            mid = leaf_tile(0, z, y)
            shifts[2, z + 2, y + 2] = mid
            mid = mid.astype(F32)
            before = leaf_tile(1, z, y).astype(F32)
            after = before if xs == 2 else leaf_tile(2, z, y).astype(F32)
            shifts[0, z + 2, y + 2] = roll(jnp.where(blocks >= 2, before, mid), 2 * width).astype(BF16)
            shifts[1, z + 2, y + 2] = roll(jnp.where(blocks >= 3, before, mid), width).astype(BF16)
            shifts[3, z + 2, y + 2] = roll(jnp.where(blocks < 1, after, mid), -width).astype(BF16)
            shifts[4, z + 2, y + 2] = roll(jnp.where(blocks < 2, after, mid), -2 * width).astype(BF16)

    def one_tile(k, zb, z, yb):
        if yb == 1:
            if zb == 1:
                return sources[k][leaf + z]
            return (mz_prev if zb == 0 else mz_next)[xs * 2 * by + k * 2 + z]
        side = yb // 2
        if zb != 1:
            return tile_at(y3[side], base3 + (xs * 8 + (k * 2 + zb // 2) * 2 + z) * rank, rank)
        if k == 0:
            return tile_at(y1[side], base1 + (2 * bz + z) * rank, rank)
        return tile_at(y2[side], base2 + ((xs - 1) * bz * 2 + (k - 1) * 2 + z) * rank, rank)

    odd = blocks % 2 == 1
    upper = blocks >= 2

    def swap(value):
        return jnp.where(odd, roll(value, width), roll(value, -width))

    for zb in range(3):
        for z in range(2):
            rows = []
            for yb in range(3):
                mid = one_tile(0, zb, z, yb).astype(F32)
                before = one_tile(1, zb, z, yb).astype(F32)
                after = before if xs == 2 else one_tile(2, zb, z, yb).astype(F32)
                rows.append([
                    before,
                    swap(jnp.where(odd, before, mid)),
                    mid,
                    swap(jnp.where(odd, mid, after)),
                    after,
                ])
            for k in range(5):
                low, mid, high = (rows[yb][k] for yb in range(3))
                group = [
                    low,
                    roll(jnp.where(upper, low, mid), 2 * width),
                    mid,
                    roll(jnp.where(upper, mid, high), 2 * width),
                    high,
                ]
                for m in range(5):
                    ones[k, m, 2 * zb + z] = group[m].astype(BF16)

    first = base3 + xs * 12 * rank
    per = 128 // width

    def two_tile(s, t):
        if s == 0:
            return mine_two[t]
        if s == 1 or s == ny - 1:
            return tile_at(y3[1 if s == 1 else 0], first + t * rank, rank)
        return far_two[s - 2][t]

    stacked = []
    for s in range(ny):
        for b in range(nz * nx):
            tile = two_tile(s, b // per).astype(F32)
            stacked.append(jnp.where(blocks == b % per, tile, 0.0).astype(BF16))
    two = dot(coarse[...], jnp.concatenate(stacked, axis=0))
    two = two + roll(two, 2 * width)
    two = (two + roll(two, width)).astype(BF16)

    for e in range(entries):
        ox, oy, oz = far_offset(1, e)
        for z in range(2):
            columns[0, e * rank : (e + 1) * rank, 128 * z : 128 * (z + 1)] = ones[ox, oy, z + oz]
    local_one = dot(coupling[1], columns[0])
    from_two = dot(down_one[...], two)
    ups = []
    for z in range(2):
        total = local_one[:, 128 * z : 128 * (z + 1)]
        for j in range(2):
            for i in range(2):
                child = 4 * i + 2 * j + z
                part = from_two[child * rank : (child + 1) * rank]
                total = total + jnp.where(blocks == 2 * j + i, part, 0.0)
        total = total.astype(BF16).astype(F32)
        half = roll(total, 2 * width)
        for up in (
            jnp.where(blocks == 0, total, jnp.where(blocks == 3, half, roll(total, width))),
            jnp.where(blocks == 0, half, jnp.where(blocks == 3, total, roll(total, -width))),
        ):
            ups.append(
                jnp.concatenate(
                    [jnp.where(odd, 0.0, up).astype(BF16), jnp.where(odd, up, 0.0).astype(BF16)], axis=0
                )
            )
    ups = jnp.concatenate(ups, axis=1)
    for j in range(2):
        for l in range(2):
            part = dot(down_zero[2 * j + l], ups)
            for z in range(2):
                for y in range(2):
                    at = 128 * (2 * z + y)
                    local[2 * z + l, 2 * y + j] = part[:, at : at + 128]

    lane = lax.broadcasted_iota(jnp.int32, (rhs, pts), 1)

    def step(z, carry):
        for half in range(by // 2):
            y = 2 * half
            for e in range(entries):
                ox, oy, oz = far_offset(0, e)
                for k in range(2):
                    columns[half, e * rank : (e + 1) * rank, 128 * k : 128 * (k + 1)] = shifts[ox, z + oz, y + oy + k]
            total = dot(coupling[0], columns[half])
            total = total + jnp.concatenate([local[z, y], local[z, y + 1]], axis=1)
            result = dot(total.astype(BF16), basis[...], ((0,), (0,))) + near[z * (by // 2) + half]
            for k in range(2):
                for x in range(bx):
                    at = (k * bx + x) * rhs
                    value = result[at : at + rhs]
                    if y + k in (0, by - 1) and x in (0, bx - 1):
                        start = pl.multiple_of(z * rhs, rhs)
                        value = value + corners[0 if y + k == 0 else 1, 0 if x == 0 else 1, pl.ds(start, rhs), :]
                    keep = lane < counts[x, y + k, z]
                    out[x, y + k, z] = jnp.where(keep, value, 0.0)
        return carry

    lax.fori_loop(0, bz, step, 0)


def body(charges, counts, near_offsets, near_blocks, leaf_basis, transfer, far_offsets, coupling, coarse_coupling):
    bx, by, bz, rhs, pts = charges.shape
    rank = leaf_basis.shape[0]
    entries = far_offsets.shape[1]
    stencil = near_blocks.shape[0]
    nx, ny, nz = (lax.axis_size(a) for a in ("gx", "gy", "gz"))
    assert (bx, by, bz) == (4, 4, 4) and bx * rhs == 128 and pts == 128
    xs = 2 if nx == 2 else 3
    geo = dict(nx=nx, ny=ny, nz=nz, xs=xs, bx=bx, by=by, bz=bz, rhs=rhs, rank=rank)
    geo["extra_x"] = max(nx - 3, 0)
    geo["extra_z"] = max(nz - 3, 0)
    geo["extra_y"] = max(ny - 3, 0)
    per = 128 // rhs
    tiles_x = -(-nx // per)
    tiles_z = -(-nx * nz // per)

    def shape(*dims, dtype=BF16):
        return jax.ShapeDtypeStruct(dims, dtype)

    def part(kernel):
        return functools.partial(kernel, geo)

    near_table = near_offsets.T
    far_table = far_offsets.transpose(2, 0, 1)

    face = shape(by, bx, rhs, pts)
    message = shape(bz * bx * rhs + (bz * 2 + 2) * rank, 128)
    own, z_high, z_low, mom, y_high, y_low = run(
        first_kernel,
        (shape(bz, by, bx, rhs, pts), face, face, shape(bz * by + 3, rank, 128), message, message),
        (counts, charges, leaf_basis, transfer),
        hbm=(0, 1, 2, 3),
        scratch=[
            pltpu.SMEM(counts.shape, jnp.int32),
            pltpu.VMEM(charges.shape, BF16),
            pltpu.VMEM(leaf_basis.shape, BF16),
            pltpu.VMEM(transfer.shape, BF16),
            pltpu.SemaphoreType.DMA((3 + bx,)),
        ],
    )
    cz_prev = from_shift(z_high, "gz", nz, -1)
    cz_next = from_shift(z_low, "gz", nz, 1)
    if nx == 2:
        sources = [mom, from_shift(mom, "gx", nx, 1)]
    else:
        sources = [mom, from_shift(mom, "gx", nx, -1), from_shift(mom, "gx", nx, 1)]
    extra = [from_shift(mom[bz * by + 2], "gx", nx, s) for s in range(2, nx - 1)]
    y1 = [from_shift(y_high, "gy", ny, -1), from_shift(y_low, "gy", ny, 1)]

    weights = run(
        weight_kernel,
        (
            shape(2, rank, entries * rank),
            shape(rank, nx * ny * nz * rank),
            shape(8 * rank, rank),
            shape(4, rank, 2 * rank),
        ),
        (coupling, coarse_coupling, transfer),
    )

    charge = shape(bz + 2, by, rhs, pts)
    moment = shape(xs * 2 * by + xs * 2 + tiles_x, rank, 128)
    message = shape(2 * bx * rhs + (xs - 1) * (bz * 2 + 2) * rank, 128)
    x_high, x_low, z_high, z_low, y_high, y_low, two_x = run(
        part(second_kernel),
        (charge, charge, moment, moment, message, message, shape(tiles_x, rank, 128)),
        (own, cz_prev, cz_next, *sources, *extra),
    )
    cx_prev = from_shift(x_high, "gx", nx, -1)
    cx_next = from_shift(x_low, "gx", nx, 1)
    mz_prev = from_shift(z_high, "gz", nz, -1)
    mz_next = from_shift(z_low, "gz", nz, 1)
    extra = [from_shift(two_x, "gz", nz, s) for s in range(2, nz - 1)]
    y2 = [from_shift(y_high, "gy", ny, -1), from_shift(y_low, "gy", ny, 1)]

    message = shape(2 * (bz + 2) * rhs + (xs * 12 + tiles_z) * rank, 128)
    y_high, y_low, two_z = run(
        part(third_kernel),
        (message, message, shape(tiles_z, rank, 128)),
        (cx_prev, cx_next, mz_prev, mz_next, two_x, *extra),
    )
    y3 = [from_shift(y_high, "gy", ny, -1), from_shift(y_low, "gy", ny, 1)]
    extra = [from_shift(two_z, "gy", ny, s) for s in range(2, ny - 1)]

    near = run(
        part(near_kernel),
        shape(bz * by // 2, 2 * bx * rhs, pts, dtype=F32),
        (near_table, near_blocks, own, cz_prev, cz_next, cx_prev, cx_next, *y1, *y2),
        smem=(0,),
        scratch=[
            pltpu.VMEM((bz + 2, by + 2, (bx + 2) * rhs, pts), BF16),
            pltpu.SMEM((stencil,), jnp.int32),
        ],
        limit=16,
        flops=2 * bx * by * bz * rhs * pts * pts * stencil,
    )
    return run(
        part(final_kernel),
        shape(bx, by, bz, rhs, pts, dtype=F32),
        (
            counts,
            near_table,
            far_table,
            near,
            near_blocks,
            leaf_basis,
            *weights,
            *sources,
            mz_prev,
            mz_next,
            *y1,
            *y2,
            *y3,
            two_z,
            *extra,
        ),
        smem=(0, 1, 2),
        limit=24,
        scratch=[
            pltpu.VMEM((5, bz + 4, by + 4, rank, 128), BF16),
            pltpu.VMEM((5, 5, 6, rank, 128), BF16),
            pltpu.VMEM((by // 2, entries * rank, 256), BF16),
            pltpu.VMEM((bz, by, rank, 128), F32),
            pltpu.VMEM((2, 2, bz * rhs, pts), F32),
            pltpu.SMEM((stencil,), jnp.int32),
        ],
    )


def solution(mesh):
    in_specs = (
        P("gx", "gy", "gz", None, None),
        P("gx", "gy", "gz"),
        P(),
        P(),
        P(),
        P(),
        P(),
        P(),
        P(),
    )
    out_specs = P("gx", "gy", "gz", None, None)

    return jax.shard_map(body, mesh=mesh, in_specs=in_specs, out_specs=out_specs, check_vma=False)
```

profile of v0, /device:TPU:0, one launch (start us, length us, event | category | flops | bytes accessed | tf_op | source)
XLA Modules:
  0.0 67.0 jit_solution(16147372475414515925)
XLA Ops:
  0.0 0.0 copy-start.2
  0.0 1.0 %copy-done.2 = bf16[4,4,4,32,128]{4,3,2,1,0:T(8,128)(2,1)S(1)} copy-done((bf16[4,4,4,32,128]{4,3,2,1,0:T(8,128)(2,1)S(1)}, bf16[4,4,4,32,128]{4,3,2,1,0:T(8,128)(2,1)}, u32[]{:S(2)}) %copy-start.2) | copy-done | bytes 524312
  1.0 0.0 copy-start.3
  1.0 0.9 %copy-done.3 = bf16[8,48,48]{2,1,0:T(8,128)(2,1)S(1)} copy-done((bf16[8,48,48]{2,1,0:T(8,128)(2,1)S(1)}, bf16[8,48,48]{2,1,0:T(8,128)(2,1)}, u32[]{:S(2)}) %copy-start.3) | copy-done | bytes 36888
  1.9 0.0 copy-start.6
  1.9 0.7 %copy-done.6 = bf16[48,128]{1,0:T(8,128)(2,1)S(1)} copy-done((bf16[48,128]{1,0:T(8,128)(2,1)S(1)}, bf16[48,128]{1,0:T(8,128)(2,1)}, u32[]{:S(2)}) %copy-start.6) | copy-done | bytes 12312
  2.6 0.0 copy-start.8
  2.6 0.7 %copy-done.8 = s32[4,4,4]{2,1,0:T(4,128)S(1)} copy-done((s32[4,4,4]{2,1,0:T(4,128)S(1)}, s32[4,4,4]{2,1,0:T(4,128)}, u32[]{:S(2)}) %copy-start.8) | copy-done | bytes 280
  3.3 1.9 %shard_map.91 = (bf16[4,4,4,32,128]{4,3,2,1,0:T(8,128)(2,1)S(1)}, bf16[4,4,32,128]{3,2,1,0:T(8,128)(2,1)S(1)}, bf16[4,4,32,128]{3,2,1,0:T(8,128)(2,1)S(1)}, bf16...) custom-call(s32[4,4,4]{2,1,0:T(4,128)S(1)} %copy-done.8, ...), custom_call_target="tpu_custom_call" | custom-call | tf_op jit(solution)/shard_map/pallas_call | solution.py:36
  5.2 3.0 %collective-permute-start.2 = (bf16[19,48,128]{2,1,0:T(8,128)(2,1)S(1)}, bf16[19,48,128]{2,1,0:T(8,128)(2,1)S(1)}, u32[]{:S(2)}, u32[]{:S(2)}) collective-permute-start(bf16[19,48,128]{2,1,0:T(8,128)(2,1)S(1)} %get-tuple-element.28.refs_3_.refs_10_), channel_id=1, source_target_pairs={{0,16},{16,0},{1,17},{17,1},{2,18},{18,2},{3,19},{19,3},{4,20},{20... | collective-permute-start | bytes 700424 | tf_op jit(solution)/shard_map/ppermute | solution.py:16
  8.3 1.6 %collective-permute-start = (bf16[4,4,32,128]{3,2,1,0:T(8,128)(2,1)S(1)}, bf16[4,4,32,128]{3,2,1,0:T(8,128)(2,1)S(1)}, u32[]{:S(2)}, u32[]{:S(2)}) collective-permute-start(bf16[4,4,32,128]{3,2,1,0:T(8,128)(2,1)S(1)} %get-tuple-element.26), channel_id=1, source_target_pairs={{0,1},{1,2},{2,3},{3,0},{4,5},{5,6},{6,7},{7,4},{8,9},{9,10},{10,1... | collective-permute-start | bytes 393224 | tf_op jit(solution)/shard_map/ppermute | solution.py:16
  9.8 2.3 %collective-permute-start.1 = (bf16[4,4,32,128]{3,2,1,0:T(8,128)(2,1)S(1)}, bf16[4,4,32,128]{3,2,1,0:T(8,128)(2,1)S(1)}, u32[]{:S(2)}, u32[]{:S(2)}) collective-permute-start(bf16[4,4,32,128]{3,2,1,0:T(8,128)(2,1)S(1)} %get-tuple-element.27), channel_id=1, source_target_pairs={{0,3},{1,0},{2,1},{3,2},{4,7},{5,4},{6,5},{7,6},{8,11},{9,8},{10,9... | collective-permute-start | bytes 393224 | tf_op jit(solution)/shard_map/ppermute | solution.py:16
  12.1 4.3 %collective-permute-done.refs_1_.cz_prev = bf16[4,4,32,128]{3,2,1,0:T(8,128)(2,1)S(1)} collective-permute-done((bf16[4,4,32,128]{3,2,1,0:T(8,128)(2,1)S(1)}, bf16[4,4,32,128]{3,2,1,0:T(8,128)(2,1)S(1)}, u32[]{:S(2)}, u32[]{:S(2)}) %collective-permute-start) | collective-permute-done | bytes 131104 | tf_op jit(solution)/shard_map/ppermute | solution.py:16
  16.4 0.9 %collective-permute-done.1.refs_2_.cz_next = bf16[4,4,32,128]{3,2,1,0:T(8,128)(2,1)S(1)} collective-permute-done((bf16[4,4,32,128]{3,2,1,0:T(8,128)(2,1)S(1)}, bf16[4,4,32,128]{3,2,1,0:T(8,128)(2,1)S(1)}, u32[]{:S(2)}, u32[]{:S(2)}) %collective-permute-start.1) | collective-permute-done | bytes 131104 | tf_op jit(solution)/shard_map/ppermute | solution.py:16
  17.3 0.0 collective-permute-done.2.refs_4_.refs_11_
  17.3 0.0 copy-start.5
  17.3 0.1 shard_map.92
  17.5 0.0 copy-start.1
  17.5 1.2 %collective-permute-start.9 = (bf16[21,48,128]{2,1,0:T(8,128)(2,1)S(1)}, bf16[21,48,128]{2,1,0:T(8,128)(2,1)S(1)}, u32[]{:S(2)}, u32[]{:S(2)}) collective-permute-start(bf16[21,48,128]{2,1,0:T(8,128)(2,1)S(1)} %get-tuple-element.39), channel_id=1, source_target_pairs={{0,1},{1,2},{2,3},{3,0},{4,5},{5,6},{6,7},{7,4},{8,9},{9,10},{10,1... | collective-permute-start | bytes 774152 | tf_op jit(solution)/shard_map/ppermute | solution.py:16
  18.7 2.7 %collective-permute-start.10 = (bf16[21,48,128]{2,1,0:T(8,128)(2,1)S(1)}, bf16[21,48,128]{2,1,0:T(8,128)(2,1)S(1)}, u32[]{:S(2)}, u32[]{:S(2)}) collective-permute-start(bf16[21,48,128]{2,1,0:T(8,128)(2,1)S(1)} %get-tuple-element.40), channel_id=1, source_target_pairs={{0,3},{1,0},{2,1},{3,2},{4,7},{5,4},{6,5},{7,6},{8,11},{9,8},{10,9... | collective-permute-start | bytes 774152 | tf_op jit(solution)/shard_map/ppermute | solution.py:16
  21.4 0.0 collective-permute-start.11
  21.4 0.5 collective-permute-start.3
  21.9 1.5 %collective-permute-start.4 = (bf16[6,4,32,128]{3,2,1,0:T(8,128)(2,1)S(1)}, bf16[6,4,32,128]{3,2,1,0:T(8,128)(2,1)S(1)}, u32[]{:S(2)}, u32[]{:S(2)}) collective-permute-start(bf16[6,4,32,128]{3,2,1,0:T(8,128)(2,1)S(1)} %get-tuple-element.30), channel_id=1, source_target_pairs={{0,16},{16,0},{1,17},{17,1},{2,18},{18,2},{3,19},{19,3},{4,20},{20... | collective-permute-start | bytes 589832 | tf_op jit(solution)/shard_map/ppermute | solution.py:16
  23.4 8.7 %collective-permute-done.11.refs_5_ = bf16[1,48,128]{2,1,0:T(8,128)(2,1)S(1)} collective-permute-done((bf16[1,48,128]{2,1,0:T(8,128)(2,1)S(1)}, bf16[1,48,128]{2,1,0:T(8,128)(2,1)S(1)}, u32[]{:S(2)}, u32[]{:S(2)}) %collective-permute-start.11) | collective-permute-done | bytes 12320 | tf_op jit(solution)/shard_map/ppermute | solution.py:16
  32.1 0.0 collective-permute-start.5
  32.1 0.0 collective-permute-done.3.cx_prev.refs_0_
  32.1 0.0 copy-start.4
  32.1 0.0 copy-start
  32.1 1.7 %collective-permute-start.6 = (bf16[992,128]{1,0:T(8,128)(2,1)S(1)}, bf16[992,128]{1,0:T(8,128)(2,1)S(1)}, u32[]{:S(2)}, u32[]{:S(2)}) collective-permute-start(bf16[992,128]{1,0:T(8,128)(2,1)S(1)} %get-tuple-element.32), channel_id=1, source_target_pairs={{0,12},{4,0},{8,4},{12,8},{1,13},{5,1},{9,5},{13,9},{2,14},{6,2},{... | collective-permute-start | bytes 761864 | tf_op jit(solution)/shard_map/ppermute | solution.py:16
  33.8 0.0 collective-permute-done.4.cx_next.refs_1_
  33.8 0.0 collective-permute-done.9.refs_2_.refs_12_
  33.8 0.0 collective-permute-done.10.refs_3_.refs_13_
  33.8 0.1 shard_map.95
  33.9 0.1 collective-permute-start.12
  34.0 1.7 %collective-permute-start.13 = (bf16[1632,128]{1,0:T(8,128)(2,1)S(1)}, bf16[1632,128]{1,0:T(8,128)(2,1)S(1)}, u32[]{:S(2)}, u32[]{:S(2)}) collective-permute-start(bf16[1632,128]{1,0:T(8,128)(2,1)S(1)} %get-tuple-element.43), channel_id=1, source_target_pairs={{0,12},{4,0},{8,4},{12,8},{1,13},{5,1},{9,5},{13,9},{2,14},{6,2},{... | collective-permute-start | bytes 1253384 | tf_op jit(solution)/shard_map/ppermute | solution.py:16
  35.7 0.0 collective-permute-start.7
  35.7 2.9 %collective-permute-done.5.refs_0_.refs_14_ = bf16[992,128]{1,0:T(8,128)(2,1)S(1)} collective-permute-done((bf16[992,128]{1,0:T(8,128)(2,1)S(1)}, bf16[992,128]{1,0:T(8,128)(2,1)S(1)}, u32[]{:S(2)}, u32[]{:S(2)}) %collective-permute-start.5) | collective-permute-done | bytes 253984 | tf_op jit(solution)/shard_map/ppermute | solution.py:16
  38.7 0.0 collective-permute-start.8
  38.7 0.0 copy-done.5
  38.7 0.0 copy-done.1
  38.7 0.0 copy-done.4
  38.7 0.4 shard_map.94
  39.1 0.0 copy-start.11
  39.1 1.2 %collective-permute-done.6.refs_1_.refs_15_ = bf16[992,128]{1,0:T(8,128)(2,1)S(1)} collective-permute-done((bf16[992,128]{1,0:T(8,128)(2,1)S(1)}, bf16[992,128]{1,0:T(8,128)(2,1)S(1)}, u32[]{:S(2)}, u32[]{:S(2)}) %collective-permute-start.6) | collective-permute-done | bytes 253984 | tf_op jit(solution)/shard_map/ppermute | solution.py:16
  40.3 1.5 %collective-permute-start.14 = (bf16[2,48,128]{2,1,0:T(8,128)(2,1)S(1)}, bf16[2,48,128]{2,1,0:T(8,128)(2,1)S(1)}, u32[]{:S(2)}, u32[]{:S(2)}) collective-permute-start(bf16[2,48,128]{2,1,0:T(8,128)(2,1)S(1)} %get-tuple-element.44.refs_20_), channel_id=1, source_target_pairs={{0,8},{4,12},{8,0},{12,4},{1,9},{5,13},{9,1},{13,5},{2,10},{6,14},... | collective-permute-start | bytes 73736 | tf_op jit(solution)/shard_map/ppermute | solution.py:16
  41.9 9.8 %collective-permute-done.7.refs_2_.refs_16_ = bf16[736,128]{1,0:T(8,128)(2,1)S(1)} collective-permute-done((bf16[736,128]{1,0:T(8,128)(2,1)S(1)}, bf16[736,128]{1,0:T(8,128)(2,1)S(1)}, u32[]{:S(2)}, u32[]{:S(2)}) %collective-permute-start.7) | collective-permute-done | bytes 188448 | tf_op jit(solution)/shard_map/ppermute | solution.py:16
  51.7 1.1 %collective-permute-done.8.refs_3_.refs_17_ = bf16[736,128]{1,0:T(8,128)(2,1)S(1)} collective-permute-done((bf16[736,128]{1,0:T(8,128)(2,1)S(1)}, bf16[736,128]{1,0:T(8,128)(2,1)S(1)}, u32[]{:S(2)}, u32[]{:S(2)}) %collective-permute-start.8) | collective-permute-done | bytes 188448 | tf_op jit(solution)/shard_map/ppermute | solution.py:16
  52.8 0.0 copy-done
  52.8 0.0 copy-done.11
  52.8 0.0 copy-start.7
  52.8 0.0 copy-start.10
  52.8 5.9 %shard_map.93.refs_3_ = f32[8,256,128]{2,1,0:T(8,128)S(1)} custom-call(s32[3,27]{1,0:T(4,128)S(1)} %bitcast.3, bf16[27,128,128]{2,1,0:T(8,128)(2,1)S(1)} %copy-done, bf16[4,4,4,32,128]{4,3,2,1,0:T(8,128)(2,1)S(1)} %get-tuple-element.25.refs_0_.own, bf16[4,4,32,128]{3,2,1,0:T(8,128)(2,1)S(1)} %collective-permute-done.refs_1_.cz_prev, ...), custom_call_target="tpu_custom_call" | custom-call | flops 1811939328 | tf_op jit(solution)/shard_map/pallas_call | solution.py:36
  58.7 0.0 copy-start.9
  58.7 0.0 collective-permute-done.14.refs_21_
  58.7 0.0 collective-permute-done.12.refs_18_
  58.7 0.0 collective-permute-done.13.refs_19_
  58.8 0.0 copy-done.7
  58.8 0.0 copy-done.10
  58.8 0.6 copy-done.9
  59.4 7.6 %shard_map.96 = f32[4,4,4,32,128]{4,3,2,1,0:T(8,128)} custom-call(s32[4,4,4]{2,1,0:T(4,128)S(1)} %copy-done.9, s32[3,27]{1,0:T(4,128)S(1)} %bitcast.4, s32[3,2,32]{2,1,0:T(2,128)S(1)} %bitcast.2, f32[8,256,128]{2,1,0:T(8,128)S(1)} %shard_map.93.refs_3_, bf16[27,128,128]{2,1,0:T(8,128)(2,1)S(1)} %copy-done, bf16[48,128]{1,0:T(8,128)(2,1)S(1)} %copy-done.7, ...), custom_call_target="tpu_custom_call" | custom-call | tf_op jit(solution)/shard_map/pallas_call | solution.py:36
Async XLA Ops:
  0.0 1.0 %copy-start.2 = (bf16[4,4,4,32,128]{4,3,2,1,0:T(8,128)(2,1)S(1)}, bf16[4,4,4,32,128]{4,3,2,1,0:T(8,128)(2,1)}, u32[]{:S(2)}) copy-start(bf16[4,4,4,32,128]{4,3,2,1,0:T(8,128)(2,1)} %charges_in.1) | copy-start | bytes 1572868
  1.0 0.9 %copy-start.3 = (bf16[8,48,48]{2,1,0:T(8,128)(2,1)S(1)}, bf16[8,48,48]{2,1,0:T(8,128)(2,1)}, u32[]{:S(2)}) copy-start(bf16[8,48,48]{2,1,0:T(8,128)(2,1)} %transfer.1) | copy-start | bytes 110596
  1.9 0.7 %copy-start.6 = (bf16[48,128]{1,0:T(8,128)(2,1)S(1)}, bf16[48,128]{1,0:T(8,128)(2,1)}, u32[]{:S(2)}) copy-start(bf16[48,128]{1,0:T(8,128)(2,1)} %refs_5_.1) | copy-start | bytes 36868
  2.6 0.7 %copy-start.8 = (s32[4,4,4]{2,1,0:T(4,128)S(1)}, s32[4,4,4]{2,1,0:T(4,128)}, u32[]{:S(2)}) copy-start(s32[4,4,4]{2,1,0:T(4,128)} %refs_0_.1) | copy-start | bytes 772
  5.2 12.1 %collective-permute-start.2 = (bf16[19,48,128]{2,1,0:T(8,128)(2,1)S(1)}, bf16[19,48,128]{2,1,0:T(8,128)(2,1)S(1)}, u32[]{:S(2)}, u32[]{:S(2)}) collective-permute-start(bf16[19,48,128]{2,1,0:T(8,128)(2,1)S(1)} %get-tuple-element.28.refs_3_.refs_10_), channel_id=1, source_target_pairs={{0,16},{16,0},{1,17},{17,1},{2,18},{18,2},{3,19},{19,3},{4,20},{20... | collective-permute-start | bytes 700424 | tf_op jit(solution)/shard_map/ppermute | solution.py:16
  8.3 8.2 %collective-permute-start = (bf16[4,4,32,128]{3,2,1,0:T(8,128)(2,1)S(1)}, bf16[4,4,32,128]{3,2,1,0:T(8,128)(2,1)S(1)}, u32[]{:S(2)}, u32[]{:S(2)}) collective-permute-start(bf16[4,4,32,128]{3,2,1,0:T(8,128)(2,1)S(1)} %get-tuple-element.26), channel_id=1, source_target_pairs={{0,1},{1,2},{2,3},{3,0},{4,5},{5,6},{6,7},{7,4},{8,9},{9,10},{10,1... | collective-permute-start | bytes 393224 | tf_op jit(solution)/shard_map/ppermute | solution.py:16
  9.8 7.5 %collective-permute-start.1 = (bf16[4,4,32,128]{3,2,1,0:T(8,128)(2,1)S(1)}, bf16[4,4,32,128]{3,2,1,0:T(8,128)(2,1)S(1)}, u32[]{:S(2)}, u32[]{:S(2)}) collective-permute-start(bf16[4,4,32,128]{3,2,1,0:T(8,128)(2,1)S(1)} %get-tuple-element.27), channel_id=1, source_target_pairs={{0,3},{1,0},{2,1},{3,2},{4,7},{5,4},{6,5},{7,6},{8,11},{9,8},{10,9... | collective-permute-start | bytes 393224 | tf_op jit(solution)/shard_map/ppermute | solution.py:16
  17.3 21.3 %copy-start.5 = (bf16[2,4,4,48,48]{4,3,2,1,0:T(8,128)(2,1)S(1)}, bf16[2,4,4,48,48]{4,3,2,1,0:T(8,128)(2,1)}, u32[]{:S(2)}) copy-start(bf16[2,4,4,48,48]{4,3,2,1,0:T(8,128)(2,1)} %coarse_in.1) | copy-start | bytes 442372
  17.5 21.2 %copy-start.1 = (bf16[2,32,48,48]{3,2,1,0:T(8,128)(2,1)S(1)}, bf16[2,32,48,48]{3,2,1,0:T(8,128)(2,1)}, u32[]{:S(2)}) copy-start(bf16[2,32,48,48]{3,2,1,0:T(8,128)(2,1)} %coupling_in.1) | copy-start | bytes 884740
  17.5 16.4 %collective-permute-start.9 = (bf16[21,48,128]{2,1,0:T(8,128)(2,1)S(1)}, bf16[21,48,128]{2,1,0:T(8,128)(2,1)S(1)}, u32[]{:S(2)}, u32[]{:S(2)}) collective-permute-start(bf16[21,48,128]{2,1,0:T(8,128)(2,1)S(1)} %get-tuple-element.39), channel_id=1, source_target_pairs={{0,1},{1,2},{2,3},{3,0},{4,5},{5,6},{6,7},{7,4},{8,9},{9,10},{10,1... | collective-permute-start | bytes 774152 | tf_op jit(solution)/shard_map/ppermute | solution.py:16
  18.7 15.2 %collective-permute-start.10 = (bf16[21,48,128]{2,1,0:T(8,128)(2,1)S(1)}, bf16[21,48,128]{2,1,0:T(8,128)(2,1)S(1)}, u32[]{:S(2)}, u32[]{:S(2)}) collective-permute-start(bf16[21,48,128]{2,1,0:T(8,128)(2,1)S(1)} %get-tuple-element.40), channel_id=1, source_target_pairs={{0,3},{1,0},{2,1},{3,2},{4,7},{5,4},{6,5},{7,6},{8,11},{9,8},{10,9... | collective-permute-start | bytes 774152 | tf_op jit(solution)/shard_map/ppermute | solution.py:16
  21.4 10.7 %collective-permute-start.11 = (bf16[1,48,128]{2,1,0:T(8,128)(2,1)S(1)}, bf16[1,48,128]{2,1,0:T(8,128)(2,1)S(1)}, u32[]{:S(2)}, u32[]{:S(2)}) collective-permute-start(bf16[1,48,128]{2,1,0:T(8,128)(2,1)S(1)} %get-tuple-element.41.refs_4_), channel_id=1, source_target_pairs={{0,2},{1,3},{2,0},{3,1},{4,6},{5,7},{6,4},{7,5},{8,10},{9,11},{10,... | collective-permute-start | bytes 36872 | tf_op jit(solution)/shard_map/ppermute | solution.py:16
  21.4 10.7 %collective-permute-start.3 = (bf16[6,4,32,128]{3,2,1,0:T(8,128)(2,1)S(1)}, bf16[6,4,32,128]{3,2,1,0:T(8,128)(2,1)S(1)}, u32[]{:S(2)}, u32[]{:S(2)}) collective-permute-start(bf16[6,4,32,128]{3,2,1,0:T(8,128)(2,1)S(1)} %get-tuple-element.29), channel_id=1, source_target_pairs={{0,16},{16,0},{1,17},{17,1},{2,18},{18,2},{3,19},{19,3},{4,20},{20... | collective-permute-start | bytes 589832 | tf_op jit(solution)/shard_map/ppermute | solution.py:16
  21.9 11.9 %collective-permute-start.4 = (bf16[6,4,32,128]{3,2,1,0:T(8,128)(2,1)S(1)}, bf16[6,4,32,128]{3,2,1,0:T(8,128)(2,1)S(1)}, u32[]{:S(2)}, u32[]{:S(2)}) collective-permute-start(bf16[6,4,32,128]{3,2,1,0:T(8,128)(2,1)S(1)} %get-tuple-element.30), channel_id=1, source_target_pairs={{0,16},{16,0},{1,17},{17,1},{2,18},{18,2},{3,19},{19,3},{4,20},{20... | collective-permute-start | bytes 589832 | tf_op jit(solution)/shard_map/ppermute | solution.py:16
  32.1 6.6 %collective-permute-start.5 = (bf16[992,128]{1,0:T(8,128)(2,1)S(1)}, bf16[992,128]{1,0:T(8,128)(2,1)S(1)}, u32[]{:S(2)}, u32[]{:S(2)}) collective-permute-start(bf16[992,128]{1,0:T(8,128)(2,1)S(1)} %get-tuple-element.31), channel_id=1, source_target_pairs={{0,4},{4,8},{8,12},{12,0},{1,5},{5,9},{9,13},{13,1},{2,6},{6,10},{... | collective-permute-start | bytes 761864 | tf_op jit(solution)/shard_map/ppermute | solution.py:16
  32.1 6.6 %copy-start.4 = (bf16[8,48,48]{2,1,0:T(8,128)(2,1)S(1)}, bf16[8,48,48]{2,1,0:T(8,128)(2,1)}, u32[]{:S(2)}) copy-start(bf16[8,48,48]{2,1,0:T(8,128)(2,1)} %transfer.1) | copy-start | bytes 110596
  32.1 20.7 %copy-start = (bf16[27,128,128]{2,1,0:T(8,128)(2,1)S(1)}, bf16[27,128,128]{2,1,0:T(8,128)(2,1)}, u32[]{:S(2)}) copy-start(bf16[27,128,128]{2,1,0:T(8,128)(2,1)} %refs_4_.1) | copy-start | bytes 2654212
  32.1 8.3 %collective-permute-start.6 = (bf16[992,128]{1,0:T(8,128)(2,1)S(1)}, bf16[992,128]{1,0:T(8,128)(2,1)S(1)}, u32[]{:S(2)}, u32[]{:S(2)}) collective-permute-start(bf16[992,128]{1,0:T(8,128)(2,1)S(1)} %get-tuple-element.32), channel_id=1, source_target_pairs={{0,12},{4,0},{8,4},{12,8},{1,13},{5,1},{9,5},{13,9},{2,14},{6,2},{... | collective-permute-start | bytes 761864 | tf_op jit(solution)/shard_map/ppermute | solution.py:16
  33.9 24.8 %collective-permute-start.12 = (bf16[1632,128]{1,0:T(8,128)(2,1)S(1)}, bf16[1632,128]{1,0:T(8,128)(2,1)S(1)}, u32[]{:S(2)}, u32[]{:S(2)}) collective-permute-start(bf16[1632,128]{1,0:T(8,128)(2,1)S(1)} %get-tuple-element.42), channel_id=1, source_target_pairs={{0,4},{4,8},{8,12},{12,0},{1,5},{5,9},{9,13},{13,1},{2,6},{6,10},{... | collective-permute-start | bytes 1253384 | tf_op jit(solution)/shard_map/ppermute | solution.py:16
  34.0 24.8 %collective-permute-start.13 = (bf16[1632,128]{1,0:T(8,128)(2,1)S(1)}, bf16[1632,128]{1,0:T(8,128)(2,1)S(1)}, u32[]{:S(2)}, u32[]{:S(2)}) collective-permute-start(bf16[1632,128]{1,0:T(8,128)(2,1)S(1)} %get-tuple-element.43), channel_id=1, source_target_pairs={{0,12},{4,0},{8,4},{12,8},{1,13},{5,1},{9,5},{13,9},{2,14},{6,2},{... | collective-permute-start | bytes 1253384 | tf_op jit(solution)/shard_map/ppermute | solution.py:16
  35.7 15.9 %collective-permute-start.7 = (bf16[736,128]{1,0:T(8,128)(2,1)S(1)}, bf16[736,128]{1,0:T(8,128)(2,1)S(1)}, u32[]{:S(2)}, u32[]{:S(2)}) collective-permute-start(bf16[736,128]{1,0:T(8,128)(2,1)S(1)} %get-tuple-element.33), channel_id=1, source_target_pairs={{0,4},{4,8},{8,12},{12,0},{1,5},{5,9},{9,13},{13,1},{2,6},{6,10},{... | collective-permute-start | bytes 565256 | tf_op jit(solution)/shard_map/ppermute | solution.py:16
  38.7 14.1 %collective-permute-start.8 = (bf16[736,128]{1,0:T(8,128)(2,1)S(1)}, bf16[736,128]{1,0:T(8,128)(2,1)S(1)}, u32[]{:S(2)}, u32[]{:S(2)}) collective-permute-start(bf16[736,128]{1,0:T(8,128)(2,1)S(1)} %get-tuple-element.34), channel_id=1, source_target_pairs={{0,12},{4,0},{8,4},{12,8},{1,13},{5,1},{9,5},{13,9},{2,14},{6,2},{... | collective-permute-start | bytes 565256 | tf_op jit(solution)/shard_map/ppermute | solution.py:16
  39.1 13.7 %copy-start.11 = (s32[27,3]{0,1:T(4,128)S(1)}, s32[27,3]{0,1:T(4,128)}, u32[]{:S(2)}) copy-start(s32[27,3]{0,1:T(4,128)} %param.11) | copy-start | bytes 976
  40.3 18.4 %collective-permute-start.14 = (bf16[2,48,128]{2,1,0:T(8,128)(2,1)S(1)}, bf16[2,48,128]{2,1,0:T(8,128)(2,1)S(1)}, u32[]{:S(2)}, u32[]{:S(2)}) collective-permute-start(bf16[2,48,128]{2,1,0:T(8,128)(2,1)S(1)} %get-tuple-element.44.refs_20_), channel_id=1, source_target_pairs={{0,8},{4,12},{8,0},{12,4},{1,9},{5,13},{9,1},{13,5},{2,10},{6,14},... | collective-permute-start | bytes 73736 | tf_op jit(solution)/shard_map/ppermute | solution.py:16
  52.8 6.0 %copy-start.7 = (bf16[48,128]{1,0:T(8,128)(2,1)S(1)}, bf16[48,128]{1,0:T(8,128)(2,1)}, u32[]{:S(2)}) copy-start(bf16[48,128]{1,0:T(8,128)(2,1)} %refs_5_.1) | copy-start | bytes 36868
  52.8 6.0 %copy-start.10 = (s32[2,32,3]{1,0,2:T(2,128)S(1)}, s32[2,32,3]{1,0,2:T(2,128)}, u32[]{:S(2)}) copy-start(s32[2,32,3]{1,0,2:T(2,128)} %param.15) | copy-start | bytes 2308
  58.7 0.7 %copy-start.9 = (s32[4,4,4]{2,1,0:T(4,128)S(1)}, s32[4,4,4]{2,1,0:T(4,128)}, u32[]{:S(2)}) copy-start(s32[4,4,4]{2,1,0:T(4,128)} %refs_0_.1) | copy-start | bytes 772
where the time goes:
time: 67.6 us; the launch traced here: 67 us
  waiting for transfers between devices  29 us (43%)
  starting transfers between devices  17.8 us (26%)
  Pallas kernels  16 us (24%)
  local copies, waits for them, and re-layouts  4.01 us (6%)
    ppermute x15, waiting for transfers between devices, from_shift(): lax.ppermute(value, axis, [(i, (i - shift) % size) for i in range(size)])  29 us
    ppermute x15, starting transfers between devices, from_shift(): lax.ppermute(value, axis, [(i, (i - shift) % size) for i in range(size)])  17.8 us
    pallas_call x6, Pallas kernels, run(): pl.pallas_call(kernel, out_shape=out_shape, in_specs=[spec(i) for i in ra...  16 us
    unnamed x24, local copies, waits for them, and re-layouts  4.01 us
  transfers between devices with their start and end apart: 15, of which 7 were waited for; matrix products, arithmetic and copies ran while one was open for 0% of the time, Pallas kernels for 10%

commit v1 on v0

v1 whole, which is shorter than its diff:
```python
import functools

import jax
import jax.numpy as jnp
from jax import lax
from jax.experimental import pallas as pl
from jax.experimental.pallas import tpu as pltpu
from jax.sharding import PartitionSpec as P


F32 = jnp.float32
BF16 = jnp.bfloat16


def from_shift(value, axis, size, shift):
    return lax.ppermute(value, axis, [(i, (i - shift) % size) for i in range(size)])


def spec_vmem():
    return pl.BlockSpec(memory_space=pltpu.VMEM)


def spec_smem():
    return pl.BlockSpec(memory_space=pltpu.SMEM)


def run(kernel, out_shape, args, smem=(), hbm=(), scratch=(), flops=None, limit=8, hbm_out=(), aliases=None):
    def spec(i):
        if i in hbm:
            return pl.BlockSpec(memory_space=pltpu.HBM)
        return spec_smem() if i in smem else spec_vmem()

    cost = None
    if flops is not None:
        cost = pl.CostEstimate(flops=flops, transcendentals=0, bytes_accessed=0)
    count = len(out_shape) if isinstance(out_shape, tuple) else 1
    outs = tuple(pl.BlockSpec(memory_space=pltpu.HBM) if i in hbm_out else spec_vmem() for i in range(count))
    return pl.pallas_call(
        kernel,
        out_shape=out_shape,
        in_specs=[spec(i) for i in range(len(args))],
        out_specs=outs if isinstance(out_shape, tuple) else outs[0],
        input_output_aliases=aliases or {},
        scratch_shapes=scratch,
        compiler_params=pltpu.CompilerParams(vmem_limit_bytes=limit * 1024 * 1024),
        cost_estimate=cost,
    )(*args)


def lane_blocks(rows, width):
    return lax.broadcasted_iota(jnp.int32, (rows, 128), 1) // width


def roll(value, shift):
    shift = shift % 128
    return value if shift == 0 else pltpu.roll(value, shift, 1)


def dot(a, b, dims=((1,), (0,))):
    return lax.dot_general(a, b, (dims, ((), ())), preferred_element_type=F32)


def assemble(sources, width, load):
    per = 128 // width
    out = []
    for start in range(0, len(sources), per):
        total = None
        for d, (key, b) in enumerate(sources[start : start + per]):
            moved = roll(load(key).astype(F32), width * (d - b))
            if total is None:
                total = moved
                blocks = lane_blocks(moved.shape[0], width)
            else:
                total = jnp.where(blocks == d, moved, total)
        out.append(total.astype(BF16))
    return out


def tile_at(ref, start, rank):
    return ref[start : start + rank, :]


def start_kernel(out):
    out[...] = jnp.zeros(out.shape, out.dtype)


def first_kernel(token, counts_in, charges_in, basis_in, transfer_in, own, faces, mom, z_high, z_low, y_high, y_low, two, counts, charges, basis, transfer, sems):
    bx, by, bz, rhs, pts = charges.shape
    rank = basis.shape[0]
    width = rhs
    copies = [
        pltpu.make_async_copy(counts_in, counts, sems.at[0]),
        pltpu.make_async_copy(basis_in, basis, sems.at[1]),
        pltpu.make_async_copy(transfer_in, transfer, sems.at[2]),
    ]
    parts = [pltpu.make_async_copy(charges_in.at[x], charges.at[x], sems.at[3 + x]) for x in range(bx)]
    for c in copies[:1] + parts + copies[1:]:
        c.start()
    lane = lax.broadcasted_iota(jnp.int32, (rhs, pts), 1)
    copies[0].wait()
    for x in range(bx):
        parts[x].wait()
        for y in range(by):
            for z in range(bz):
                keep = lane < counts[x, y, z]
                value = jnp.where(keep, charges[x, y, z].astype(F32), 0.0).astype(BF16)
                own[z, y, x] = value
                if x == 0:
                    faces[0, z, y] = value
                if x == bx - 1:
                    faces[1, z, y] = value
                at = (z * bx + x) * rhs
                if y == 0:
                    y_low[at : at + rhs] = value
                if y == by - 1:
                    y_high[at : at + rhs] = value
    copies[1].wait()
    copies[2].wait()
    base = bz * bx * rhs
    leaf = {}
    for z in range(bz):
        for y in range(0, by, 2):
            rows = own[z, y : y + 2].reshape(2 * bx * rhs, pts)
            value = dot(basis[...], rows, ((1,), (1,))).astype(BF16)
            for k in range(2):
                tile = value[:, 128 * k : 128 * (k + 1)]
                leaf[z, y + k] = tile
                mom[z * by + y + k] = tile
                (z_low if z < 2 else z_high)[z % 2 * by + y + k] = tile
                at = base + (z * 2 + k) * rank
                (y_low if y == 0 else y_high)[at : at + rank] = tile
    sums = [None, None]
    for i in range(2):
        for j in range(2):
            for l in range(2):
                cols = jnp.concatenate([leaf[2 * z + l, 2 * y + j] for z in range(2) for y in range(2)], axis=1)
                part = dot(transfer[4 * i + 2 * j + l], cols)
                sums[i] = part if sums[i] is None else sums[i] + part
    blocks = lane_blocks(rank, width)
    first = bz * by
    one = []
    for z in range(2):
        whole = []
        for y in range(2):
            at = 128 * (z * 2 + y)
            whole.append(sums[0][:, at : at + 128] + roll(sums[1][:, at : at + 128], -width))
        packed = jnp.where(
            blocks == 0,
            whole[0],
            jnp.where(
                blocks == 1,
                roll(whole[0], -width),
                jnp.where(blocks == 2, roll(whole[1], 2 * width), roll(whole[1], width)),
            ),
        ).astype(BF16)
        one.append(packed)
        mom[first + z] = packed
        z_high[2 * by + z] = packed
        z_low[2 * by + z] = packed
        at = base + (2 * bz + z) * rank
        y_high[at : at + rank] = packed
        y_low[at : at + rank] = packed
    total = None
    for j in range(2):
        for i in range(2):
            part = dot(transfer[4 * i + 2 * j], one[0]) + dot(transfer[4 * i + 2 * j + 1], one[1])
            part = roll(part, -width * (2 * j + i))
            total = part if total is None else total + part
    total = total.astype(BF16)
    z_high[2 * by + 2] = total
    z_low[2 * by + 2] = total
    two[0] = total


class Reader:
    def __init__(self, refs):
        self.refs = iter(refs)

    def take(self, count):
        return [next(self.refs) for _ in range(count)]

    def faces(self, geo):
        if geo["nx"] == 2:
            (both,) = self.take(1)
            return both.at[1], both.at[0]
        before, after = self.take(2)
        return before.at[0], after.at[0]


def second_kernel(geo, *refs):
    nz, bx, by, bz, rhs, rank = (geo[k] for k in ("nz", "bx", "by", "bz", "rhs", "rank"))
    read = Reader(refs)
    (own,) = read.take(1)
    before, after = read.faces(geo)
    mom, prev, nxt, mine = read.take(4)
    far = read.take(geo["extra_z"])
    c_high, c_low, wide, y_high, y_low = read.take(5)
    leaf = bz * by
    for z in range(bz + 4):
        for y in range(by):
            if z < 2:
                tile = prev[z * by + y]
            elif z >= bz + 2:
                tile = nxt[(z - bz - 2) * by + y]
            else:
                tile = mom[(z - 2) * by + y]
            wide[z * by + y] = tile
    first = (bz + 4) * by
    for z in range(2):
        wide[first + z] = prev[2 * by + z]
        wide[first + 2 + z] = mom[leaf + z]
        wide[first + 4 + z] = nxt[2 * by + z]

    def load(key):
        if key == 0:
            return mine[0]
        if key == 1:
            return nxt[2 * by + 2]
        if key == nz - 1:
            return prev[2 * by + 2]
        return far[key - 2][0]

    for t, tile in enumerate(assemble([(k, 0) for k in range(nz)], rhs, load)):
        wide[first + 6 + t] = tile
    for out, z in ((c_high, bz - 1), (c_low, 0)):
        for y in range(by):
            out[y, 0] = before[z, y]
            out[y, 1 : bx + 1] = own[z, y]
            out[y, bx + 1] = after[z, y]
    base = 2 * bz * rhs
    for out, y in ((y_high, by - 1), (y_low, 0)):
        for k, s in enumerate((before, after)):
            for z in range(bz):
                at = (k * bz + z) * rhs
                out[at : at + rhs] = s[z, y]
        start = by - 2 if y else 0
        for zh in range(4):
            s = prev if zh < 2 else nxt
            for yy in range(2):
                at = base + (zh * 2 + yy) * rank
                out[at : at + rank] = s[zh % 2 * by + start + yy]
        for side, s in enumerate((prev, nxt)):
            for z in range(2):
                at = base + (8 + side * 2 + z) * rank
                out[at : at + rank] = s[2 * by + z]


def third_kernel(geo, *refs):
    nx, nz, xs, bx, by, bz, rhs, rank = (geo[k] for k in ("nx", "nz", "xs", "bx", "by", "bz", "rhs", "rank"))
    read = Reader(refs)
    prev, nxt = read.take(2)
    sources = read.take(xs)
    far = read.take(geo["extra_x"])
    y_high, y_low, two = read.take(3)
    base = 2 * (bx + 2) * rhs
    first = (bz + 4) * by
    for out, y in ((y_high, by - 1), (y_low, 0)):
        for k, s in enumerate((prev, nxt)):
            at = k * (bx + 2) * rhs
            out[at : at + (bx + 2) * rhs] = s[y].reshape((bx + 2) * rhs, s.shape[3])
        start = by - 2 if y else 0
        for k in range(1, xs):
            for z in range(bz + 4):
                for yy in range(2):
                    at = base + (((k - 1) * (bz + 4) + z) * 2 + yy) * rank
                    out[at : at + rank] = sources[k][z * by + start + yy]
            for z in range(6):
                at = base + ((xs - 1) * (bz + 4) * 2 + (k - 1) * 6 + z) * rank
                out[at : at + rank] = sources[k][first + z]
    per = 128 // rhs
    order = [((s, b // per), b % per) for s in range(nx) for b in range(nz)]

    def load(key):
        s, t = key
        if s == 0:
            return sources[0][first + 6 + t]
        if s == 1:
            return sources[xs - 1][first + 6 + t]
        if s == nx - 1:
            return sources[1][first + 6 + t]
        return far[s - 2][t]

    for t, tile in enumerate(assemble(order, rhs, load)):
        at = base + ((xs - 1) * (2 * (bz + 4) + 6) + t) * rank
        y_high[at : at + rank] = tile
        y_low[at : at + rank] = tile
        two[t] = tile


def near_weights(inverse, near_blocks, codes):
    return jnp.concatenate([near_blocks[inverse[c]] for c in codes], axis=1)


def find_inverse(table, inverse, count):
    for s in range(count):
        ox, oy, oz = (table[d, s] + 1 for d in range(3))
        inverse[(ox * 3 + oy) * 3 + oz] = s


def store_windows(shifts, at, stride, blocks, width, mid, before, after):
    shifts[2 * stride + at] = mid
    mid = mid.astype(F32)
    same = before is after
    before = before.astype(F32)
    after = before if same else after.astype(F32)
    shifts[at] = roll(jnp.where(blocks >= 2, before, mid), 2 * width).astype(BF16)
    shifts[stride + at] = roll(jnp.where(blocks >= 3, before, mid), width).astype(BF16)
    shifts[3 * stride + at] = roll(jnp.where(blocks < 1, after, mid), -width).astype(BF16)
    shifts[4 * stride + at] = roll(jnp.where(blocks < 2, after, mid), -2 * width).astype(BF16)


def near_kernel(geo, *refs):
    xs, bx, by, bz, rhs, rank = (geo[k] for k in ("xs", "bx", "by", "bz", "rhs", "rank"))
    read = Reader(refs)
    table, near_blocks, own = read.take(3)
    before, after = read.faces(geo)
    cz_prev, cz_next = read.take(2)
    y1, y2 = read.take(2), read.take(2)
    sources = read.take(xs)
    out, shifts, wide, inverse = read.take(4)
    pts = wide.shape[3]
    stencil = near_blocks.shape[0]
    find_inverse(table, inverse, stencil)
    rows = (bx + 2) * rhs
    for z in range(bz + 2):
        outer = z in (0, bz + 1)
        for k, y in enumerate((0, by + 1)):
            if outer:
                wide[z, y] = jnp.zeros((rows, pts), BF16)
                continue
            at = (z - 1) * rhs
            wide[z, y, 0:rhs] = y2[k][at : at + rhs]
            wide[z, y, rhs : rows - rhs] = y1[k][bx * at : bx * (at + rhs)]
            wide[z, y, rows - rhs :] = y2[k][bz * rhs + at : bz * rhs + at + rhs]
        for y in range(1, by + 1):
            if outer:
                wide[z, y] = (cz_prev if z == 0 else cz_next)[y - 1].reshape(rows, pts)
                continue
            wide[z, y, 0:rhs] = before[z - 1, y - 1]
            wide[z, y, rhs : rows - rhs] = own[z - 1, y - 1].reshape(bx * rhs, pts)
            wide[z, y, rows - rhs :] = after[z - 1, y - 1]
    weights = near_weights(inverse, near_blocks, range(stencil))

    def step(number, carry):
        z = number // (by // 2)
        y = number % (by // 2) * 2
        windows = []
        for ox in range(3):
            for oy in range(3):
                for oz in range(3):
                    window = wide[z + oz, pl.ds(y + oy, 2), ox * rhs : (ox + bx) * rhs, :]
                    windows.append(window.reshape(2 * bx * rhs, pts))
        out[number] = dot(jnp.concatenate(windows, axis=1), weights, ((1,), (1,)))
        return carry

    lax.fori_loop(0, bz * by // 2, step, 0)
    blocks = lane_blocks(rank, rhs)
    for z in range(bz + 4):
        for y in range(by):
            tiles = [s[z * by + y] for s in sources]
            store_windows(
                shifts, z * (by + 4) + y + 2, (bz + 4) * (by + 4), blocks, rhs, tiles[0], tiles[1], tiles[-1]
            )


def weight_kernel(coupling_in, coarse_in, transfer, coupling, coarse, down_one, down_zero):
    entries, rank = coupling_in.shape[1:3]
    for level in range(2):
        coupling[level] = jnp.concatenate([coupling_in[level, e] for e in range(entries)], axis=1)
    nx, ny, nz = coarse_in.shape[:3]
    coarse[...] = jnp.concatenate(
        [coarse_in[x, y, z] for y in range(ny) for x in range(nx) for z in range(nz)], axis=1
    )
    turned = [transfer[c].astype(F32).T.astype(BF16) for c in range(8)]
    for c in range(8):
        down_one[c * rank : (c + 1) * rank] = turned[c]
    for k in range(4):
        down_zero[k] = jnp.concatenate([turned[k], turned[4 + k]], axis=1)


def final_kernel(geo, *refs):
    nx, ny, nz, xs, bx, by, bz, rhs, rank = (
        geo[k] for k in ("nx", "ny", "nz", "xs", "bx", "by", "bz", "rhs", "rank")
    )
    width = rhs
    read = Reader(refs)
    counts, near_table, far_table = read.take(3)
    near, near_blocks, basis, coupling, coarse, down_one, down_zero, _ = read.take(8)
    sources = read.take(xs)
    y1, y2, y3 = read.take(2), read.take(2), read.take(2)
    (mine_two,) = read.take(1)
    far_two = read.take(geo["extra_y"])
    out, shifts = read.take(2)
    ones, corners, planes, inverse, sems = read.take(5)
    pts = basis.shape[1]
    blocks = lane_blocks(rank, width)
    stencil = near_blocks.shape[0]
    entries = coupling.shape[2] // rank
    base1 = bz * bx * rhs
    base2 = 2 * bz * rhs
    base3 = 2 * (bx + 2) * rhs
    first = (bz + 4) * by

    def leaf_tile(k, z, side, yy):
        if k > 0:
            return tile_at(y3[side], base3 + (((k - 1) * (bz + 4) + z + 2) * 2 + yy) * rank, rank)
        if 0 <= z < bz:
            return tile_at(y1[side], base1 + (z * 2 + yy) * rank, rank)
        zh = z + 2 if z < 0 else z - bz + 2
        return tile_at(y2[side], base2 + (zh * 2 + yy) * rank, rank)

    for z in range(-2, bz + 2):
        for side in range(2):
            for yy in range(2):
                tiles = [leaf_tile(k, z, side, yy) for k in range(xs)]
                at = (z + 2) * (by + 4) + yy + side * (by + 2)
                store_windows(shifts, at, (bz + 4) * (by + 4), blocks, width, tiles[0], tiles[1], tiles[-1])

    def one_tile(k, zb, z, yb):
        if yb == 1:
            return sources[k][first + zb * 2 + z]
        side = yb // 2
        if k > 0:
            return tile_at(y3[side], base3 + ((xs - 1) * (bz + 4) * 2 + (k - 1) * 6 + zb * 2 + z) * rank, rank)
        if zb == 1:
            return tile_at(y1[side], base1 + (2 * bz + z) * rank, rank)
        return tile_at(y2[side], base2 + (8 + (zb // 2) * 2 + z) * rank, rank)

    odd = blocks % 2 == 1
    upper = blocks >= 2

    def swap(value):
        return jnp.where(odd, roll(value, width), roll(value, -width))

    for zb in range(3):
        for z in range(2):
            rows = []
            for yb in range(3):
                mid = one_tile(0, zb, z, yb).astype(F32)
                before = one_tile(1, zb, z, yb).astype(F32)
                after = before if xs == 2 else one_tile(2, zb, z, yb).astype(F32)
                rows.append([
                    before,
                    swap(jnp.where(odd, before, mid)),
                    mid,
                    swap(jnp.where(odd, mid, after)),
                    after,
                ])
            for k in range(5):
                low, mid, high = (rows[yb][k] for yb in range(3))
                group = [
                    low,
                    roll(jnp.where(upper, low, mid), 2 * width),
                    mid,
                    roll(jnp.where(upper, mid, high), 2 * width),
                    high,
                ]
                for m in range(5):
                    ones[(k * 5 + m) * 6 + 2 * zb + z] = group[m].astype(BF16)

    start_two = base3 + (xs - 1) * (2 * (bz + 4) + 6) * rank
    per = 128 // width

    def two_tile(s, t):
        if s == 0:
            return mine_two[t]
        if s == 1 or s == ny - 1:
            return tile_at(y3[1 if s == 1 else 0], start_two + t * rank, rank)
        return far_two[s - 2][t]

    stacked = []
    for s in range(ny):
        for b in range(nz * nx):
            tile = two_tile(s, b // per).astype(F32)
            stacked.append(jnp.where(blocks == b % per, tile, 0.0).astype(BF16))
    two = dot(coarse[...], jnp.concatenate(stacked, axis=0))
    two = two + roll(two, 2 * width)
    two = (two + roll(two, width)).astype(BF16)

    starts = []
    for e in range(entries):
        ox, oy, oz = (far_table[d, 1, e] + 2 for d in range(3))
        starts.append((ox * 5 + oy) * 6 + oz)
    columns = [jnp.concatenate([ones[s + z] for s in starts], axis=0) for z in range(2)]
    local_one = dot(coupling[1], jnp.concatenate(columns, axis=1))
    from_two = dot(down_one[...], two)
    ups = []
    for z in range(2):
        total = local_one[:, 128 * z : 128 * (z + 1)]
        for j in range(2):
            for i in range(2):
                child = 4 * i + 2 * j + z
                part = from_two[child * rank : (child + 1) * rank]
                total = total + jnp.where(blocks == 2 * j + i, part, 0.0)
        total = total.astype(BF16).astype(F32)
        half = roll(total, 2 * width)
        for up in (
            jnp.where(blocks == 0, total, jnp.where(blocks == 3, half, roll(total, width))),
            jnp.where(blocks == 0, half, jnp.where(blocks == 3, total, roll(total, -width))),
        ):
            ups.append(
                jnp.concatenate(
                    [jnp.where(odd, 0.0, up).astype(BF16), jnp.where(odd, up, 0.0).astype(BF16)], axis=0
                )
            )
    ups = jnp.concatenate(ups, axis=1)
    local = {}
    for j in range(2):
        for l in range(2):
            part = dot(down_zero[2 * j + l], ups)
            for z in range(2):
                for y in range(2):
                    at = 128 * (2 * z + y)
                    local[2 * z + l, 2 * y + j] = part[:, at : at + 128]

    find_inverse(near_table, inverse, stencil)
    for oy, yk in ((0, 0), (2, 1)):
        for oz, zk in ((0, 0), (2, 1)):
            weights = near_weights(inverse, near_blocks, [(ox * 3 + oy) * 3 + oz for ox in range(3)])
            windows = []
            for ox in range(3):
                at = (zk * (bx + 2) + ox) * rhs
                windows.append(y3[yk][at : at + bx * rhs])
            corners[yk, zk] = dot(jnp.concatenate(windows, axis=1), weights, ((1,), (1,)))

    lane = lax.broadcasted_iota(jnp.int32, (rhs, pts), 1)
    starts = []
    for e in range(entries):
        ox, oy, oz = (far_table[d, 0, e] + 2 for d in range(3))
        starts.append((ox * (bz + 4) + oz) * (by + 4) + oy)
    copies = []
    for z in range(bz):
        for half in range(by // 2):
            y = 2 * half
            columns = [
                jnp.concatenate([shifts[s + z * (by + 4) + y + k] for s in starts], axis=0) for k in range(2)
            ]
            total = dot(coupling[0], jnp.concatenate(columns, axis=1))
            total = total + jnp.concatenate([local[z, y], local[z, y + 1]], axis=1)
            result = dot(total.astype(BF16), basis[...], ((0,), (0,))) + near[z * (by // 2) + half]
            for k in range(2):
                block = result[k * bx * rhs : (k + 1) * bx * rhs]
                if y + k in (0, by - 1) and z in (0, bz - 1):
                    block = block + corners[0 if y + k == 0 else 1, 0 if z == 0 else 1]
                for x in range(bx):
                    keep = lane < counts[x, y + k, z]
                    planes[z, x, y + k] = jnp.where(keep, block[x * rhs : (x + 1) * rhs], 0.0)
        copies.append(pltpu.make_async_copy(planes.at[z], out.at[:, :, z], sems.at[z]))
        copies[-1].start()
    for c in copies:
        c.wait()


def body(charges, counts, near_offsets, near_blocks, leaf_basis, transfer, far_offsets, coupling, coarse_coupling):
    bx, by, bz, rhs, pts = charges.shape
    rank = leaf_basis.shape[0]
    entries = far_offsets.shape[1]
    stencil = near_blocks.shape[0]
    nx, ny, nz = (lax.axis_size(a) for a in ("gx", "gy", "gz"))
    assert (bx, by, bz) == (4, 4, 4) and bx * rhs == 128 and pts == 128
    xs = 2 if nx == 2 else 3
    geo = dict(nx=nx, ny=ny, nz=nz, xs=xs, bx=bx, by=by, bz=bz, rhs=rhs, rank=rank)
    geo["extra_x"] = max(nx - 3, 0)
    geo["extra_z"] = max(nz - 3, 0)
    geo["extra_y"] = max(ny - 3, 0)
    per = 128 // rhs
    tiles_z = -(-nz // per)
    tiles_x = -(-nx * nz // per)

    def shape(*dims, dtype=BF16):
        return jax.ShapeDtypeStruct(dims, dtype)

    def part(kernel):
        return functools.partial(kernel, geo)

    near_table = near_offsets.T
    far_table = far_offsets.transpose(2, 0, 1)

    token = run(start_kernel, shape(8, 128, dtype=jnp.int32), (), flops=10**10)
    side = shape(2 * by + 3, rank, 128)
    message = shape(bz * bx * rhs + (bz * 2 + 2) * rank, 128)
    own, faces, mom, z_high, z_low, y_high, y_low, two = run(
        first_kernel,
        (
            shape(bz, by, bx, rhs, pts),
            shape(2, bz, by, rhs, pts),
            shape(bz * by + 2, rank, 128),
            side,
            side,
            message,
            message,
            shape(1, rank, 128),
        ),
        (token, counts, charges, leaf_basis, transfer),
        hbm=(1, 2, 3, 4),
        scratch=[
            pltpu.SMEM(counts.shape, jnp.int32),
            pltpu.VMEM(charges.shape, BF16),
            pltpu.VMEM(leaf_basis.shape, BF16),
            pltpu.VMEM(transfer.shape, BF16),
            pltpu.SemaphoreType.DMA((3 + bx,)),
        ],
    )
    mz_prev = from_shift(z_high, "gz", nz, -1)
    mz_next = from_shift(z_low, "gz", nz, 1)
    if nx == 2:
        faces = [from_shift(faces, "gx", nx, 1)]
    else:
        faces = [from_shift(faces[1:], "gx", nx, -1), from_shift(faces[:1], "gx", nx, 1)]
    extra = [from_shift(two, "gz", nz, s) for s in range(2, nz - 1)]
    y1 = [from_shift(y_high, "gy", ny, -1), from_shift(y_low, "gy", ny, 1)]

    weights = run(
        weight_kernel,
        (
            shape(2, rank, entries * rank),
            shape(rank, nx * ny * nz * rank),
            shape(8 * rank, rank),
            shape(4, rank, 2 * rank),
        ),
        (coupling, coarse_coupling, transfer),
    )

    charge = shape(by, bx + 2, rhs, pts)
    message = shape(2 * bz * rhs + 12 * rank, 128)
    c_high, c_low, wide, y_high, y_low = run(
        part(second_kernel),
        (charge, charge, shape((bz + 4) * by + 6 + tiles_z, rank, 128), message, message),
        (own, *faces, mom, mz_prev, mz_next, two, *extra),
    )
    if nx == 2:
        sources = [wide, from_shift(wide, "gx", nx, 1)]
    else:
        sources = [wide, from_shift(wide, "gx", nx, -1), from_shift(wide, "gx", nx, 1)]
    cz_prev = from_shift(c_high, "gz", nz, -1)
    cz_next = from_shift(c_low, "gz", nz, 1)
    y2 = [from_shift(y_high, "gy", ny, -1), from_shift(y_low, "gy", ny, 1)]
    extra = [from_shift(wide[-tiles_z:], "gx", nx, s) for s in range(2, nx - 1)]

    message = shape(2 * (bx + 2) * rhs + ((xs - 1) * (2 * (bz + 4) + 6) + tiles_x) * rank, 128)
    y_high, y_low, two = run(
        part(third_kernel), (message, message, shape(tiles_x, rank, 128)), (cz_prev, cz_next, *sources, *extra)
    )
    y3 = [from_shift(y_high, "gy", ny, -1), from_shift(y_low, "gy", ny, 1)]
    extra = [from_shift(two, "gy", ny, s) for s in range(2, ny - 1)]

    windows = shape(5 * (bz + 4) * (by + 4), rank, 128)
    near, shifts = run(
        part(near_kernel),
        (shape(bz * by // 2, 2 * bx * rhs, pts, dtype=F32), windows),
        (near_table, near_blocks, own, *faces, cz_prev, cz_next, *y1, *y2, *sources),
        smem=(0,),
        scratch=[
            pltpu.VMEM((bz + 2, by + 2, (bx + 2) * rhs, pts), BF16),
            pltpu.SMEM((stencil,), jnp.int32),
        ],
        limit=16,
        flops=2 * bx * by * bz * rhs * pts * pts * stencil,
    )
    args = (
        counts,
        near_table,
        far_table,
        near,
        near_blocks,
        leaf_basis,
        *weights,
        shifts,
        *sources,
        *y1,
        *y2,
        *y3,
        two,
        *extra,
    )
    potentials, _ = run(
        part(final_kernel),
        (shape(bx, by, bz, rhs, pts, dtype=F32), windows),
        args,
        smem=(0, 1, 2),
        hbm_out=(0,),
        aliases={10: 1},
        limit=24,
        scratch=[
            pltpu.VMEM((5 * 5 * 6, rank, 128), BF16),
            pltpu.VMEM((2, 2, bx * rhs, pts), F32),
            pltpu.VMEM((bz, bx, by, rhs, pts), F32),
            pltpu.SMEM((stencil,), jnp.int32),
            pltpu.SemaphoreType.DMA((bz,)),
        ],
    )
    return potentials


def solution(mesh):
    in_specs = (
        P("gx", "gy", "gz", None, None),
        P("gx", "gy", "gz"),
        P(),
        P(),
        P(),
        P(),
        P(),
        P(),
        P(),
    )
    out_specs = P("gx", "gy", "gz", None, None)

    return jax.shard_map(body, mesh=mesh, in_specs=in_specs, out_specs=out_specs, check_vma=False)
```

time: 67.6 us -> 56.8 us (0.84)
  waiting for transfers between devices: 29 us -> 22.5 us
  local copies, waits for them, and re-layouts: 4.01 us -> 1.12 us
  Pallas kernels: 16 us -> 14.2 us
    ppermute x15 -> x14, waiting for transfers between devices: 29 us -> 22.5 us  [from_shift(): lax.ppermute(value, axis, [(i, (i - shift) % size) for i in range(size)])]
    unnamed x24 -> x18, local copies, waits for them, and re-layouts: 4.01 us -> 1.12 us
    pallas_call x6 -> x7, Pallas kernels: 16 us -> 14.2 us  [run(): pl.pallas_call(kernel, out_shape=out_shape, in_specs=[spec(i) for i in ra...]
    ppermute x15 -> x14, starting transfers between devices: 17.8 us -> 18.1 us  [from_shift(): lax.ppermute(value, axis, [(i, (i - shift) % size) for i in range(size)])]
  transfers between devices with their start and end apart: 15 -> 14, of which waited for: 7 -> 5; matrix products, arithmetic and copies ran while one was open for 0% -> 0% of each run, Pallas kernels for 10% -> 12%
where the time goes in v1:
time: 56.8 us; the launch traced here: 56.1 us
  waiting for transfers between devices  22.5 us (40%)
  starting transfers between devices  18.1 us (32%)
  Pallas kernels  14.2 us (25%)
  local copies, waits for them, and re-layouts  1.12 us (2%)
    ppermute x14, waiting for transfers between devices, from_shift(): lax.ppermute(value, axis, [(i, (i - shift) % size) for i in range(size)])  22.5 us
    ppermute x14, starting transfers between devices, from_shift(): lax.ppermute(value, axis, [(i, (i - shift) % size) for i in range(size)])  18.1 us
    pallas_call x7, Pallas kernels, run(): pl.pallas_call(kernel, out_shape=out_shape, in_specs=[spec(i) for i in ra...  14.2 us
  transfers between devices with their start and end apart: 14, of which 5 were waited for; matrix products, arithmetic and copies ran while one was open for 0% of the time, Pallas kernels for 12%

profile of v1, /device:TPU:0, one launch (start us, length us, event | category | flops | bytes accessed | tf_op | source)
XLA Modules:
  0.0 56.1 jit_solution(8447126015926674638)
XLA Ops:
  0.0 0.0 copy-start.3
  0.0 0.0 copy-start.5
  0.0 0.0 copy-start.6
  0.0 0.0 copy-start.2
  0.0 0.0 copy-start.4
  0.0 0.0 copy-start.1
  0.0 0.9 %copy-done.3 = bf16[8,48,48]{2,1,0:T(8,128)(2,1)S(1)} copy-done((bf16[8,48,48]{2,1,0:T(8,128)(2,1)S(1)}, bf16[8,48,48]{2,1,0:T(8,128)(2,1)}, u32[]{:S(2)}) %copy-start.3) | copy-done | bytes 36888
  0.9 0.0 copy-done.5
  0.9 0.0 copy-done.6
  0.9 0.2 copy-done.2
  1.1 0.0 copy-start
  1.1 0.0 copy-start.8
  1.1 1.9 %shard_map.92 = (bf16[4,4,4,32,128]{4,3,2,1,0:T(8,128)(2,1)S(1)}, bf16[2,4,4,32,128]{4,3,2,1,0:T(8,128)(2,1)S(1)}, bf16[18,48,128]{2,1,0:T(8,128)(2,1)S(1)}, bf1...) custom-call(s32[8,128]{1,0:T(8,128)S(1)} %shard_map.91.token, ...), custom_call_target="tpu_custom_call" | custom-call | tf_op jit(solution)/shard_map/pallas_call | solution.py:38
  3.1 3.0 %collective-permute-start = (bf16[2,4,4,32,128]{4,3,2,1,0:T(8,128)(2,1)S(1)}, bf16[2,4,4,32,128]{4,3,2,1,0:T(8,128)(2,1)S(1)}, u32[]{:S(2)}, u32[]{:S(2)}) collective-permute-start(bf16[2,4,4,32,128]{4,3,2,1,0:T(8,128)(2,1)S(1)} %get-tuple-element.29), channel_id=1, source_target_pairs={{0,16},{16,0},{1,17},{17,1},{2,18},{18,2},{3,19},{19,3},{4,20},{20... | collective-permute-start | bytes 786440 | tf_op jit(solution)/shard_map/ppermute | solution.py:16
  6.1 1.6 %collective-permute-start.1 = (bf16[11,48,128]{2,1,0:T(8,128)(2,1)S(1)}, bf16[11,48,128]{2,1,0:T(8,128)(2,1)S(1)}, u32[]{:S(2)}, u32[]{:S(2)}) collective-permute-start(bf16[11,48,128]{2,1,0:T(8,128)(2,1)S(1)} %get-tuple-element.31), channel_id=1, source_target_pairs={{0,1},{1,2},{2,3},{3,0},{4,5},{5,6},{6,7},{7,4},{8,9},{9,10},{10,1... | collective-permute-start | bytes 405512 | tf_op jit(solution)/shard_map/ppermute | solution.py:16
  7.7 2.2 %collective-permute-start.2 = (bf16[11,48,128]{2,1,0:T(8,128)(2,1)S(1)}, bf16[11,48,128]{2,1,0:T(8,128)(2,1)S(1)}, u32[]{:S(2)}, u32[]{:S(2)}) collective-permute-start(bf16[11,48,128]{2,1,0:T(8,128)(2,1)S(1)} %get-tuple-element.32), channel_id=1, source_target_pairs={{0,3},{1,0},{2,1},{3,2},{4,7},{5,4},{6,5},{7,6},{8,11},{9,8},{10,9... | collective-permute-start | bytes 405512 | tf_op jit(solution)/shard_map/ppermute | solution.py:16
  9.9 0.8 %collective-permute-start.3 = (bf16[1,48,128]{2,1,0:T(8,128)(2,1)S(1)}, bf16[1,48,128]{2,1,0:T(8,128)(2,1)S(1)}, u32[]{:S(2)}, u32[]{:S(2)}) collective-permute-start(bf16[1,48,128]{2,1,0:T(8,128)(2,1)S(1)} %get-tuple-element.33.refs_5_), channel_id=1, source_target_pairs={{0,2},{1,3},{2,0},{3,1},{4,6},{5,7},{6,4},{7,5},{8,10},{9,11},{10,... | collective-permute-start | bytes 36872 | tf_op jit(solution)/shard_map/ppermute | solution.py:16
  10.7 5.7 %collective-permute-done.3.refs_6_ = bf16[1,48,128]{2,1,0:T(8,128)(2,1)S(1)} collective-permute-done((bf16[1,48,128]{2,1,0:T(8,128)(2,1)S(1)}, bf16[1,48,128]{2,1,0:T(8,128)(2,1)S(1)}, u32[]{:S(2)}, u32[]{:S(2)}) %collective-permute-start.3) | collective-permute-done | bytes 12320 | tf_op jit(solution)/shard_map/ppermute | solution.py:16
  16.4 0.0 collective-permute-done.1.refs_3_
  16.4 0.0 collective-permute-done.2.refs_4_
  16.4 0.0 collective-permute-done.refs_1_.refs_3_
  16.4 0.1 shard_map.93
  16.6 0.6 %collective-permute-start.10 = (bf16[39,48,128]{2,1,0:T(8,128)(2,1)S(1)}, bf16[39,48,128]{2,1,0:T(8,128)(2,1)S(1)}, u32[]{:S(2)}, u32[]{:S(2)}) collective-permute-start(bf16[39,48,128]{2,1,0:T(8,128)(2,1)S(1)} %get-tuple-element.40.refs_10_.refs_2_.refs_11_), channel_id=1, source_target_pairs={{0,16},{16,0},{1,17},{17,1},{2,18},{18,2},{3,19},{19,3},{4,20},{20... | collective-permute-start | bytes 1437704 | tf_op jit(solution)/shard_map/ppermute | solution.py:16
  17.2 0.0 collective-permute-start.6
  17.2 0.4 collective-permute-start.4
  17.6 3.4 %collective-permute-start.5 = (bf16[4,6,32,128]{3,2,1,0:T(8,128)(2,1)S(1)}, bf16[4,6,32,128]{3,2,1,0:T(8,128)(2,1)S(1)}, u32[]{:S(2)}, u32[]{:S(2)}) collective-permute-start(bf16[4,6,32,128]{3,2,1,0:T(8,128)(2,1)S(1)} %get-tuple-element.35), channel_id=1, source_target_pairs={{0,3},{1,0},{2,1},{3,2},{4,7},{5,4},{6,5},{7,6},{8,11},{9,8},{10,9... | collective-permute-start | bytes 589832 | tf_op jit(solution)/shard_map/ppermute | solution.py:16
  21.0 1.2 %collective-permute-start.7 = (bf16[992,128]{1,0:T(8,128)(2,1)S(1)}, bf16[992,128]{1,0:T(8,128)(2,1)S(1)}, u32[]{:S(2)}, u32[]{:S(2)}) collective-permute-start(bf16[992,128]{1,0:T(8,128)(2,1)S(1)} %get-tuple-element.37), channel_id=1, source_target_pairs={{0,12},{4,0},{8,4},{12,8},{1,13},{5,1},{9,5},{13,9},{2,14},{6,2},{... | collective-permute-start | bytes 761864 | tf_op jit(solution)/shard_map/ppermute | solution.py:16
  22.2 4.0 %collective-permute-done.4.refs_4_.refs_0_ = bf16[4,6,32,128]{3,2,1,0:T(8,128)(2,1)S(1)} collective-permute-done((bf16[4,6,32,128]{3,2,1,0:T(8,128)(2,1)S(1)}, bf16[4,6,32,128]{3,2,1,0:T(8,128)(2,1)S(1)}, u32[]{:S(2)}, u32[]{:S(2)}) %collective-permute-start.4) | collective-permute-done | bytes 196640 | tf_op jit(solution)/shard_map/ppermute | solution.py:16
  26.2 3.0 %collective-permute-done.5.refs_5_.refs_1_ = bf16[4,6,32,128]{3,2,1,0:T(8,128)(2,1)S(1)} collective-permute-done((bf16[4,6,32,128]{3,2,1,0:T(8,128)(2,1)S(1)}, bf16[4,6,32,128]{3,2,1,0:T(8,128)(2,1)S(1)}, u32[]{:S(2)}, u32[]{:S(2)}) %collective-permute-start.5) | collective-permute-done | bytes 196640 | tf_op jit(solution)/shard_map/ppermute | solution.py:16
  29.2 0.0 collective-permute-done.10.refs_11_.refs_3_.refs_12_
  29.2 0.1 shard_map.96
  29.3 0.3 collective-permute-start.11
  29.5 1.5 %collective-permute-start.12 = (bf16[1536,128]{1,0:T(8,128)(2,1)S(1)}, bf16[1536,128]{1,0:T(8,128)(2,1)S(1)}, u32[]{:S(2)}, u32[]{:S(2)}) collective-permute-start(bf16[1536,128]{1,0:T(8,128)(2,1)S(1)} %get-tuple-element.48), channel_id=1, source_target_pairs={{0,12},{4,0},{8,4},{12,8},{1,13},{5,1},{9,5},{13,9},{2,14},{6,2},{... | collective-permute-start | bytes 1179656 | tf_op jit(solution)/shard_map/ppermute | solution.py:16
  31.1 0.0 collective-permute-start.8
  31.1 0.0 collective-permute-done.6.refs_6_.refs_13_
  31.1 0.0 copy-start.7
  31.1 1.7 %collective-permute-start.9 = (bf16[832,128]{1,0:T(8,128)(2,1)S(1)}, bf16[832,128]{1,0:T(8,128)(2,1)S(1)}, u32[]{:S(2)}, u32[]{:S(2)}) collective-permute-start(bf16[832,128]{1,0:T(8,128)(2,1)S(1)} %get-tuple-element.39), channel_id=1, source_target_pairs={{0,12},{4,0},{8,4},{12,8},{1,13},{5,1},{9,5},{13,9},{2,14},{6,2},{... | collective-permute-start | bytes 638984 | tf_op jit(solution)/shard_map/ppermute | solution.py:16
  32.8 0.0 copy-done.4
  32.8 0.0 copy-done.1
  32.8 0.4 shard_map.95
  33.3 0.0 collective-permute-done.7.refs_7_.refs_14_
  33.3 1.3 %collective-permute-start.13 = (bf16[2,48,128]{2,1,0:T(8,128)(2,1)S(1)}, bf16[2,48,128]{2,1,0:T(8,128)(2,1)S(1)}, u32[]{:S(2)}, u32[]{:S(2)}) collective-permute-start(bf16[2,48,128]{2,1,0:T(8,128)(2,1)S(1)} %get-tuple-element.49.refs_19_), channel_id=1, source_target_pairs={{0,8},{4,12},{8,0},{12,4},{1,9},{5,13},{9,1},{13,5},{2,10},{6,14},... | collective-permute-start | bytes 73736 | tf_op jit(solution)/shard_map/ppermute | solution.py:16
  34.6 9.1 %collective-permute-done.8.refs_8_.refs_15_ = bf16[832,128]{1,0:T(8,128)(2,1)S(1)} collective-permute-done((bf16[832,128]{1,0:T(8,128)(2,1)S(1)}, bf16[832,128]{1,0:T(8,128)(2,1)S(1)}, u32[]{:S(2)}, u32[]{:S(2)}) %collective-permute-start.8) | collective-permute-done | bytes 213024 | tf_op jit(solution)/shard_map/ppermute | solution.py:16
  43.7 0.6 %collective-permute-done.9.refs_9_.refs_16_ = bf16[832,128]{1,0:T(8,128)(2,1)S(1)} collective-permute-done((bf16[832,128]{1,0:T(8,128)(2,1)S(1)}, bf16[832,128]{1,0:T(8,128)(2,1)S(1)}, u32[]{:S(2)}, u32[]{:S(2)}) %collective-permute-start.9) | collective-permute-done | bytes 213024 | tf_op jit(solution)/shard_map/ppermute | solution.py:16
  44.4 0.0 copy-done
  44.4 0.0 copy-done.8
  44.4 6.4 %shard_map.94 = (f32[8,256,128]{2,1,0:T(8,128)S(1)}, bf16[320,48,128]{2,1,0:T(8,128)(2,1)S(1)}) custom-call(s32[3,27]{1,0:T(4,128)S(1)} %bitcast.3, bf16[27,128,128]{2,1,0:T(8,128)(2,1)S(1)} %copy-done, bf16[4,4,4,32,128]{4,3,2,1,0:T(8,128)(2,1)S(1)} %get-tuple-element.28.refs_0_.refs_2_, ...), custom_call_target="tpu_custom_call" | custom-call | flops 1811939328 | tf_op jit(solution)/shard_map/pallas_call | solution.py:38
  50.8 0.0 collective-permute-done.13.refs_20_
  50.8 0.0 collective-permute-done.11.refs_17_
  50.8 0.0 collective-permute-done.12.refs_18_
  50.8 0.0 copy-done.7
  50.8 5.3 %shard_map.97 = (f32[4,4,4,32,128]{4,3,2,1,0:T(8,128)}, bf16[320,48,128]{2,1,0:T(8,128)(2,1)S(1)}) custom-call(s32[4,4,4]{2,1,0:T(4,128)S(1)} %copy-done.6, s32[3,27]{1,0:T(4,128)S(1)} %bitcast.4, s32[3,2,32]{2,1,0:T(2,128)S(1)} %bitcast.2, f32[8,256,128]{2,1,0:T(8,128)S(1)} %get-tuple-element.41.refs_3_, ...), custom_call_target="tpu_custom_call", output_to_operand_aliasing={{1}: (10, {})} | custom-call | tf_op jit(solution)/shard_map/pallas_call | solution.py:38
  (1 shorter events, 0.0 us)
Async XLA Ops:
  0.0 0.9 %copy-start.3 = (bf16[8,48,48]{2,1,0:T(8,128)(2,1)S(1)}, bf16[8,48,48]{2,1,0:T(8,128)(2,1)}, u32[]{:S(2)}) copy-start(bf16[8,48,48]{2,1,0:T(8,128)(2,1)} %transfer.1) | copy-start | bytes 110596
  0.0 0.9 %copy-start.5 = (bf16[48,128]{1,0:T(8,128)(2,1)S(1)}, bf16[48,128]{1,0:T(8,128)(2,1)}, u32[]{:S(2)}) copy-start(bf16[48,128]{1,0:T(8,128)(2,1)} %refs_5_.1) | copy-start | bytes 36868
  0.0 0.9 %copy-start.6 = (s32[4,4,4]{2,1,0:T(4,128)S(1)}, s32[4,4,4]{2,1,0:T(4,128)}, u32[]{:S(2)}) copy-start(s32[4,4,4]{2,1,0:T(4,128)} %refs_0_.1) | copy-start | bytes 772
  0.0 1.1 %copy-start.2 = (bf16[4,4,4,32,128]{4,3,2,1,0:T(8,128)(2,1)S(1)}, bf16[4,4,4,32,128]{4,3,2,1,0:T(8,128)(2,1)}, u32[]{:S(2)}) copy-start(bf16[4,4,4,32,128]{4,3,2,1,0:T(8,128)(2,1)} %charges_in.1) | copy-start | bytes 1572868
  0.0 32.8 %copy-start.4 = (bf16[2,4,4,48,48]{4,3,2,1,0:T(8,128)(2,1)S(1)}, bf16[2,4,4,48,48]{4,3,2,1,0:T(8,128)(2,1)}, u32[]{:S(2)}) copy-start(bf16[2,4,4,48,48]{4,3,2,1,0:T(8,128)(2,1)} %coarse_in.1) | copy-start | bytes 442372
  0.0 32.8 %copy-start.1 = (bf16[2,32,48,48]{3,2,1,0:T(8,128)(2,1)S(1)}, bf16[2,32,48,48]{3,2,1,0:T(8,128)(2,1)}, u32[]{:S(2)}) copy-start(bf16[2,32,48,48]{3,2,1,0:T(8,128)(2,1)} %coupling_in.1) | copy-start | bytes 884740
  1.1 43.2 %copy-start = (bf16[27,128,128]{2,1,0:T(8,128)(2,1)S(1)}, bf16[27,128,128]{2,1,0:T(8,128)(2,1)}, u32[]{:S(2)}) copy-start(bf16[27,128,128]{2,1,0:T(8,128)(2,1)} %refs_4_.1) | copy-start | bytes 2654212
  1.1 43.2 %copy-start.8 = (s32[27,3]{0,1:T(4,128)S(1)}, s32[27,3]{0,1:T(4,128)}, u32[]{:S(2)}) copy-start(s32[27,3]{0,1:T(4,128)} %param.11) | copy-start | bytes 976
  3.1 13.4 %collective-permute-start = (bf16[2,4,4,32,128]{4,3,2,1,0:T(8,128)(2,1)S(1)}, bf16[2,4,4,32,128]{4,3,2,1,0:T(8,128)(2,1)S(1)}, u32[]{:S(2)}, u32[]{:S(2)}) collective-permute-start(bf16[2,4,4,32,128]{4,3,2,1,0:T(8,128)(2,1)S(1)} %get-tuple-element.29), channel_id=1, source_target_pairs={{0,16},{16,0},{1,17},{17,1},{2,18},{18,2},{3,19},{19,3},{4,20},{20... | collective-permute-start | bytes 786440 | tf_op jit(solution)/shard_map/ppermute | solution.py:16
  6.1 10.3 %collective-permute-start.1 = (bf16[11,48,128]{2,1,0:T(8,128)(2,1)S(1)}, bf16[11,48,128]{2,1,0:T(8,128)(2,1)S(1)}, u32[]{:S(2)}, u32[]{:S(2)}) collective-permute-start(bf16[11,48,128]{2,1,0:T(8,128)(2,1)S(1)} %get-tuple-element.31), channel_id=1, source_target_pairs={{0,1},{1,2},{2,3},{3,0},{4,5},{5,6},{6,7},{7,4},{8,9},{9,10},{10,1... | collective-permute-start | bytes 405512 | tf_op jit(solution)/shard_map/ppermute | solution.py:16
  7.7 8.8 %collective-permute-start.2 = (bf16[11,48,128]{2,1,0:T(8,128)(2,1)S(1)}, bf16[11,48,128]{2,1,0:T(8,128)(2,1)S(1)}, u32[]{:S(2)}, u32[]{:S(2)}) collective-permute-start(bf16[11,48,128]{2,1,0:T(8,128)(2,1)S(1)} %get-tuple-element.32), channel_id=1, source_target_pairs={{0,3},{1,0},{2,1},{3,2},{4,7},{5,4},{6,5},{7,6},{8,11},{9,8},{10,9... | collective-permute-start | bytes 405512 | tf_op jit(solution)/shard_map/ppermute | solution.py:16
  9.9 6.5 %collective-permute-start.3 = (bf16[1,48,128]{2,1,0:T(8,128)(2,1)S(1)}, bf16[1,48,128]{2,1,0:T(8,128)(2,1)S(1)}, u32[]{:S(2)}, u32[]{:S(2)}) collective-permute-start(bf16[1,48,128]{2,1,0:T(8,128)(2,1)S(1)} %get-tuple-element.33.refs_5_), channel_id=1, source_target_pairs={{0,2},{1,3},{2,0},{3,1},{4,6},{5,7},{6,4},{7,5},{8,10},{9,11},{10,... | collective-permute-start | bytes 36872 | tf_op jit(solution)/shard_map/ppermute | solution.py:16
  16.6 12.6 %collective-permute-start.10 = (bf16[39,48,128]{2,1,0:T(8,128)(2,1)S(1)}, bf16[39,48,128]{2,1,0:T(8,128)(2,1)S(1)}, u32[]{:S(2)}, u32[]{:S(2)}) collective-permute-start(bf16[39,48,128]{2,1,0:T(8,128)(2,1)S(1)} %get-tuple-element.40.refs_10_.refs_2_.refs_11_), channel_id=1, source_target_pairs={{0,16},{16,0},{1,17},{17,1},{2,18},{18,2},{3,19},{19,3},{4,20},{20... | collective-permute-start | bytes 1437704 | tf_op jit(solution)/shard_map/ppermute | solution.py:16
  17.2 13.9 %collective-permute-start.6 = (bf16[992,128]{1,0:T(8,128)(2,1)S(1)}, bf16[992,128]{1,0:T(8,128)(2,1)S(1)}, u32[]{:S(2)}, u32[]{:S(2)}) collective-permute-start(bf16[992,128]{1,0:T(8,128)(2,1)S(1)} %get-tuple-element.36), channel_id=1, source_target_pairs={{0,4},{4,8},{8,12},{12,0},{1,5},{5,9},{9,13},{13,1},{2,6},{6,10},{... | collective-permute-start | bytes 761864 | tf_op jit(solution)/shard_map/ppermute | solution.py:16
  17.2 9.0 %collective-permute-start.4 = (bf16[4,6,32,128]{3,2,1,0:T(8,128)(2,1)S(1)}, bf16[4,6,32,128]{3,2,1,0:T(8,128)(2,1)S(1)}, u32[]{:S(2)}, u32[]{:S(2)}) collective-permute-start(bf16[4,6,32,128]{3,2,1,0:T(8,128)(2,1)S(1)} %get-tuple-element.34), channel_id=1, source_target_pairs={{0,1},{1,2},{2,3},{3,0},{4,5},{5,6},{6,7},{7,4},{8,9},{9,10},{10,1... | collective-permute-start | bytes 589832 | tf_op jit(solution)/shard_map/ppermute | solution.py:16
  17.6 11.6 %collective-permute-start.5 = (bf16[4,6,32,128]{3,2,1,0:T(8,128)(2,1)S(1)}, bf16[4,6,32,128]{3,2,1,0:T(8,128)(2,1)S(1)}, u32[]{:S(2)}, u32[]{:S(2)}) collective-permute-start(bf16[4,6,32,128]{3,2,1,0:T(8,128)(2,1)S(1)} %get-tuple-element.35), channel_id=1, source_target_pairs={{0,3},{1,0},{2,1},{3,2},{4,7},{5,4},{6,5},{7,6},{8,11},{9,8},{10,9... | collective-permute-start | bytes 589832 | tf_op jit(solution)/shard_map/ppermute | solution.py:16
  21.0 12.3 %collective-permute-start.7 = (bf16[992,128]{1,0:T(8,128)(2,1)S(1)}, bf16[992,128]{1,0:T(8,128)(2,1)S(1)}, u32[]{:S(2)}, u32[]{:S(2)}) collective-permute-start(bf16[992,128]{1,0:T(8,128)(2,1)S(1)} %get-tuple-element.37), channel_id=1, source_target_pairs={{0,12},{4,0},{8,4},{12,8},{1,13},{5,1},{9,5},{13,9},{2,14},{6,2},{... | collective-permute-start | bytes 761864 | tf_op jit(solution)/shard_map/ppermute | solution.py:16
  29.3 21.5 %collective-permute-start.11 = (bf16[1536,128]{1,0:T(8,128)(2,1)S(1)}, bf16[1536,128]{1,0:T(8,128)(2,1)S(1)}, u32[]{:S(2)}, u32[]{:S(2)}) collective-permute-start(bf16[1536,128]{1,0:T(8,128)(2,1)S(1)} %get-tuple-element.47), channel_id=1, source_target_pairs={{0,4},{4,8},{8,12},{12,0},{1,5},{5,9},{9,13},{13,1},{2,6},{6,10},{... | collective-permute-start | bytes 1179656 | tf_op jit(solution)/shard_map/ppermute | solution.py:16
  29.5 21.2 %collective-permute-start.12 = (bf16[1536,128]{1,0:T(8,128)(2,1)S(1)}, bf16[1536,128]{1,0:T(8,128)(2,1)S(1)}, u32[]{:S(2)}, u32[]{:S(2)}) collective-permute-start(bf16[1536,128]{1,0:T(8,128)(2,1)S(1)} %get-tuple-element.48), channel_id=1, source_target_pairs={{0,12},{4,0},{8,4},{12,8},{1,13},{5,1},{9,5},{13,9},{2,14},{6,2},{... | collective-permute-start | bytes 1179656 | tf_op jit(solution)/shard_map/ppermute | solution.py:16
  31.1 12.7 %collective-permute-start.8 = (bf16[832,128]{1,0:T(8,128)(2,1)S(1)}, bf16[832,128]{1,0:T(8,128)(2,1)S(1)}, u32[]{:S(2)}, u32[]{:S(2)}) collective-permute-start(bf16[832,128]{1,0:T(8,128)(2,1)S(1)} %get-tuple-element.38), channel_id=1, source_target_pairs={{0,4},{4,8},{8,12},{12,0},{1,5},{5,9},{9,13},{13,1},{2,6},{6,10},{... | collective-permute-start | bytes 638984 | tf_op jit(solution)/shard_map/ppermute | solution.py:16
  31.1 19.7 %copy-start.7 = (s32[2,32,3]{1,0,2:T(2,128)S(1)}, s32[2,32,3]{1,0,2:T(2,128)}, u32[]{:S(2)}) copy-start(s32[2,32,3]{1,0,2:T(2,128)} %param.15) | copy-start | bytes 2308
  31.1 13.3 %collective-permute-start.9 = (bf16[832,128]{1,0:T(8,128)(2,1)S(1)}, bf16[832,128]{1,0:T(8,128)(2,1)S(1)}, u32[]{:S(2)}, u32[]{:S(2)}) collective-permute-start(bf16[832,128]{1,0:T(8,128)(2,1)S(1)} %get-tuple-element.39), channel_id=1, source_target_pairs={{0,12},{4,0},{8,4},{12,8},{1,13},{5,1},{9,5},{13,9},{2,14},{6,2},{... | collective-permute-start | bytes 638984 | tf_op jit(solution)/shard_map/ppermute | solution.py:16
  33.3 17.5 %collective-permute-start.13 = (bf16[2,48,128]{2,1,0:T(8,128)(2,1)S(1)}, bf16[2,48,128]{2,1,0:T(8,128)(2,1)S(1)}, u32[]{:S(2)}, u32[]{:S(2)}) collective-permute-start(bf16[2,48,128]{2,1,0:T(8,128)(2,1)S(1)} %get-tuple-element.49.refs_19_), channel_id=1, source_target_pairs={{0,8},{4,12},{8,0},{12,4},{1,9},{5,13},{9,1},{13,5},{2,10},{6,14},... | collective-permute-start | bytes 73736 | tf_op jit(solution)/shard_map/ppermute | solution.py:16

commit v2 on v1

--- a/solution.py
+++ b/solution.py
@@ -24,10 +24,10 @@
     return pl.BlockSpec(memory_space=pltpu.SMEM)
 
 
-def run(kernel, out_shape, args, smem=(), hbm=(), scratch=(), flops=None, limit=8, hbm_out=(), aliases=None):
+def run(kernel, out_shape, args, smem=(), anywhere=(), scratch=(), flops=None, limit=8, hbm_out=(), aliases=None):
     def spec(i):
-        if i in hbm:
-            return pl.BlockSpec(memory_space=pltpu.HBM)
+        if i in anywhere:
+            return pl.BlockSpec(memory_space=pl.ANY)
         return spec_smem() if i in smem else spec_vmem()
 
     cost = None
@@ -84,26 +84,14 @@
     out[...] = jnp.zeros(out.shape, out.dtype)
 
 
-def first_kernel(token, counts_in, charges_in, basis_in, transfer_in, own, faces, mom, z_high, z_low, y_high, y_low, two, counts, charges, basis, transfer, sems):
+def first_kernel(token, live, charges, basis, transfer, own, faces, mom, z_high, z_low, y_high, y_low, two):
     bx, by, bz, rhs, pts = charges.shape
     rank = basis.shape[0]
     width = rhs
-    copies = [
-        pltpu.make_async_copy(counts_in, counts, sems.at[0]),
-        pltpu.make_async_copy(basis_in, basis, sems.at[1]),
-        pltpu.make_async_copy(transfer_in, transfer, sems.at[2]),
-    ]
-    parts = [pltpu.make_async_copy(charges_in.at[x], charges.at[x], sems.at[3 + x]) for x in range(bx)]
-    for c in copies[:1] + parts + copies[1:]:
-        c.start()
-    lane = lax.broadcasted_iota(jnp.int32, (rhs, pts), 1)
-    copies[0].wait()
     for x in range(bx):
-        parts[x].wait()
         for y in range(by):
             for z in range(bz):
-                keep = lane < counts[x, y, z]
-                value = jnp.where(keep, charges[x, y, z].astype(F32), 0.0).astype(BF16)
+                value = (charges[x, y, z].astype(F32) * live[x, y, z : z + 1]).astype(BF16)
                 own[z, y, x] = value
                 if x == 0:
                     faces[0, z, y] = value
@@ -114,8 +102,6 @@
                     y_low[at : at + rhs] = value
                 if y == by - 1:
                     y_high[at : at + rhs] = value
-    copies[1].wait()
-    copies[2].wait()
     base = bz * bx * rhs
     leaf = {}
     for z in range(bz):
@@ -195,7 +181,6 @@
     mom, prev, nxt, mine = read.take(4)
     far = read.take(geo["extra_z"])
     c_high, c_low, wide, y_high, y_low = read.take(5)
-    leaf = bz * by
     for z in range(bz + 4):
         for y in range(by):
             if z < 2:
@@ -206,10 +191,6 @@
                 tile = mom[(z - 2) * by + y]
             wide[z * by + y] = tile
     first = (bz + 4) * by
-    for z in range(2):
-        wide[first + z] = prev[2 * by + z]
-        wide[first + 2 + z] = mom[leaf + z]
-        wide[first + 4 + z] = nxt[2 * by + z]
 
     def load(key):
         if key == 0:
@@ -221,7 +202,7 @@
         return far[key - 2][0]
 
     for t, tile in enumerate(assemble([(k, 0) for k in range(nz)], rhs, load)):
-        wide[first + 6 + t] = tile
+        wide[first + t] = tile
     for out, z in ((c_high, bz - 1), (c_low, 0)):
         for y in range(by):
             out[y, 0] = before[z, y]
@@ -250,8 +231,22 @@
     read = Reader(refs)
     prev, nxt = read.take(2)
     sources = read.take(xs)
+    mom, mz_prev, mz_next = read.take(3)
+    y1, y2 = read.take(2), read.take(2)
     far = read.take(geo["extra_x"])
-    y_high, y_low, two = read.take(3)
+    y_high, y_low, one, two = read.take(4)
+    base1 = bz * bx * rhs
+    base2 = 2 * bz * rhs
+    for yb in range(3):
+        for zb in range(3):
+            for z in range(2):
+                if yb == 1:
+                    tile = mom[bz * by + z] if zb == 1 else (mz_prev if zb == 0 else mz_next)[2 * by + z]
+                elif zb == 1:
+                    tile = tile_at(y1[yb // 2], base1 + (2 * bz + z) * rank, rank)
+                else:
+                    tile = tile_at(y2[yb // 2], base2 + (8 + (zb // 2) * 2 + z) * rank, rank)
+                one[(yb * 3 + zb) * 2 + z] = tile
     base = 2 * (bx + 2) * rhs
     first = (bz + 4) * by
     for out, y in ((y_high, by - 1), (y_low, 0)):
@@ -264,24 +259,21 @@
                 for yy in range(2):
                     at = base + (((k - 1) * (bz + 4) + z) * 2 + yy) * rank
                     out[at : at + rank] = sources[k][z * by + start + yy]
-            for z in range(6):
-                at = base + ((xs - 1) * (bz + 4) * 2 + (k - 1) * 6 + z) * rank
-                out[at : at + rank] = sources[k][first + z]
     per = 128 // rhs
     order = [((s, b // per), b % per) for s in range(nx) for b in range(nz)]
 
     def load(key):
         s, t = key
         if s == 0:
-            return sources[0][first + 6 + t]
+            return sources[0][first + t]
         if s == 1:
-            return sources[xs - 1][first + 6 + t]
+            return sources[xs - 1][first + t]
         if s == nx - 1:
-            return sources[1][first + 6 + t]
+            return sources[1][first + t]
         return far[s - 2][t]
 
     for t, tile in enumerate(assemble(order, rhs, load)):
-        at = base + ((xs - 1) * (2 * (bz + 4) + 6) + t) * rank
+        at = base + ((xs - 1) * 2 * (bz + 4) + t) * rank
         y_high[at : at + rank] = tile
         y_low[at : at + rank] = tile
         two[t] = tile
@@ -309,6 +301,18 @@
     shifts[4 * stride + at] = roll(jnp.where(blocks < 2, after, mid), -2 * width).astype(BF16)
 
 
+def windows_y(blocks, width, tiles):
+    low, mid, high = (t.astype(F32) for t in tiles)
+    upper = blocks >= 2
+    return [
+        low,
+        roll(jnp.where(upper, low, mid), 2 * width),
+        mid,
+        roll(jnp.where(upper, mid, high), 2 * width),
+        high,
+    ]
+
+
 def near_kernel(geo, *refs):
     xs, bx, by, bz, rhs, rank = (geo[k] for k in ("xs", "bx", "by", "bz", "rhs", "rank"))
     read = Reader(refs)
@@ -317,7 +321,8 @@
     cz_prev, cz_next = read.take(2)
     y1, y2 = read.take(2), read.take(2)
     sources = read.take(xs)
-    out, shifts, wide, inverse = read.take(4)
+    (one,) = read.take(1)
+    out, shifts, ones, corner_weights, wide, inverse = read.take(6)
     pts = wide.shape[3]
     stencil = near_blocks.shape[0]
     find_inverse(table, inverse, stencil)
@@ -361,6 +366,15 @@
             store_windows(
                 shifts, z * (by + 4) + y + 2, (bz + 4) * (by + 4), blocks, rhs, tiles[0], tiles[1], tiles[-1]
             )
+    for z in range(6):
+        for m, mid in enumerate(windows_y(blocks, rhs, [one[yb * 6 + z] for yb in range(3)])):
+            ones[(10 + m) * 6 + z] = mid.astype(BF16)
+            ones[(5 + m) * 6 + z] = roll(mid, rhs).astype(BF16)
+            ones[(15 + m) * 6 + z] = roll(mid, -rhs).astype(BF16)
+    for yk in range(2):
+        for zk in range(2):
+            codes = [(ox * 3 + 2 * yk) * 3 + 2 * zk for ox in range(3)]
+            corner_weights[yk, zk] = near_weights(inverse, near_blocks, codes)
 
 
 def weight_kernel(coupling_in, coarse_in, transfer, coupling, coarse, down_one, down_zero):
@@ -384,22 +398,21 @@
     )
     width = rhs
     read = Reader(refs)
-    counts, near_table, far_table = read.take(3)
-    near, near_blocks, basis, coupling, coarse, down_one, down_zero, _ = read.take(8)
-    sources = read.take(xs)
+    far_in, live, near, corner_weights, basis, coupling, coarse, down_one, down_zero = read.take(9)
+    read.take(2)
+    beside = read.take(xs - 1)
     y1, y2, y3 = read.take(2), read.take(2), read.take(2)
     (mine_two,) = read.take(1)
     far_two = read.take(geo["extra_y"])
-    out, shifts = read.take(2)
-    ones, corners, planes, inverse, sems = read.take(5)
-    pts = basis.shape[1]
+    out, shifts, ones = read.take(3)
+    corners, planes, far_table, sems = read.take(4)
+    table_copy = pltpu.make_async_copy(far_in, far_table, sems.at[bz])
+    table_copy.start()
     blocks = lane_blocks(rank, width)
-    stencil = near_blocks.shape[0]
     entries = coupling.shape[2] // rank
     base1 = bz * bx * rhs
     base2 = 2 * bz * rhs
     base3 = 2 * (bx + 2) * rhs
-    first = (bz + 4) * by
 
     def leaf_tile(k, z, side, yy):
         if k > 0:
@@ -416,49 +429,19 @@
                 at = (z + 2) * (by + 4) + yy + side * (by + 2)
                 store_windows(shifts, at, (bz + 4) * (by + 4), blocks, width, tiles[0], tiles[1], tiles[-1])
 
-    def one_tile(k, zb, z, yb):
-        if yb == 1:
-            return sources[k][first + zb * 2 + z]
-        side = yb // 2
-        if k > 0:
-            return tile_at(y3[side], base3 + ((xs - 1) * (bz + 4) * 2 + (k - 1) * 6 + zb * 2 + z) * rank, rank)
-        if zb == 1:
-            return tile_at(y1[side], base1 + (2 * bz + z) * rank, rank)
-        return tile_at(y2[side], base2 + (8 + (zb // 2) * 2 + z) * rank, rank)
-
     odd = blocks % 2 == 1
-    upper = blocks >= 2
-
-    def swap(value):
-        return jnp.where(odd, roll(value, width), roll(value, -width))
-
-    for zb in range(3):
-        for z in range(2):
-            rows = []
-            for yb in range(3):
-                mid = one_tile(0, zb, z, yb).astype(F32)
-                before = one_tile(1, zb, z, yb).astype(F32)
-                after = before if xs == 2 else one_tile(2, zb, z, yb).astype(F32)
-                rows.append([
-                    before,
-                    swap(jnp.where(odd, before, mid)),
-                    mid,
-                    swap(jnp.where(odd, mid, after)),
-                    after,
-                ])
-            for k in range(5):
-                low, mid, high = (rows[yb][k] for yb in range(3))
-                group = [
-                    low,
-                    roll(jnp.where(upper, low, mid), 2 * width),
-                    mid,
-                    roll(jnp.where(upper, mid, high), 2 * width),
-                    high,
-                ]
-                for m in range(5):
-                    ones[(k * 5 + m) * 6 + 2 * zb + z] = group[m].astype(BF16)
-
-    start_two = base3 + (xs - 1) * (2 * (bz + 4) + 6) * rank
+    for z in range(6):
+        sides = [windows_y(blocks, width, [s[yb * 6 + z] for yb in range(3)]) for s in beside]
+        for m in range(5):
+            before, after = sides[0][m], sides[-1][m]
+            ones[m * 6 + z] = before.astype(BF16)
+            ones[(20 + m) * 6 + z] = after.astype(BF16)
+            at = (5 + m) * 6 + z
+            ones[at] = jnp.where(odd, ones[at].astype(F32), roll(before, -width)).astype(BF16)
+            at = (15 + m) * 6 + z
+            ones[at] = jnp.where(odd, roll(after, width), ones[at].astype(F32)).astype(BF16)
+
+    start_two = base3 + (xs - 1) * 2 * (bz + 4) * rank
     per = 128 // width
 
     def two_tile(s, t):
@@ -477,6 +460,7 @@
     two = two + roll(two, 2 * width)
     two = (two + roll(two, width)).astype(BF16)
 
+    table_copy.wait()
     starts = []
     for e in range(entries):
         ox, oy, oz = (far_table[d, 1, e] + 2 for d in range(3))
@@ -513,17 +497,14 @@
                     at = 128 * (2 * z + y)
                     local[2 * z + l, 2 * y + j] = part[:, at : at + 128]
 
-    find_inverse(near_table, inverse, stencil)
-    for oy, yk in ((0, 0), (2, 1)):
-        for oz, zk in ((0, 0), (2, 1)):
-            weights = near_weights(inverse, near_blocks, [(ox * 3 + oy) * 3 + oz for ox in range(3)])
+    for yk in range(2):
+        for zk in range(2):
             windows = []
             for ox in range(3):
                 at = (zk * (bx + 2) + ox) * rhs
                 windows.append(y3[yk][at : at + bx * rhs])
-            corners[yk, zk] = dot(jnp.concatenate(windows, axis=1), weights, ((1,), (1,)))
-
-    lane = lax.broadcasted_iota(jnp.int32, (rhs, pts), 1)
+            corners[yk, zk] = dot(jnp.concatenate(windows, axis=1), corner_weights[yk, zk], ((1,), (1,)))
+
     starts = []
     for e in range(entries):
         ox, oy, oz = (far_table[d, 0, e] + 2 for d in range(3))
@@ -543,8 +524,7 @@
                 if y + k in (0, by - 1) and z in (0, bz - 1):
                     block = block + corners[0 if y + k == 0 else 1, 0 if z == 0 else 1]
                 for x in range(bx):
-                    keep = lane < counts[x, y + k, z]
-                    planes[z, x, y + k] = jnp.where(keep, block[x * rhs : (x + 1) * rhs], 0.0)
+                    planes[z, x, y + k] = block[x * rhs : (x + 1) * rhs] * live[x, y + k, z : z + 1]
         copies.append(pltpu.make_async_copy(planes.at[z], out.at[:, :, z], sems.at[z]))
         copies[-1].start()
     for c in copies:
@@ -573,6 +553,7 @@
     def part(kernel):
         return functools.partial(kernel, geo)
 
+    live = (jnp.arange(pts, dtype=jnp.int32) < counts[..., None]).astype(F32)
     near_table = near_offsets.T
     far_table = far_offsets.transpose(2, 0, 1)
 
@@ -591,15 +572,7 @@
             message,
             shape(1, rank, 128),
         ),
-        (token, counts, charges, leaf_basis, transfer),
-        hbm=(1, 2, 3, 4),
-        scratch=[
-            pltpu.SMEM(counts.shape, jnp.int32),
-            pltpu.VMEM(charges.shape, BF16),
-            pltpu.VMEM(leaf_basis.shape, BF16),
-            pltpu.VMEM(transfer.shape, BF16),
-            pltpu.SemaphoreType.DMA((3 + bx,)),
-        ],
+        (token, live, charges, leaf_basis, transfer),
     )
     mz_prev = from_shift(z_high, "gz", nz, -1)
     mz_next = from_shift(z_low, "gz", nz, 1)
@@ -625,7 +598,7 @@
     message = shape(2 * bz * rhs + 12 * rank, 128)
     c_high, c_low, wide, y_high, y_low = run(
         part(second_kernel),
-        (charge, charge, shape((bz + 4) * by + 6 + tiles_z, rank, 128), message, message),
+        (charge, charge, shape((bz + 4) * by + tiles_z, rank, 128), message, message),
         (own, *faces, mom, mz_prev, mz_next, two, *extra),
     )
     if nx == 2:
@@ -637,18 +610,30 @@
     y2 = [from_shift(y_high, "gy", ny, -1), from_shift(y_low, "gy", ny, 1)]
     extra = [from_shift(wide[-tiles_z:], "gx", nx, s) for s in range(2, nx - 1)]
 
-    message = shape(2 * (bx + 2) * rhs + ((xs - 1) * (2 * (bz + 4) + 6) + tiles_x) * rank, 128)
-    y_high, y_low, two = run(
-        part(third_kernel), (message, message, shape(tiles_x, rank, 128)), (cz_prev, cz_next, *sources, *extra)
-    )
+    message = shape(2 * (bx + 2) * rhs + ((xs - 1) * 2 * (bz + 4) + tiles_x) * rank, 128)
+    y_high, y_low, one, two = run(
+        part(third_kernel),
+        (message, message, shape(18, rank, 128), shape(tiles_x, rank, 128)),
+        (cz_prev, cz_next, *sources, mom, mz_prev, mz_next, *y1, *y2, *extra),
+    )
+    if nx == 2:
+        beside = [from_shift(one, "gx", nx, 1)]
+    else:
+        beside = [from_shift(one, "gx", nx, -1), from_shift(one, "gx", nx, 1)]
     y3 = [from_shift(y_high, "gy", ny, -1), from_shift(y_low, "gy", ny, 1)]
     extra = [from_shift(two, "gy", ny, s) for s in range(2, ny - 1)]
 
     windows = shape(5 * (bz + 4) * (by + 4), rank, 128)
-    near, shifts = run(
+    columns = shape(5 * 5 * 6, rank, 128)
+    near, shifts, ones, corner_weights = run(
         part(near_kernel),
-        (shape(bz * by // 2, 2 * bx * rhs, pts, dtype=F32), windows),
-        (near_table, near_blocks, own, *faces, cz_prev, cz_next, *y1, *y2, *sources),
+        (
+            shape(bz * by // 2, 2 * bx * rhs, pts, dtype=F32),
+            windows,
+            columns,
+            shape(2, 2, pts, 3 * pts),
+        ),
+        (near_table, near_blocks, own, *faces, cz_prev, cz_next, *y1, *y2, *sources, one),
         smem=(0,),
         scratch=[
             pltpu.VMEM((bz + 2, by + 2, (bx + 2) * rhs, pts), BF16),
@@ -658,35 +643,34 @@
         flops=2 * bx * by * bz * rhs * pts * pts * stencil,
     )
     args = (
-        counts,
-        near_table,
         far_table,
+        live,
         near,
-        near_blocks,
+        corner_weights,
         leaf_basis,
         *weights,
         shifts,
-        *sources,
+        ones,
+        *beside,
         *y1,
         *y2,
         *y3,
         two,
         *extra,
     )
-    potentials, _ = run(
+    potentials, _, _ = run(
         part(final_kernel),
-        (shape(bx, by, bz, rhs, pts, dtype=F32), windows),
+        (shape(bx, by, bz, rhs, pts, dtype=F32), windows, columns),
         args,
-        smem=(0, 1, 2),
+        anywhere=(0,),
         hbm_out=(0,),
-        aliases={10: 1},
+        aliases={9: 1, 10: 2},
         limit=24,
         scratch=[
-            pltpu.VMEM((5 * 5 * 6, rank, 128), BF16),
             pltpu.VMEM((2, 2, bx * rhs, pts), F32),
             pltpu.VMEM((bz, bx, by, rhs, pts), F32),
-            pltpu.SMEM((stencil,), jnp.int32),
-            pltpu.SemaphoreType.DMA((bz,)),
+            pltpu.SMEM(far_table.shape, jnp.int32),
+            pltpu.SemaphoreType.DMA((bz + 1,)),
         ],
     )
     return potentials

time: 56.8 us -> 48.1 us (0.85)
  waiting for transfers between devices: 22.5 us -> 17 us
  starting transfers between devices: 18.1 us -> 15.8 us
    ppermute x14 -> x15, waiting for transfers between devices: 22.5 us -> 17 us  [from_shift(): lax.ppermute(value, axis, [(i, (i - shift) % size) for i in range(size)])]
    ppermute x14 -> x15, starting transfers between devices: 18.1 us -> 15.8 us  [from_shift(): lax.ppermute(value, axis, [(i, (i - shift) % size) for i in range(size)])]
  transfers between devices with their start and end apart: 14 -> 15, of which waited for: 5 -> 4; matrix products, arithmetic and copies ran while one was open for 0% -> 0% of each run, Pallas kernels for 12% -> 16%
where the time goes in v2:
time: 48.1 us; the launch traced here: 47.9 us
  waiting for transfers between devices  17 us (35%)
  starting transfers between devices  15.8 us (33%)
  Pallas kernels  13.9 us (29%)
  local copies, waits for them, and re-layouts  1.04 us (2%)
    ppermute x15, waiting for transfers between devices, from_shift(): lax.ppermute(value, axis, [(i, (i - shift) % size) for i in range(size)])  17 us
    ppermute x15, starting transfers between devices, from_shift(): lax.ppermute(value, axis, [(i, (i - shift) % size) for i in range(size)])  15.8 us
    pallas_call x7, Pallas kernels, run(): pl.pallas_call(kernel, out_shape=out_shape, in_specs=[spec(i) for i in ra...  13.9 us
    unnamed x18, local copies, waits for them, and re-layouts  1.04 us
  transfers between devices with their start and end apart: 15, of which 4 were waited for; matrix products, arithmetic and copies ran while one was open for 0% of the time, Pallas kernels for 16%

profile of v2, /device:TPU:0, one launch (start us, length us, event | category | flops | bytes accessed | tf_op | source)
XLA Modules:
  0.0 47.9 jit_solution(14309763760826086249)
XLA Ops:
  0.0 0.0 copy-start.8
  0.0 0.0 copy-start.3
  0.0 0.0 copy-start.4
  0.0 0.0 copy-start.1
  0.0 0.7 %copy-done.8 = s32[4,4,4]{2,1,0:T(4,128)S(1)} copy-done((s32[4,4,4]{2,1,0:T(4,128)S(1)}, s32[4,4,4]{2,1,0:T(4,128)}, u32[]{:S(2)}) %copy-start.8) | copy-done | bytes 280
  0.7 0.0 copy-start
  0.7 0.0 copy-start.2
  0.7 0.0 copy-start.6
  0.7 0.0 copy-start.7
  0.7 0.1 fusion.live.refs_1_
  0.8 0.1 copy-done.3
  0.9 0.0 copy-done.4
  0.9 0.2 copy-done.1
  1.1 1.0 %shard_map.92 = (bf16[4,4,4,32,128]{4,3,2,1,0:T(8,128)(2,1)S(1)}, bf16[2,4,4,32,128]{4,3,2,1,0:T(8,128)(2,1)S(1)}, bf16[18,48,128]{2,1,0:T(8,128)(2,1)S(1)}, bf1...) custom-call(s32[8,128]{1,0:T(8,128)S(1)} %shard_map.91.token, ...), custom_call_target="tpu_custom_call" | custom-call | tf_op jit(solution)/shard_map/pallas_call | solution.py:38
  2.1 3.0 %collective-permute-start = (bf16[2,4,4,32,128]{4,3,2,1,0:T(8,128)(2,1)S(1)}, bf16[2,4,4,32,128]{4,3,2,1,0:T(8,128)(2,1)S(1)}, u32[]{:S(2)}, u32[]{:S(2)}) collective-permute-start(bf16[2,4,4,32,128]{4,3,2,1,0:T(8,128)(2,1)S(1)} %get-tuple-element.32), channel_id=1, source_target_pairs={{0,16},{16,0},{1,17},{17,1},{2,18},{18,2},{3,19},{19,3},{4,20},{20... | collective-permute-start | bytes 786440 | tf_op jit(solution)/shard_map/ppermute | solution.py:16
  5.1 1.6 %collective-permute-start.1 = (bf16[11,48,128]{2,1,0:T(8,128)(2,1)S(1)}, bf16[11,48,128]{2,1,0:T(8,128)(2,1)S(1)}, u32[]{:S(2)}, u32[]{:S(2)}) collective-permute-start(bf16[11,48,128]{2,1,0:T(8,128)(2,1)S(1)} %get-tuple-element.34), channel_id=1, source_target_pairs={{0,1},{1,2},{2,3},{3,0},{4,5},{5,6},{6,7},{7,4},{8,9},{9,10},{10,1... | collective-permute-start | bytes 405512 | tf_op jit(solution)/shard_map/ppermute | solution.py:16
  6.7 2.2 %collective-permute-start.2 = (bf16[11,48,128]{2,1,0:T(8,128)(2,1)S(1)}, bf16[11,48,128]{2,1,0:T(8,128)(2,1)S(1)}, u32[]{:S(2)}, u32[]{:S(2)}) collective-permute-start(bf16[11,48,128]{2,1,0:T(8,128)(2,1)S(1)} %get-tuple-element.35), channel_id=1, source_target_pairs={{0,3},{1,0},{2,1},{3,2},{4,7},{5,4},{6,5},{7,6},{8,11},{9,8},{10,9... | collective-permute-start | bytes 405512 | tf_op jit(solution)/shard_map/ppermute | solution.py:16
  9.0 0.8 %collective-permute-start.3 = (bf16[1,48,128]{2,1,0:T(8,128)(2,1)S(1)}, bf16[1,48,128]{2,1,0:T(8,128)(2,1)S(1)}, u32[]{:S(2)}, u32[]{:S(2)}) collective-permute-start(bf16[1,48,128]{2,1,0:T(8,128)(2,1)S(1)} %get-tuple-element.36.refs_5_), channel_id=1, source_target_pairs={{0,2},{1,3},{2,0},{3,1},{4,6},{5,7},{6,4},{7,5},{8,10},{9,11},{10,... | collective-permute-start | bytes 36872 | tf_op jit(solution)/shard_map/ppermute | solution.py:16
  9.8 0.0 collective-permute-start.6
  9.8 5.7 %collective-permute-done.3.refs_6_ = bf16[1,48,128]{2,1,0:T(8,128)(2,1)S(1)} collective-permute-done((bf16[1,48,128]{2,1,0:T(8,128)(2,1)S(1)}, bf16[1,48,128]{2,1,0:T(8,128)(2,1)S(1)}, u32[]{:S(2)}, u32[]{:S(2)}) %collective-permute-start.3) | collective-permute-done | bytes 12320 | tf_op jit(solution)/shard_map/ppermute | solution.py:16
  15.5 0.5 %collective-permute-start.7 = (bf16[992,128]{1,0:T(8,128)(2,1)S(1)}, bf16[992,128]{1,0:T(8,128)(2,1)S(1)}, u32[]{:S(2)}, u32[]{:S(2)}) collective-permute-start(bf16[992,128]{1,0:T(8,128)(2,1)S(1)} %get-tuple-element.40), channel_id=1, source_target_pairs={{0,12},{4,0},{8,4},{12,8},{1,13},{5,1},{9,5},{13,9},{2,14},{6,2},{... | collective-permute-start | bytes 761864 | tf_op jit(solution)/shard_map/ppermute | solution.py:16
  16.0 0.0 collective-permute-done.1.refs_3_.refs_5_
  16.0 0.0 collective-permute-done.2.refs_4_.refs_6_
  16.0 0.0 collective-permute-done.refs_1_.refs_3_
  16.0 0.1 shard_map.93
  16.1 0.6 %collective-permute-start.10 = (bf16[33,48,128]{2,1,0:T(8,128)(2,1)S(1)}, bf16[33,48,128]{2,1,0:T(8,128)(2,1)S(1)}, u32[]{:S(2)}, u32[]{:S(2)}) collective-permute-start(bf16[33,48,128]{2,1,0:T(8,128)(2,1)S(1)} %get-tuple-element.43.refs_2_.refs_10_), channel_id=1, source_target_pairs={{0,16},{16,0},{1,17},{17,1},{2,18},{18,2},{3,19},{19,3},{4,20},{20... | collective-permute-start | bytes 1216520 | tf_op jit(solution)/shard_map/ppermute | solution.py:16
  16.7 0.0 collective-permute-start.8
  16.7 1.7 %collective-permute-start.9 = (bf16[832,128]{1,0:T(8,128)(2,1)S(1)}, bf16[832,128]{1,0:T(8,128)(2,1)S(1)}, u32[]{:S(2)}, u32[]{:S(2)}) collective-permute-start(bf16[832,128]{1,0:T(8,128)(2,1)S(1)} %get-tuple-element.42), channel_id=1, source_target_pairs={{0,12},{4,0},{8,4},{12,8},{1,13},{5,1},{9,5},{13,9},{2,14},{6,2},{... | collective-permute-start | bytes 638984 | tf_op jit(solution)/shard_map/ppermute | solution.py:16
  18.5 0.0 collective-permute-done.6.refs_7_.refs_6_.refs_12_
  18.5 0.0 collective-permute-start.4
  18.5 2.8 %collective-permute-done.7.refs_8_.refs_7_.refs_13_ = bf16[992,128]{1,0:T(8,128)(2,1)S(1)} collective-permute-done((bf16[992,128]{1,0:T(8,128)(2,1)S(1)}, bf16[992,128]{1,0:T(8,128)(2,1)S(1)}, u32[]{:S(2)}, u32[]{:S(2)}) %collective-permute-start.7) | collective-permute-done | bytes 253984 | tf_op jit(solution)/shard_map/ppermute | solution.py:16
  21.3 1.0 %collective-permute-start.5 = (bf16[4,6,32,128]{3,2,1,0:T(8,128)(2,1)S(1)}, bf16[4,6,32,128]{3,2,1,0:T(8,128)(2,1)S(1)}, u32[]{:S(2)}, u32[]{:S(2)}) collective-permute-start(bf16[4,6,32,128]{3,2,1,0:T(8,128)(2,1)S(1)} %get-tuple-element.38), channel_id=1, source_target_pairs={{0,3},{1,0},{2,1},{3,2},{4,7},{5,4},{6,5},{7,6},{8,11},{9,8},{10,9... | collective-permute-start | bytes 589832 | tf_op jit(solution)/shard_map/ppermute | solution.py:16
  22.3 4.8 %collective-permute-done.4.refs_0_.refs_4_ = bf16[4,6,32,128]{3,2,1,0:T(8,128)(2,1)S(1)} collective-permute-done((bf16[4,6,32,128]{3,2,1,0:T(8,128)(2,1)S(1)}, bf16[4,6,32,128]{3,2,1,0:T(8,128)(2,1)S(1)}, u32[]{:S(2)}, u32[]{:S(2)}) %collective-permute-start.4) | collective-permute-done | bytes 196640 | tf_op jit(solution)/shard_map/ppermute | solution.py:16
  27.1 3.6 %collective-permute-done.5.refs_1_.refs_5_ = bf16[4,6,32,128]{3,2,1,0:T(8,128)(2,1)S(1)} collective-permute-done((bf16[4,6,32,128]{3,2,1,0:T(8,128)(2,1)S(1)}, bf16[4,6,32,128]{3,2,1,0:T(8,128)(2,1)S(1)}, u32[]{:S(2)}, u32[]{:S(2)}) %collective-permute-start.5) | collective-permute-done | bytes 196640 | tf_op jit(solution)/shard_map/ppermute | solution.py:16
  30.7 0.0 collective-permute-done.8.refs_9_.refs_8_.refs_14_
  30.7 0.0 collective-permute-done.9.refs_10_.refs_9_.refs_15_
  30.7 0.0 collective-permute-done.10.refs_3_.refs_11_
  30.7 0.1 shard_map.94
  30.8 0.2 collective-permute-start.12
  31.0 1.6 %collective-permute-start.13 = (bf16[1248,128]{1,0:T(8,128)(2,1)S(1)}, bf16[1248,128]{1,0:T(8,128)(2,1)S(1)}, u32[]{:S(2)}, u32[]{:S(2)}) collective-permute-start(bf16[1248,128]{1,0:T(8,128)(2,1)S(1)} %get-tuple-element.54), channel_id=1, source_target_pairs={{0,12},{4,0},{8,4},{12,8},{1,13},{5,1},{9,5},{13,9},{2,14},{6,2},{... | collective-permute-start | bytes 958472 | tf_op jit(solution)/shard_map/ppermute | solution.py:16
  32.6 0.0 copy-start.5
  32.6 1.5 %collective-permute-start.11 = (bf16[18,48,128]{2,1,0:T(8,128)(2,1)S(1)}, bf16[18,48,128]{2,1,0:T(8,128)(2,1)S(1)}, u32[]{:S(2)}, u32[]{:S(2)}) collective-permute-start(bf16[18,48,128]{2,1,0:T(8,128)(2,1)S(1)} %get-tuple-element.44.refs_12_), channel_id=1, source_target_pairs={{0,16},{16,0},{1,17},{17,1},{2,18},{18,2},{3,19},{19,3},{4,20},{20... | collective-permute-start | bytes 663560 | tf_op jit(solution)/shard_map/ppermute | solution.py:16
  34.1 0.0 copy-done
  34.1 0.0 copy-done.2
  34.1 0.4 shard_map.96
  34.5 1.0 %collective-permute-start.14 = (bf16[2,48,128]{2,1,0:T(8,128)(2,1)S(1)}, bf16[2,48,128]{2,1,0:T(8,128)(2,1)S(1)}, u32[]{:S(2)}, u32[]{:S(2)}) collective-permute-start(bf16[2,48,128]{2,1,0:T(8,128)(2,1)S(1)} %get-tuple-element.55.refs_18_), channel_id=1, source_target_pairs={{0,8},{4,12},{8,0},{12,4},{1,9},{5,13},{9,1},{13,5},{2,10},{6,14},... | collective-permute-start | bytes 73736 | tf_op jit(solution)/shard_map/ppermute | solution.py:16
  35.6 0.0 copy-done.6
  35.6 0.0 copy-done.7
  35.6 6.9 %shard_map.95 = (f32[8,256,128]{2,1,0:T(8,128)S(1)}, bf16[320,48,128]{2,1,0:T(8,128)(2,1)S(1)}, bf16[150,48,128]{2,1,0:T(8,128)(2,1)S(1)}, bf16[2,2,128,384]{3,2,1,0:T(8,128)(2,1)S(1)}) custom-call(s32[3,27]{1,0:T(4,128)S(1)} %bitcast.3, bf16[27,128,128]{2,1,0:T(8,128)(2,1)S(1)} %copy-done.6, ...), custom_call_target="tpu_custom_call" | custom-call | flops 1811939328 | tf_op jit(solution)/shard_map/pallas_call | solution.py:38
  42.5 0.0 collective-permute-done.14.refs_19_
  42.5 0.0 collective-permute-done.11.refs_11_
  42.5 0.0 collective-permute-done.12.refs_16_
  42.5 0.0 collective-permute-done.13.refs_17_
  42.6 0.0 copy-done.5
  42.6 5.3 %shard_map.97 = (f32[4,4,4,32,128]{4,3,2,1,0:T(8,128)}, bf16[320,48,128]{2,1,0:T(8,128)(2,1)S(1)}, bf16[150,48,128]{2,1,0:T(8,128)(2,1)S(1)}) custom-call(s32[3,2,32]{2,1,0:T(2,128)S(1)} %bitcast.2, f32[4,4,4,128]{3,2,1,0:T(4,128)S(1)} %fusion.live.refs_1_, ...), custom_call_target="tpu_custom_call", output_to_operand_aliasing={{1}: (9, {}), {2}: (10, {})} | custom-call | tf_op jit(solution)/shard_map/pallas_call | solution.py:38
  (1 shorter events, 0.0 us)
Async XLA Ops:
  0.0 0.7 %copy-start.8 = (s32[4,4,4]{2,1,0:T(4,128)S(1)}, s32[4,4,4]{2,1,0:T(4,128)}, u32[]{:S(2)}) copy-start(s32[4,4,4]{2,1,0:T(4,128)} %param.10) | copy-start | bytes 772
  0.0 0.9 %copy-start.3 = (bf16[8,48,48]{2,1,0:T(8,128)(2,1)S(1)}, bf16[8,48,48]{2,1,0:T(8,128)(2,1)}, u32[]{:S(2)}) copy-start(bf16[8,48,48]{2,1,0:T(8,128)(2,1)} %transfer.3) | copy-start | bytes 110596
  0.0 0.9 %copy-start.4 = (bf16[48,128]{1,0:T(8,128)(2,1)S(1)}, bf16[48,128]{1,0:T(8,128)(2,1)}, u32[]{:S(2)}) copy-start(bf16[48,128]{1,0:T(8,128)(2,1)} %refs_4_.1) | copy-start | bytes 36868
  0.0 1.1 %copy-start.1 = (bf16[4,4,4,32,128]{4,3,2,1,0:T(8,128)(2,1)S(1)}, bf16[4,4,4,32,128]{4,3,2,1,0:T(8,128)(2,1)}, u32[]{:S(2)}) copy-start(bf16[4,4,4,32,128]{4,3,2,1,0:T(8,128)(2,1)} %charges.1) | copy-start | bytes 1572868
  0.7 33.4 %copy-start = (bf16[2,32,48,48]{3,2,1,0:T(8,128)(2,1)S(1)}, bf16[2,32,48,48]{3,2,1,0:T(8,128)(2,1)}, u32[]{:S(2)}) copy-start(bf16[2,32,48,48]{3,2,1,0:T(8,128)(2,1)} %coupling_in.1) | copy-start | bytes 884740
  0.7 33.4 %copy-start.2 = (bf16[2,4,4,48,48]{4,3,2,1,0:T(8,128)(2,1)S(1)}, bf16[2,4,4,48,48]{4,3,2,1,0:T(8,128)(2,1)}, u32[]{:S(2)}) copy-start(bf16[2,4,4,48,48]{4,3,2,1,0:T(8,128)(2,1)} %coarse_in.1) | copy-start | bytes 442372
  0.7 34.9 %copy-start.6 = (bf16[27,128,128]{2,1,0:T(8,128)(2,1)S(1)}, bf16[27,128,128]{2,1,0:T(8,128)(2,1)}, u32[]{:S(2)}) copy-start(bf16[27,128,128]{2,1,0:T(8,128)(2,1)} %refs_1_.1) | copy-start | bytes 2654212
  0.7 34.9 %copy-start.7 = (s32[27,3]{0,1:T(4,128)S(1)}, s32[27,3]{0,1:T(4,128)}, u32[]{:S(2)}) copy-start(s32[27,3]{0,1:T(4,128)} %param.11) | copy-start | bytes 976
  2.1 13.9 %collective-permute-start = (bf16[2,4,4,32,128]{4,3,2,1,0:T(8,128)(2,1)S(1)}, bf16[2,4,4,32,128]{4,3,2,1,0:T(8,128)(2,1)S(1)}, u32[]{:S(2)}, u32[]{:S(2)}) collective-permute-start(bf16[2,4,4,32,128]{4,3,2,1,0:T(8,128)(2,1)S(1)} %get-tuple-element.32), channel_id=1, source_target_pairs={{0,16},{16,0},{1,17},{17,1},{2,18},{18,2},{3,19},{19,3},{4,20},{20... | collective-permute-start | bytes 786440 | tf_op jit(solution)/shard_map/ppermute | solution.py:16
  5.1 10.8 %collective-permute-start.1 = (bf16[11,48,128]{2,1,0:T(8,128)(2,1)S(1)}, bf16[11,48,128]{2,1,0:T(8,128)(2,1)S(1)}, u32[]{:S(2)}, u32[]{:S(2)}) collective-permute-start(bf16[11,48,128]{2,1,0:T(8,128)(2,1)S(1)} %get-tuple-element.34), channel_id=1, source_target_pairs={{0,1},{1,2},{2,3},{3,0},{4,5},{5,6},{6,7},{7,4},{8,9},{9,10},{10,1... | collective-permute-start | bytes 405512 | tf_op jit(solution)/shard_map/ppermute | solution.py:16
  6.7 9.3 %collective-permute-start.2 = (bf16[11,48,128]{2,1,0:T(8,128)(2,1)S(1)}, bf16[11,48,128]{2,1,0:T(8,128)(2,1)S(1)}, u32[]{:S(2)}, u32[]{:S(2)}) collective-permute-start(bf16[11,48,128]{2,1,0:T(8,128)(2,1)S(1)} %get-tuple-element.35), channel_id=1, source_target_pairs={{0,3},{1,0},{2,1},{3,2},{4,7},{5,4},{6,5},{7,6},{8,11},{9,8},{10,9... | collective-permute-start | bytes 405512 | tf_op jit(solution)/shard_map/ppermute | solution.py:16
  9.0 6.5 %collective-permute-start.3 = (bf16[1,48,128]{2,1,0:T(8,128)(2,1)S(1)}, bf16[1,48,128]{2,1,0:T(8,128)(2,1)S(1)}, u32[]{:S(2)}, u32[]{:S(2)}) collective-permute-start(bf16[1,48,128]{2,1,0:T(8,128)(2,1)S(1)} %get-tuple-element.36.refs_5_), channel_id=1, source_target_pairs={{0,2},{1,3},{2,0},{3,1},{4,6},{5,7},{6,4},{7,5},{8,10},{9,11},{10,... | collective-permute-start | bytes 36872 | tf_op jit(solution)/shard_map/ppermute | solution.py:16
  9.8 8.7 %collective-permute-start.6 = (bf16[992,128]{1,0:T(8,128)(2,1)S(1)}, bf16[992,128]{1,0:T(8,128)(2,1)S(1)}, u32[]{:S(2)}, u32[]{:S(2)}) collective-permute-start(bf16[992,128]{1,0:T(8,128)(2,1)S(1)} %get-tuple-element.39), channel_id=1, source_target_pairs={{0,4},{4,8},{8,12},{12,0},{1,5},{5,9},{9,13},{13,1},{2,6},{6,10},{... | collective-permute-start | bytes 761864 | tf_op jit(solution)/shard_map/ppermute | solution.py:16
  15.5 5.8 %collective-permute-start.7 = (bf16[992,128]{1,0:T(8,128)(2,1)S(1)}, bf16[992,128]{1,0:T(8,128)(2,1)S(1)}, u32[]{:S(2)}, u32[]{:S(2)}) collective-permute-start(bf16[992,128]{1,0:T(8,128)(2,1)S(1)} %get-tuple-element.40), channel_id=1, source_target_pairs={{0,12},{4,0},{8,4},{12,8},{1,13},{5,1},{9,5},{13,9},{2,14},{6,2},{... | collective-permute-start | bytes 761864 | tf_op jit(solution)/shard_map/ppermute | solution.py:16
  16.1 14.6 %collective-permute-start.10 = (bf16[33,48,128]{2,1,0:T(8,128)(2,1)S(1)}, bf16[33,48,128]{2,1,0:T(8,128)(2,1)S(1)}, u32[]{:S(2)}, u32[]{:S(2)}) collective-permute-start(bf16[33,48,128]{2,1,0:T(8,128)(2,1)S(1)} %get-tuple-element.43.refs_2_.refs_10_), channel_id=1, source_target_pairs={{0,16},{16,0},{1,17},{17,1},{2,18},{18,2},{3,19},{19,3},{4,20},{20... | collective-permute-start | bytes 1216520 | tf_op jit(solution)/shard_map/ppermute | solution.py:16
  16.7 14.0 %collective-permute-start.8 = (bf16[832,128]{1,0:T(8,128)(2,1)S(1)}, bf16[832,128]{1,0:T(8,128)(2,1)S(1)}, u32[]{:S(2)}, u32[]{:S(2)}) collective-permute-start(bf16[832,128]{1,0:T(8,128)(2,1)S(1)} %get-tuple-element.41), channel_id=1, source_target_pairs={{0,4},{4,8},{8,12},{12,0},{1,5},{5,9},{9,13},{13,1},{2,6},{6,10},{... | collective-permute-start | bytes 638984 | tf_op jit(solution)/shard_map/ppermute | solution.py:16
  16.7 14.0 %collective-permute-start.9 = (bf16[832,128]{1,0:T(8,128)(2,1)S(1)}, bf16[832,128]{1,0:T(8,128)(2,1)S(1)}, u32[]{:S(2)}, u32[]{:S(2)}) collective-permute-start(bf16[832,128]{1,0:T(8,128)(2,1)S(1)} %get-tuple-element.42), channel_id=1, source_target_pairs={{0,12},{4,0},{8,4},{12,8},{1,13},{5,1},{9,5},{13,9},{2,14},{6,2},{... | collective-permute-start | bytes 638984 | tf_op jit(solution)/shard_map/ppermute | solution.py:16
  18.5 8.7 %collective-permute-start.4 = (bf16[4,6,32,128]{3,2,1,0:T(8,128)(2,1)S(1)}, bf16[4,6,32,128]{3,2,1,0:T(8,128)(2,1)S(1)}, u32[]{:S(2)}, u32[]{:S(2)}) collective-permute-start(bf16[4,6,32,128]{3,2,1,0:T(8,128)(2,1)S(1)} %get-tuple-element.37), channel_id=1, source_target_pairs={{0,1},{1,2},{2,3},{3,0},{4,5},{5,6},{6,7},{7,4},{8,9},{9,10},{10,1... | collective-permute-start | bytes 589832 | tf_op jit(solution)/shard_map/ppermute | solution.py:16
  21.3 9.4 %collective-permute-start.5 = (bf16[4,6,32,128]{3,2,1,0:T(8,128)(2,1)S(1)}, bf16[4,6,32,128]{3,2,1,0:T(8,128)(2,1)S(1)}, u32[]{:S(2)}, u32[]{:S(2)}) collective-permute-start(bf16[4,6,32,128]{3,2,1,0:T(8,128)(2,1)S(1)} %get-tuple-element.38), channel_id=1, source_target_pairs={{0,3},{1,0},{2,1},{3,2},{4,7},{5,4},{6,5},{7,6},{8,11},{9,8},{10,9... | collective-permute-start | bytes 589832 | tf_op jit(solution)/shard_map/ppermute | solution.py:16
  30.8 11.7 %collective-permute-start.12 = (bf16[1248,128]{1,0:T(8,128)(2,1)S(1)}, bf16[1248,128]{1,0:T(8,128)(2,1)S(1)}, u32[]{:S(2)}, u32[]{:S(2)}) collective-permute-start(bf16[1248,128]{1,0:T(8,128)(2,1)S(1)} %get-tuple-element.53), channel_id=1, source_target_pairs={{0,4},{4,8},{8,12},{12,0},{1,5},{5,9},{9,13},{13,1},{2,6},{6,10},{... | collective-permute-start | bytes 958472 | tf_op jit(solution)/shard_map/ppermute | solution.py:16
  31.0 11.6 %collective-permute-start.13 = (bf16[1248,128]{1,0:T(8,128)(2,1)S(1)}, bf16[1248,128]{1,0:T(8,128)(2,1)S(1)}, u32[]{:S(2)}, u32[]{:S(2)}) collective-permute-start(bf16[1248,128]{1,0:T(8,128)(2,1)S(1)} %get-tuple-element.54), channel_id=1, source_target_pairs={{0,12},{4,0},{8,4},{12,8},{1,13},{5,1},{9,5},{13,9},{2,14},{6,2},{... | collective-permute-start | bytes 958472 | tf_op jit(solution)/shard_map/ppermute | solution.py:16
  32.6 9.9 %copy-start.5 = (s32[2,32,3]{1,0,2:T(2,128)S(1)}, s32[2,32,3]{1,0,2:T(2,128)}, u32[]{:S(2)}) copy-start(s32[2,32,3]{1,0,2:T(2,128)} %param.15) | copy-start | bytes 2308
  32.6 9.9 %collective-permute-start.11 = (bf16[18,48,128]{2,1,0:T(8,128)(2,1)S(1)}, bf16[18,48,128]{2,1,0:T(8,128)(2,1)S(1)}, u32[]{:S(2)}, u32[]{:S(2)}) collective-permute-start(bf16[18,48,128]{2,1,0:T(8,128)(2,1)S(1)} %get-tuple-element.44.refs_12_), channel_id=1, source_target_pairs={{0,16},{16,0},{1,17},{17,1},{2,18},{18,2},{3,19},{19,3},{4,20},{20... | collective-permute-start | bytes 663560 | tf_op jit(solution)/shard_map/ppermute | solution.py:16
  34.5 8.0 %collective-permute-start.14 = (bf16[2,48,128]{2,1,0:T(8,128)(2,1)S(1)}, bf16[2,48,128]{2,1,0:T(8,128)(2,1)S(1)}, u32[]{:S(2)}, u32[]{:S(2)}) collective-permute-start(bf16[2,48,128]{2,1,0:T(8,128)(2,1)S(1)} %get-tuple-element.55.refs_18_), channel_id=1, source_target_pairs={{0,8},{4,12},{8,0},{12,4},{1,9},{5,13},{9,1},{13,5},{2,10},{6,14},... | collective-permute-start | bytes 73736 | tf_op jit(solution)/shard_map/ppermute | solution.py:16

commit v3 on v2

--- a/solution.py
+++ b/solution.py
@@ -49,6 +49,16 @@
 
 def lane_blocks(rows, width):
     return lax.broadcasted_iota(jnp.int32, (rows, 128), 1) // width
+
+
+class Masks:
+    def __init__(self, rank, width):
+        lanes = lax.broadcasted_iota(jnp.int16, (rank, 128), 1)
+        bound = [jnp.int16(width * k) for k in range(4)]
+        self.first = lanes < bound[1]
+        self.lower = lanes < bound[2]
+        self.last = lanes >= bound[3]
+        self.odd = ((lanes >= bound[1]) & self.lower) | self.last
 
 
 def roll(value, shift):
@@ -289,88 +299,123 @@
         inverse[(ox * 3 + oy) * 3 + oz] = s
 
 
-def store_windows(shifts, at, stride, blocks, width, mid, before, after):
+def store_windows(shifts, at, stride, masks, width, mid, before, after):
+    shifts[at] = roll(jnp.where(masks.lower, mid, before), 2 * width)
+    shifts[stride + at] = roll(jnp.where(masks.last, before, mid), width)
     shifts[2 * stride + at] = mid
-    mid = mid.astype(F32)
-    same = before is after
-    before = before.astype(F32)
-    after = before if same else after.astype(F32)
-    shifts[at] = roll(jnp.where(blocks >= 2, before, mid), 2 * width).astype(BF16)
-    shifts[stride + at] = roll(jnp.where(blocks >= 3, before, mid), width).astype(BF16)
-    shifts[3 * stride + at] = roll(jnp.where(blocks < 1, after, mid), -width).astype(BF16)
-    shifts[4 * stride + at] = roll(jnp.where(blocks < 2, after, mid), -2 * width).astype(BF16)
-
-
-def windows_y(blocks, width, tiles):
-    low, mid, high = (t.astype(F32) for t in tiles)
-    upper = blocks >= 2
+    shifts[3 * stride + at] = roll(jnp.where(masks.first, after, mid), -width)
+    shifts[4 * stride + at] = roll(jnp.where(masks.lower, after, mid), 2 * width)
+
+
+def windows_y(masks, width, tiles):
+    low, mid, high = tiles
     return [
         low,
-        roll(jnp.where(upper, low, mid), 2 * width),
+        roll(jnp.where(masks.lower, mid, low), 2 * width),
         mid,
-        roll(jnp.where(upper, mid, high), 2 * width),
+        roll(jnp.where(masks.lower, high, mid), 2 * width),
         high,
     ]
+
+
+def near_product(geo, weights, window, out, first, planes):
+    bx, by, rhs = (geo[k] for k in ("bx", "by", "rhs"))
+    rows, blocks = [], ([], [])
+    for plane in planes:
+        for ox in range(3):
+            for oy in range(3):
+                rows.append(window(first + plane, oy, ox))
+                for k in range(2):
+                    blocks[k].append(weights(ox, oy, plane + 1 - k))
+    right = jnp.concatenate([jnp.concatenate(b, axis=1) for b in blocks], axis=0)
+    value = dot(jnp.concatenate(rows, axis=1), right, ((1,), (1,)))
+    for k in range(2):
+        out[first + k] = value[:, 128 * k : 128 * (k + 1)]
+
+
+def inner_kernel(geo, *refs):
+    bx, by, bz, rhs = (geo[k] for k in ("bx", "by", "bz", "rhs"))
+    read = Reader(refs)
+    table, near_blocks, own = read.take(3)
+    before, after = read.faces(geo)
+    y1 = read.take(2)
+    out, wide, inverse = read.take(3)
+    pts = wide.shape[3]
+    find_inverse(table, inverse, near_blocks.shape[0])
+    rows = (bx + 2) * rhs
+    none = jnp.zeros((rhs, pts), BF16)
+    for z in range(bz):
+        for k, y in enumerate((0, by + 1)):
+            wide[z, y, 0:rhs] = none
+            wide[z, y, rhs : rows - rhs] = y1[k][z * bx * rhs : (z + 1) * bx * rhs]
+            wide[z, y, rows - rhs :] = none
+        for y in range(1, by + 1):
+            wide[z, y, 0:rhs] = before[z, y - 1]
+            wide[z, y, rhs : rows - rhs] = own[z, y - 1].reshape(bx * rhs, pts)
+            wide[z, y, rows - rhs :] = after[z, y - 1]
+    empty = jnp.zeros((pts, pts), BF16)
+
+    def weights(ox, oy, oz):
+        return near_blocks[inverse[(ox * 3 + oy) * 3 + oz]] if 0 <= oz < 3 else empty
+
+    def window(z, oy, ox):
+        return wide[z, oy : oy + by, ox * rhs : (ox + bx) * rhs, :].reshape(by * bx * rhs, pts)
+
+    for first in range(0, bz, 2):
+        planes = [p for p in range(-1, 3) if 0 <= first + p < bz]
+        near_product(geo, weights, window, out, first, planes)
 
 
 def near_kernel(geo, *refs):
     xs, bx, by, bz, rhs, rank = (geo[k] for k in ("xs", "bx", "by", "bz", "rhs", "rank"))
     read = Reader(refs)
-    table, near_blocks, own = read.take(3)
-    before, after = read.faces(geo)
+    table, near_blocks = read.take(2)
+    read.take(1)
     cz_prev, cz_next = read.take(2)
-    y1, y2 = read.take(2), read.take(2)
+    y2 = read.take(2)
     sources = read.take(xs)
     (one,) = read.take(1)
     out, shifts, ones, corner_weights, wide, inverse = read.take(6)
     pts = wide.shape[3]
-    stencil = near_blocks.shape[0]
-    find_inverse(table, inverse, stencil)
+    find_inverse(table, inverse, near_blocks.shape[0])
     rows = (bx + 2) * rhs
-    for z in range(bz + 2):
-        outer = z in (0, bz + 1)
-        for k, y in enumerate((0, by + 1)):
-            if outer:
-                wide[z, y] = jnp.zeros((rows, pts), BF16)
-                continue
-            at = (z - 1) * rhs
-            wide[z, y, 0:rhs] = y2[k][at : at + rhs]
-            wide[z, y, rhs : rows - rhs] = y1[k][bx * at : bx * (at + rhs)]
-            wide[z, y, rows - rhs :] = y2[k][bz * rhs + at : bz * rhs + at + rhs]
-        for y in range(1, by + 1):
-            if outer:
-                wide[z, y] = (cz_prev if z == 0 else cz_next)[y - 1].reshape(rows, pts)
-                continue
-            wide[z, y, 0:rhs] = before[z - 1, y - 1]
-            wide[z, y, rhs : rows - rhs] = own[z - 1, y - 1].reshape(bx * rhs, pts)
-            wide[z, y, rows - rhs :] = after[z - 1, y - 1]
-    weights = near_weights(inverse, near_blocks, range(stencil))
-
-    def step(number, carry):
-        z = number // (by // 2)
-        y = number % (by // 2) * 2
-        windows = []
-        for ox in range(3):
-            for oy in range(3):
-                for oz in range(3):
-                    window = wide[z + oz, pl.ds(y + oy, 2), ox * rhs : (ox + bx) * rhs, :]
-                    windows.append(window.reshape(2 * bx * rhs, pts))
-        out[number] = dot(jnp.concatenate(windows, axis=1), weights, ((1,), (1,)))
-        return carry
-
-    lax.fori_loop(0, bz * by // 2, step, 0)
-    blocks = lane_blocks(rank, rhs)
+    for k, s in enumerate((cz_prev, cz_next)):
+        for y in (0, by + 1):
+            wide[k, y] = jnp.zeros((rows, pts), BF16)
+        for y in range(by):
+            wide[k, y + 1] = s[y].reshape(rows, pts)
+    for k, z in enumerate((0, bz - 1)):
+        codes = [(ox * 3 + oy) * 3 + 2 * k for ox in range(3) for oy in range(3)]
+        left = [
+            wide[k, oy : oy + by, ox * rhs : (ox + bx) * rhs, :].reshape(by * bx * rhs, pts)
+            for ox in range(3)
+            for oy in range(3)
+        ]
+        right = near_weights(inverse, near_blocks, codes)
+        out[z] = out[z] + dot(jnp.concatenate(left, axis=1), right, ((1,), (1,)))
+    none = jnp.zeros((rhs, pts), BF16)
+    for yk, y in enumerate((0, by - 1)):
+        for xk, x in enumerate((0, bx - 1)):
+            at = xk * bz * rhs
+            column = y2[yk][at : at + bz * rhs]
+            column = jnp.concatenate([none, column, none], axis=0)
+            left = jnp.concatenate([column[oz * rhs : (oz + bz) * rhs] for oz in range(3)], axis=1)
+            right = near_weights(inverse, near_blocks, [(6 * xk + 2 * yk) * 3 + oz for oz in range(3)])
+            value = dot(left, right, ((1,), (1,)))
+            at = (y * bx + x) * rhs
+            for z in range(bz):
+                out[z, at : at + rhs] = out[z, at : at + rhs] + value[z * rhs : (z + 1) * rhs]
+    masks = Masks(rank, rhs)
     for z in range(bz + 4):
         for y in range(by):
             tiles = [s[z * by + y] for s in sources]
-            store_windows(
-                shifts, z * (by + 4) + y + 2, (bz + 4) * (by + 4), blocks, rhs, tiles[0], tiles[1], tiles[-1]
-            )
+            at = z * (by + 4) + y + 2
+            store_windows(shifts, at, (bz + 4) * (by + 4), masks, rhs, tiles[0], tiles[1], tiles[-1])
     for z in range(6):
-        for m, mid in enumerate(windows_y(blocks, rhs, [one[yb * 6 + z] for yb in range(3)])):
-            ones[(10 + m) * 6 + z] = mid.astype(BF16)
-            ones[(5 + m) * 6 + z] = roll(mid, rhs).astype(BF16)
-            ones[(15 + m) * 6 + z] = roll(mid, -rhs).astype(BF16)
+        for m, mid in enumerate(windows_y(masks, rhs, [one[yb * 6 + z] for yb in range(3)])):
+            ones[(10 + m) * 6 + z] = mid
+            ones[(5 + m) * 6 + z] = roll(mid, rhs)
+            ones[(15 + m) * 6 + z] = roll(mid, -rhs)
     for yk in range(2):
         for zk in range(2):
             codes = [(ox * 3 + 2 * yk) * 3 + 2 * zk for ox in range(3)]
@@ -409,6 +454,7 @@
     table_copy = pltpu.make_async_copy(far_in, far_table, sems.at[bz])
     table_copy.start()
     blocks = lane_blocks(rank, width)
+    masks = Masks(rank, width)
     entries = coupling.shape[2] // rank
     base1 = bz * bx * rhs
     base2 = 2 * bz * rhs
@@ -427,19 +473,18 @@
             for yy in range(2):
                 tiles = [leaf_tile(k, z, side, yy) for k in range(xs)]
                 at = (z + 2) * (by + 4) + yy + side * (by + 2)
-                store_windows(shifts, at, (bz + 4) * (by + 4), blocks, width, tiles[0], tiles[1], tiles[-1])
-
-    odd = blocks % 2 == 1
+                store_windows(shifts, at, (bz + 4) * (by + 4), masks, width, tiles[0], tiles[1], tiles[-1])
+
     for z in range(6):
-        sides = [windows_y(blocks, width, [s[yb * 6 + z] for yb in range(3)]) for s in beside]
+        sides = [windows_y(masks, width, [s[yb * 6 + z] for yb in range(3)]) for s in beside]
         for m in range(5):
             before, after = sides[0][m], sides[-1][m]
-            ones[m * 6 + z] = before.astype(BF16)
-            ones[(20 + m) * 6 + z] = after.astype(BF16)
+            ones[m * 6 + z] = before
+            ones[(20 + m) * 6 + z] = after
             at = (5 + m) * 6 + z
-            ones[at] = jnp.where(odd, ones[at].astype(F32), roll(before, -width)).astype(BF16)
+            ones[at] = jnp.where(masks.odd, ones[at], roll(before, -width))
             at = (15 + m) * 6 + z
-            ones[at] = jnp.where(odd, roll(after, width), ones[at].astype(F32)).astype(BF16)
+            ones[at] = jnp.where(masks.odd, roll(after, width), ones[at])
 
     start_two = base3 + (xs - 1) * 2 * (bz + 4) * rank
     per = 128 // width
@@ -451,11 +496,13 @@
             return tile_at(y3[1 if s == 1 else 0], start_two + t * rank, rank)
         return far_two[s - 2][t]
 
+    lanes = lax.broadcasted_iota(jnp.int16, (rank, 128), 1)
+    quarter = [(lanes >= jnp.int16(width * b)) & (lanes < jnp.int16(width * (b + 1))) for b in range(per)]
     stacked = []
     for s in range(ny):
         for b in range(nz * nx):
-            tile = two_tile(s, b // per).astype(F32)
-            stacked.append(jnp.where(blocks == b % per, tile, 0.0).astype(BF16))
+            tile = two_tile(s, b // per)
+            stacked.append(jnp.where(quarter[b % per], tile, jnp.zeros_like(tile)))
     two = dot(coarse[...], jnp.concatenate(stacked, axis=0))
     two = two + roll(two, 2 * width)
     two = (two + roll(two, width)).astype(BF16)
@@ -476,17 +523,14 @@
                 child = 4 * i + 2 * j + z
                 part = from_two[child * rank : (child + 1) * rank]
                 total = total + jnp.where(blocks == 2 * j + i, part, 0.0)
-        total = total.astype(BF16).astype(F32)
+        total = total.astype(BF16)
         half = roll(total, 2 * width)
+        none = jnp.zeros_like(total)
         for up in (
-            jnp.where(blocks == 0, total, jnp.where(blocks == 3, half, roll(total, width))),
-            jnp.where(blocks == 0, half, jnp.where(blocks == 3, total, roll(total, -width))),
+            jnp.where(masks.first, total, jnp.where(masks.last, half, roll(total, width))),
+            jnp.where(masks.first, half, jnp.where(masks.last, total, roll(total, -width))),
         ):
-            ups.append(
-                jnp.concatenate(
-                    [jnp.where(odd, 0.0, up).astype(BF16), jnp.where(odd, up, 0.0).astype(BF16)], axis=0
-                )
-            )
+            ups.append(jnp.concatenate([jnp.where(masks.odd, none, up), jnp.where(masks.odd, up, none)], axis=0))
     ups = jnp.concatenate(ups, axis=1)
     local = {}
     for j in range(2):
@@ -509,16 +553,21 @@
     for e in range(entries):
         ox, oy, oz = (far_table[d, 0, e] + 2 for d in range(3))
         starts.append((ox * (bz + 4) + oz) * (by + 4) + oy)
+    totals = []
+    for z in range(bz):
+        for y in range(0, by, 2):
+            columns = [
+                jnp.concatenate([shifts[s + z * (by + 4) + y + k] for s in starts], axis=0) for k in range(2)
+            ]
+            total = dot(coupling[0], jnp.concatenate(columns, axis=1))
+            totals.append((total + jnp.concatenate([local[z, y], local[z, y + 1]], axis=1)).astype(BF16))
     copies = []
     for z in range(bz):
         for half in range(by // 2):
             y = 2 * half
-            columns = [
-                jnp.concatenate([shifts[s + z * (by + 4) + y + k] for s in starts], axis=0) for k in range(2)
-            ]
-            total = dot(coupling[0], jnp.concatenate(columns, axis=1))
-            total = total + jnp.concatenate([local[z, y], local[z, y + 1]], axis=1)
-            result = dot(total.astype(BF16), basis[...], ((0,), (0,))) + near[z * (by // 2) + half]
+            number = z * (by // 2) + half
+            result = dot(totals[number], basis[...], ((0,), (0,)))
+            result = result + near[z, half * 2 * bx * rhs : (half + 1) * 2 * bx * rhs]
             for k in range(2):
                 block = result[k * bx * rhs : (k + 1) * bx * rhs]
                 if y + k in (0, by - 1) and z in (0, bz - 1):
@@ -610,6 +659,20 @@
     y2 = [from_shift(y_high, "gy", ny, -1), from_shift(y_low, "gy", ny, 1)]
     extra = [from_shift(wide[-tiles_z:], "gx", nx, s) for s in range(2, nx - 1)]
 
+    field = shape(bz, by * bx * rhs, pts, dtype=F32)
+    near = run(
+        part(inner_kernel),
+        field,
+        (near_table, near_blocks, own, *faces, *y1),
+        smem=(0,),
+        scratch=[
+            pltpu.VMEM((bz, by + 2, (bx + 2) * rhs, pts), BF16),
+            pltpu.SMEM((stencil,), jnp.int32),
+        ],
+        limit=16,
+        flops=2 * bx * by * bz * rhs * pts * pts * stencil,
+    )
+
     message = shape(2 * (bx + 2) * rhs + ((xs - 1) * 2 * (bz + 4) + tiles_x) * rank, 128)
     y_high, y_low, one, two = run(
         part(third_kernel),
@@ -627,20 +690,16 @@
     columns = shape(5 * 5 * 6, rank, 128)
     near, shifts, ones, corner_weights = run(
         part(near_kernel),
-        (
-            shape(bz * by // 2, 2 * bx * rhs, pts, dtype=F32),
-            windows,
-            columns,
-            shape(2, 2, pts, 3 * pts),
-        ),
-        (near_table, near_blocks, own, *faces, cz_prev, cz_next, *y1, *y2, *sources, one),
+        (field, windows, columns, shape(2, 2, pts, 3 * pts)),
+        (near_table, near_blocks, near, cz_prev, cz_next, *y2, *sources, one),
         smem=(0,),
+        aliases={2: 0},
         scratch=[
-            pltpu.VMEM((bz + 2, by + 2, (bx + 2) * rhs, pts), BF16),
+            pltpu.VMEM((2, by + 2, (bx + 2) * rhs, pts), BF16),
             pltpu.SMEM((stencil,), jnp.int32),
         ],
         limit=16,
-        flops=2 * bx * by * bz * rhs * pts * pts * stencil,
+        flops=2 * bx * by * bz * rhs * pts * pts * 9,
     )
     args = (
         far_table,

time: 48.1 us -> 45.5 us (0.946)
  Pallas kernels: 13.9 us -> 10.2 us
  waiting for transfers between devices: 17 us -> 18.1 us
    pallas_call x7 -> x8, Pallas kernels: 13.9 us -> 10.2 us  [run(): pl.pallas_call(kernel, out_shape=out_shape, in_specs=[spec(i) for i in ra...]
    ppermute x15, waiting for transfers between devices: 17 us -> 18.1 us  [from_shift(): lax.ppermute(value, axis, [(i, (i - shift) % size) for i in range(size)])]
  transfers between devices with their start and end apart: 15 -> 15, of which waited for: 4 -> 5; matrix products, arithmetic and copies ran while one was open for 0% -> 0% of each run, Pallas kernels for 16% -> 11%
where the time goes in v3:
time: 45.5 us; the launch traced here: 45.4 us
  waiting for transfers between devices  18.1 us (40%)
  starting transfers between devices  15.9 us (35%)
  Pallas kernels  10.2 us (22%)
  local copies, waits for them, and re-layouts  1.04 us (2%)
    ppermute x15, waiting for transfers between devices, from_shift(): lax.ppermute(value, axis, [(i, (i - shift) % size) for i in range(size)])  18.1 us
    ppermute x15, starting transfers between devices, from_shift(): lax.ppermute(value, axis, [(i, (i - shift) % size) for i in range(size)])  15.9 us
    pallas_call x8, Pallas kernels, run(): pl.pallas_call(kernel, out_shape=out_shape, in_specs=[spec(i) for i in ra...  10.2 us
    unnamed x18, local copies, waits for them, and re-layouts  1.04 us
  transfers between devices with their start and end apart: 15, of which 5 were waited for; matrix products, arithmetic and copies ran while one was open for 0% of the time, Pallas kernels for 11%

profile of v3, /device:TPU:0, one launch (start us, length us, event | category | flops | bytes accessed | tf_op | source)
XLA Modules:
  0.0 45.4 jit_solution(5354024164525074675)
XLA Ops:
  0.0 0.0 copy-start.8
  0.0 0.0 copy-start.4
  0.0 0.0 copy-start.5
  0.0 0.0 copy-start.2
  0.0 0.7 %copy-done.8 = s32[4,4,4]{2,1,0:T(4,128)S(1)} copy-done((s32[4,4,4]{2,1,0:T(4,128)S(1)}, s32[4,4,4]{2,1,0:T(4,128)}, u32[]{:S(2)}) %copy-start.8) | copy-done | bytes 280
  0.7 0.0 copy-start.1
  0.7 0.0 copy-start.3
  0.7 0.0 copy-start
  0.7 0.0 copy-start.7
  0.7 0.1 fusion.live.refs_1_
  0.8 0.1 copy-done.4
  0.9 0.0 copy-done.5
  0.9 0.2 copy-done.2
  1.1 1.0 %shard_map.92 = (bf16[4,4,4,32,128]{4,3,2,1,0:T(8,128)(2,1)S(1)}, bf16[2,4,4,32,128]{4,3,2,1,0:T(8,128)(2,1)S(1)}, bf16[18,48,128]{2,1,0:T(8,128)(2,1)S(1)}, bf1...) custom-call(s32[8,128]{1,0:T(8,128)S(1)} %shard_map.91.token, ...), custom_call_target="tpu_custom_call" | custom-call | tf_op jit(solution)/shard_map/pallas_call | solution.py:38
  2.1 3.0 %collective-permute-start = (bf16[2,4,4,32,128]{4,3,2,1,0:T(8,128)(2,1)S(1)}, bf16[2,4,4,32,128]{4,3,2,1,0:T(8,128)(2,1)S(1)}, u32[]{:S(2)}, u32[]{:S(2)}) collective-permute-start(bf16[2,4,4,32,128]{4,3,2,1,0:T(8,128)(2,1)S(1)} %get-tuple-element.32), channel_id=1, source_target_pairs={{0,16},{16,0},{1,17},{17,1},{2,18},{18,2},{3,19},{19,3},{4,20},{20... | collective-permute-start | bytes 786440 | tf_op jit(solution)/shard_map/ppermute | solution.py:16
  5.1 1.6 %collective-permute-start.3 = (bf16[11,48,128]{2,1,0:T(8,128)(2,1)S(1)}, bf16[11,48,128]{2,1,0:T(8,128)(2,1)S(1)}, u32[]{:S(2)}, u32[]{:S(2)}) collective-permute-start(bf16[11,48,128]{2,1,0:T(8,128)(2,1)S(1)} %get-tuple-element.36), channel_id=1, source_target_pairs={{0,1},{1,2},{2,3},{3,0},{4,5},{5,6},{6,7},{7,4},{8,9},{9,10},{10,1... | collective-permute-start | bytes 405512 | tf_op jit(solution)/shard_map/ppermute | solution.py:16
  6.7 2.2 %collective-permute-start.4 = (bf16[11,48,128]{2,1,0:T(8,128)(2,1)S(1)}, bf16[11,48,128]{2,1,0:T(8,128)(2,1)S(1)}, u32[]{:S(2)}, u32[]{:S(2)}) collective-permute-start(bf16[11,48,128]{2,1,0:T(8,128)(2,1)S(1)} %get-tuple-element.37), channel_id=1, source_target_pairs={{0,3},{1,0},{2,1},{3,2},{4,7},{5,4},{6,5},{7,6},{8,11},{9,8},{10,9... | collective-permute-start | bytes 405512 | tf_op jit(solution)/shard_map/ppermute | solution.py:16
  9.0 0.8 %collective-permute-start.5 = (bf16[1,48,128]{2,1,0:T(8,128)(2,1)S(1)}, bf16[1,48,128]{2,1,0:T(8,128)(2,1)S(1)}, u32[]{:S(2)}, u32[]{:S(2)}) collective-permute-start(bf16[1,48,128]{2,1,0:T(8,128)(2,1)S(1)} %get-tuple-element.38.refs_5_), channel_id=1, source_target_pairs={{0,2},{1,3},{2,0},{3,1},{4,6},{5,7},{6,4},{7,5},{8,10},{9,11},{10,... | collective-permute-start | bytes 36872 | tf_op jit(solution)/shard_map/ppermute | solution.py:16
  9.8 0.0 collective-permute-start.1
  9.8 5.7 %collective-permute-done.5.refs_6_ = bf16[1,48,128]{2,1,0:T(8,128)(2,1)S(1)} collective-permute-done((bf16[1,48,128]{2,1,0:T(8,128)(2,1)S(1)}, bf16[1,48,128]{2,1,0:T(8,128)(2,1)S(1)}, u32[]{:S(2)}, u32[]{:S(2)}) %collective-permute-start.5) | collective-permute-done | bytes 12320 | tf_op jit(solution)/shard_map/ppermute | solution.py:16
  15.5 0.5 %collective-permute-start.2 = (bf16[992,128]{1,0:T(8,128)(2,1)S(1)}, bf16[992,128]{1,0:T(8,128)(2,1)S(1)}, u32[]{:S(2)}, u32[]{:S(2)}) collective-permute-start(bf16[992,128]{1,0:T(8,128)(2,1)S(1)} %get-tuple-element.34), channel_id=1, source_target_pairs={{0,12},{4,0},{8,4},{12,8},{1,13},{5,1},{9,5},{13,9},{2,14},{6,2},{... | collective-permute-start | bytes 761864 | tf_op jit(solution)/shard_map/ppermute | solution.py:16
  16.0 0.0 collective-permute-done.3.refs_3_.refs_5_
  16.0 0.0 collective-permute-done.4.refs_4_.refs_6_
  16.0 0.0 collective-permute-done.refs_3_.refs_1_
  16.0 0.1 shard_map.94
  16.1 0.6 %collective-permute-start.10 = (bf16[33,48,128]{2,1,0:T(8,128)(2,1)S(1)}, bf16[33,48,128]{2,1,0:T(8,128)(2,1)S(1)}, u32[]{:S(2)}, u32[]{:S(2)}) collective-permute-start(bf16[33,48,128]{2,1,0:T(8,128)(2,1)S(1)} %get-tuple-element.43.refs_2_.refs_7_), channel_id=1, source_target_pairs={{0,16},{16,0},{1,17},{17,1},{2,18},{18,2},{3,19},{19,3},{4,20},{20... | collective-permute-start | bytes 1216520 | tf_op jit(solution)/shard_map/ppermute | solution.py:16
  16.7 0.0 collective-permute-start.8
  16.7 1.7 %collective-permute-start.9 = (bf16[832,128]{1,0:T(8,128)(2,1)S(1)}, bf16[832,128]{1,0:T(8,128)(2,1)S(1)}, u32[]{:S(2)}, u32[]{:S(2)}) collective-permute-start(bf16[832,128]{1,0:T(8,128)(2,1)S(1)} %get-tuple-element.42), channel_id=1, source_target_pairs={{0,12},{4,0},{8,4},{12,8},{1,13},{5,1},{9,5},{13,9},{2,14},{6,2},{... | collective-permute-start | bytes 638984 | tf_op jit(solution)/shard_map/ppermute | solution.py:16
  18.5 0.0 collective-permute-done.1.refs_4_.refs_7_.refs_12_
  18.5 0.0 collective-permute-start.6
  18.5 2.8 %collective-permute-done.2.refs_5_.refs_8_.refs_13_ = bf16[992,128]{1,0:T(8,128)(2,1)S(1)} collective-permute-done((bf16[992,128]{1,0:T(8,128)(2,1)S(1)}, bf16[992,128]{1,0:T(8,128)(2,1)S(1)}, u32[]{:S(2)}, u32[]{:S(2)}) %collective-permute-start.2) | collective-permute-done | bytes 253984 | tf_op jit(solution)/shard_map/ppermute | solution.py:16
  21.3 1.0 %collective-permute-start.7 = (bf16[4,6,32,128]{3,2,1,0:T(8,128)(2,1)S(1)}, bf16[4,6,32,128]{3,2,1,0:T(8,128)(2,1)S(1)}, u32[]{:S(2)}, u32[]{:S(2)}) collective-permute-start(bf16[4,6,32,128]{3,2,1,0:T(8,128)(2,1)S(1)} %get-tuple-element.40), channel_id=1, source_target_pairs={{0,3},{1,0},{2,1},{3,2},{4,7},{5,4},{6,5},{7,6},{8,11},{9,8},{10,9... | collective-permute-start | bytes 589832 | tf_op jit(solution)/shard_map/ppermute | solution.py:16
  22.3 4.8 %collective-permute-done.6.refs_0_.refs_3_ = bf16[4,6,32,128]{3,2,1,0:T(8,128)(2,1)S(1)} collective-permute-done((bf16[4,6,32,128]{3,2,1,0:T(8,128)(2,1)S(1)}, bf16[4,6,32,128]{3,2,1,0:T(8,128)(2,1)S(1)}, u32[]{:S(2)}, u32[]{:S(2)}) %collective-permute-start.6) | collective-permute-done | bytes 196640 | tf_op jit(solution)/shard_map/ppermute | solution.py:16
  27.1 3.6 %collective-permute-done.7.refs_1_.refs_4_ = bf16[4,6,32,128]{3,2,1,0:T(8,128)(2,1)S(1)} collective-permute-done((bf16[4,6,32,128]{3,2,1,0:T(8,128)(2,1)S(1)}, bf16[4,6,32,128]{3,2,1,0:T(8,128)(2,1)S(1)}, u32[]{:S(2)}, u32[]{:S(2)}) %collective-permute-start.7) | collective-permute-done | bytes 196640 | tf_op jit(solution)/shard_map/ppermute | solution.py:16
  30.7 0.0 collective-permute-done.8.refs_9_.refs_5_.refs_14_
  30.7 0.0 collective-permute-done.9.refs_10_.refs_6_.refs_15_
  30.7 0.0 collective-permute-done.10.refs_3_.refs_8_
  30.7 0.1 shard_map.95
  30.8 0.2 collective-permute-start.12
  31.0 1.6 %collective-permute-start.13 = (bf16[1248,128]{1,0:T(8,128)(2,1)S(1)}, bf16[1248,128]{1,0:T(8,128)(2,1)S(1)}, u32[]{:S(2)}, u32[]{:S(2)}) collective-permute-start(bf16[1248,128]{1,0:T(8,128)(2,1)S(1)} %get-tuple-element.54), channel_id=1, source_target_pairs={{0,12},{4,0},{8,4},{12,8},{1,13},{5,1},{9,5},{13,9},{2,14},{6,2},{... | collective-permute-start | bytes 958472 | tf_op jit(solution)/shard_map/ppermute | solution.py:16
  32.6 0.0 copy-done.1
  32.6 0.0 copy-done.3
  32.6 0.4 shard_map.97
  33.0 1.6 %collective-permute-start.11 = (bf16[18,48,128]{2,1,0:T(8,128)(2,1)S(1)}, bf16[18,48,128]{2,1,0:T(8,128)(2,1)S(1)}, u32[]{:S(2)}, u32[]{:S(2)}) collective-permute-start(bf16[18,48,128]{2,1,0:T(8,128)(2,1)S(1)} %get-tuple-element.44.refs_9_), channel_id=1, source_target_pairs={{0,16},{16,0},{1,17},{17,1},{2,18},{18,2},{3,19},{19,3},{4,20},{20... | collective-permute-start | bytes 663560 | tf_op jit(solution)/shard_map/ppermute | solution.py:16
  34.6 0.0 copy-done
  34.6 0.0 copy-done.7
  34.6 0.0 copy-start.6
  34.6 2.7 %shard_map.93.refs_2_ = f32[4,512,128]{2,1,0:T(8,128)S(1)} custom-call(s32[3,27]{1,0:T(4,128)S(1)} %bitcast.3, bf16[27,128,128]{2,1,0:T(8,128)(2,1)S(1)} %copy-done, bf16[4,4,4,32,128]{4,3,2,1,0:T(8,128)(2,1)S(1)} %get-tuple-element.31.refs_2_.refs_0_, bf16[2,4,4,32,128]{4,3,2,1,0:T(8,128)(2,1)S(1)} %collective-permute-done.refs_3_.refs_1_, ...), custom_call_target="tpu_custom_call" | custom-call | flops 1811939328 | tf_op jit(solution)/shard_map/pallas_call | solution.py:38
  37.3 1.0 %collective-permute-start.14 = (bf16[2,48,128]{2,1,0:T(8,128)(2,1)S(1)}, bf16[2,48,128]{2,1,0:T(8,128)(2,1)S(1)}, u32[]{:S(2)}, u32[]{:S(2)}) collective-permute-start(bf16[2,48,128]{2,1,0:T(8,128)(2,1)S(1)} %get-tuple-element.55.refs_18_), channel_id=1, source_target_pairs={{0,8},{4,12},{8,0},{12,4},{1,9},{5,13},{9,1},{13,5},{2,10},{6,14},... | collective-permute-start | bytes 73736 | tf_op jit(solution)/shard_map/ppermute | solution.py:16
  38.4 1.7 %shard_map.96 = (f32[4,512,128]{2,1,0:T(8,128)S(1)}, bf16[320,48,128]{2,1,0:T(8,128)(2,1)S(1)}, bf16[150,48,128]{2,1,0:T(8,128)(2,1)S(1)}, bf16[2,2,128,384]{3,2,1,0:T(8,128)(2,1)S(1)}) custom-call(s32[3,27]{1,0:T(4,128)S(1)} %bitcast.4, bf16[27,128,128]{2,1,0:T(8,128)(2,1)S(1)} %copy-done, ...), custom_call_target="tpu_custom_call", output_to_operand_aliasing={{0}: (2, {})} | custom-call | flops 603979776 | tf_op jit(solution)/shard_map/pallas_call | solution.py:38
  40.1 1.1 %collective-permute-done.14.refs_19_ = bf16[2,48,128]{2,1,0:T(8,128)(2,1)S(1)} collective-permute-done((bf16[2,48,128]{2,1,0:T(8,128)(2,1)S(1)}, bf16[2,48,128]{2,1,0:T(8,128)(2,1)S(1)}, u32[]{:S(2)}, u32[]{:S(2)}) %collective-permute-start.14) | collective-permute-done | bytes 24608 | tf_op jit(solution)/shard_map/ppermute | solution.py:16
  41.2 0.0 collective-permute-done.11.refs_11_
  41.2 0.0 collective-permute-done.12.refs_16_
  41.2 0.0 collective-permute-done.13.refs_17_
  41.2 0.0 copy-done.6
  41.2 4.1 %shard_map.98 = (f32[4,4,4,32,128]{4,3,2,1,0:T(8,128)}, bf16[320,48,128]{2,1,0:T(8,128)(2,1)S(1)}, bf16[150,48,128]{2,1,0:T(8,128)(2,1)S(1)}) custom-call(s32[3,2,32]{2,1,0:T(2,128)S(1)} %bitcast.2, f32[4,4,4,128]{3,2,1,0:T(4,128)S(1)} %fusion.live.refs_1_, ...), custom_call_target="tpu_custom_call", output_to_operand_aliasing={{1}: (9, {}), {2}: (10, {})} | custom-call | tf_op jit(solution)/shard_map/pallas_call | solution.py:38
  (1 shorter events, 0.0 us)
Async XLA Ops:
  0.0 0.7 %copy-start.8 = (s32[4,4,4]{2,1,0:T(4,128)S(1)}, s32[4,4,4]{2,1,0:T(4,128)}, u32[]{:S(2)}) copy-start(s32[4,4,4]{2,1,0:T(4,128)} %param.10) | copy-start | bytes 772
  0.0 0.9 %copy-start.4 = (bf16[8,48,48]{2,1,0:T(8,128)(2,1)S(1)}, bf16[8,48,48]{2,1,0:T(8,128)(2,1)}, u32[]{:S(2)}) copy-start(bf16[8,48,48]{2,1,0:T(8,128)(2,1)} %transfer.3) | copy-start | bytes 110596
  0.0 0.9 %copy-start.5 = (bf16[48,128]{1,0:T(8,128)(2,1)S(1)}, bf16[48,128]{1,0:T(8,128)(2,1)}, u32[]{:S(2)}) copy-start(bf16[48,128]{1,0:T(8,128)(2,1)} %refs_4_.1) | copy-start | bytes 36868
  0.0 1.1 %copy-start.2 = (bf16[4,4,4,32,128]{4,3,2,1,0:T(8,128)(2,1)S(1)}, bf16[4,4,4,32,128]{4,3,2,1,0:T(8,128)(2,1)}, u32[]{:S(2)}) copy-start(bf16[4,4,4,32,128]{4,3,2,1,0:T(8,128)(2,1)} %charges.1) | copy-start | bytes 1572868
  0.7 31.9 %copy-start.1 = (bf16[2,32,48,48]{3,2,1,0:T(8,128)(2,1)S(1)}, bf16[2,32,48,48]{3,2,1,0:T(8,128)(2,1)}, u32[]{:S(2)}) copy-start(bf16[2,32,48,48]{3,2,1,0:T(8,128)(2,1)} %coupling_in.1) | copy-start | bytes 884740
  0.7 31.9 %copy-start.3 = (bf16[2,4,4,48,48]{4,3,2,1,0:T(8,128)(2,1)S(1)}, bf16[2,4,4,48,48]{4,3,2,1,0:T(8,128)(2,1)}, u32[]{:S(2)}) copy-start(bf16[2,4,4,48,48]{4,3,2,1,0:T(8,128)(2,1)} %coarse_in.1) | copy-start | bytes 442372
  0.7 33.9 %copy-start = (bf16[27,128,128]{2,1,0:T(8,128)(2,1)S(1)}, bf16[27,128,128]{2,1,0:T(8,128)(2,1)}, u32[]{:S(2)}) copy-start(bf16[27,128,128]{2,1,0:T(8,128)(2,1)} %refs_1_.3) | copy-start | bytes 2654212
  0.7 33.9 %copy-start.7 = (s32[27,3]{0,1:T(4,128)S(1)}, s32[27,3]{0,1:T(4,128)}, u32[]{:S(2)}) copy-start(s32[27,3]{0,1:T(4,128)} %param.11) | copy-start | bytes 976
  2.1 13.9 %collective-permute-start = (bf16[2,4,4,32,128]{4,3,2,1,0:T(8,128)(2,1)S(1)}, bf16[2,4,4,32,128]{4,3,2,1,0:T(8,128)(2,1)S(1)}, u32[]{:S(2)}, u32[]{:S(2)}) collective-permute-start(bf16[2,4,4,32,128]{4,3,2,1,0:T(8,128)(2,1)S(1)} %get-tuple-element.32), channel_id=1, source_target_pairs={{0,16},{16,0},{1,17},{17,1},{2,18},{18,2},{3,19},{19,3},{4,20},{20... | collective-permute-start | bytes 786440 | tf_op jit(solution)/shard_map/ppermute | solution.py:16
  5.1 10.8 %collective-permute-start.3 = (bf16[11,48,128]{2,1,0:T(8,128)(2,1)S(1)}, bf16[11,48,128]{2,1,0:T(8,128)(2,1)S(1)}, u32[]{:S(2)}, u32[]{:S(2)}) collective-permute-start(bf16[11,48,128]{2,1,0:T(8,128)(2,1)S(1)} %get-tuple-element.36), channel_id=1, source_target_pairs={{0,1},{1,2},{2,3},{3,0},{4,5},{5,6},{6,7},{7,4},{8,9},{9,10},{10,1... | collective-permute-start | bytes 405512 | tf_op jit(solution)/shard_map/ppermute | solution.py:16
  6.7 9.3 %collective-permute-start.4 = (bf16[11,48,128]{2,1,0:T(8,128)(2,1)S(1)}, bf16[11,48,128]{2,1,0:T(8,128)(2,1)S(1)}, u32[]{:S(2)}, u32[]{:S(2)}) collective-permute-start(bf16[11,48,128]{2,1,0:T(8,128)(2,1)S(1)} %get-tuple-element.37), channel_id=1, source_target_pairs={{0,3},{1,0},{2,1},{3,2},{4,7},{5,4},{6,5},{7,6},{8,11},{9,8},{10,9... | collective-permute-start | bytes 405512 | tf_op jit(solution)/shard_map/ppermute | solution.py:16
  9.0 6.5 %collective-permute-start.5 = (bf16[1,48,128]{2,1,0:T(8,128)(2,1)S(1)}, bf16[1,48,128]{2,1,0:T(8,128)(2,1)S(1)}, u32[]{:S(2)}, u32[]{:S(2)}) collective-permute-start(bf16[1,48,128]{2,1,0:T(8,128)(2,1)S(1)} %get-tuple-element.38.refs_5_), channel_id=1, source_target_pairs={{0,2},{1,3},{2,0},{3,1},{4,6},{5,7},{6,4},{7,5},{8,10},{9,11},{10,... | collective-permute-start | bytes 36872 | tf_op jit(solution)/shard_map/ppermute | solution.py:16
  9.8 8.7 %collective-permute-start.1 = (bf16[992,128]{1,0:T(8,128)(2,1)S(1)}, bf16[992,128]{1,0:T(8,128)(2,1)S(1)}, u32[]{:S(2)}, u32[]{:S(2)}) collective-permute-start(bf16[992,128]{1,0:T(8,128)(2,1)S(1)} %get-tuple-element.33), channel_id=1, source_target_pairs={{0,4},{4,8},{8,12},{12,0},{1,5},{5,9},{9,13},{13,1},{2,6},{6,10},{... | collective-permute-start | bytes 761864 | tf_op jit(solution)/shard_map/ppermute | solution.py:16
  15.5 5.8 %collective-permute-start.2 = (bf16[992,128]{1,0:T(8,128)(2,1)S(1)}, bf16[992,128]{1,0:T(8,128)(2,1)S(1)}, u32[]{:S(2)}, u32[]{:S(2)}) collective-permute-start(bf16[992,128]{1,0:T(8,128)(2,1)S(1)} %get-tuple-element.34), channel_id=1, source_target_pairs={{0,12},{4,0},{8,4},{12,8},{1,13},{5,1},{9,5},{13,9},{2,14},{6,2},{... | collective-permute-start | bytes 761864 | tf_op jit(solution)/shard_map/ppermute | solution.py:16
  16.1 14.6 %collective-permute-start.10 = (bf16[33,48,128]{2,1,0:T(8,128)(2,1)S(1)}, bf16[33,48,128]{2,1,0:T(8,128)(2,1)S(1)}, u32[]{:S(2)}, u32[]{:S(2)}) collective-permute-start(bf16[33,48,128]{2,1,0:T(8,128)(2,1)S(1)} %get-tuple-element.43.refs_2_.refs_7_), channel_id=1, source_target_pairs={{0,16},{16,0},{1,17},{17,1},{2,18},{18,2},{3,19},{19,3},{4,20},{20... | collective-permute-start | bytes 1216520 | tf_op jit(solution)/shard_map/ppermute | solution.py:16
  16.7 14.0 %collective-permute-start.8 = (bf16[832,128]{1,0:T(8,128)(2,1)S(1)}, bf16[832,128]{1,0:T(8,128)(2,1)S(1)}, u32[]{:S(2)}, u32[]{:S(2)}) collective-permute-start(bf16[832,128]{1,0:T(8,128)(2,1)S(1)} %get-tuple-element.41), channel_id=1, source_target_pairs={{0,4},{4,8},{8,12},{12,0},{1,5},{5,9},{9,13},{13,1},{2,6},{6,10},{... | collective-permute-start | bytes 638984 | tf_op jit(solution)/shard_map/ppermute | solution.py:16
  16.7 14.0 %collective-permute-start.9 = (bf16[832,128]{1,0:T(8,128)(2,1)S(1)}, bf16[832,128]{1,0:T(8,128)(2,1)S(1)}, u32[]{:S(2)}, u32[]{:S(2)}) collective-permute-start(bf16[832,128]{1,0:T(8,128)(2,1)S(1)} %get-tuple-element.42), channel_id=1, source_target_pairs={{0,12},{4,0},{8,4},{12,8},{1,13},{5,1},{9,5},{13,9},{2,14},{6,2},{... | collective-permute-start | bytes 638984 | tf_op jit(solution)/shard_map/ppermute | solution.py:16
  18.5 8.7 %collective-permute-start.6 = (bf16[4,6,32,128]{3,2,1,0:T(8,128)(2,1)S(1)}, bf16[4,6,32,128]{3,2,1,0:T(8,128)(2,1)S(1)}, u32[]{:S(2)}, u32[]{:S(2)}) collective-permute-start(bf16[4,6,32,128]{3,2,1,0:T(8,128)(2,1)S(1)} %get-tuple-element.39), channel_id=1, source_target_pairs={{0,1},{1,2},{2,3},{3,0},{4,5},{5,6},{6,7},{7,4},{8,9},{9,10},{10,1... | collective-permute-start | bytes 589832 | tf_op jit(solution)/shard_map/ppermute | solution.py:16
  21.3 9.4 %collective-permute-start.7 = (bf16[4,6,32,128]{3,2,1,0:T(8,128)(2,1)S(1)}, bf16[4,6,32,128]{3,2,1,0:T(8,128)(2,1)S(1)}, u32[]{:S(2)}, u32[]{:S(2)}) collective-permute-start(bf16[4,6,32,128]{3,2,1,0:T(8,128)(2,1)S(1)} %get-tuple-element.40), channel_id=1, source_target_pairs={{0,3},{1,0},{2,1},{3,2},{4,7},{5,4},{6,5},{7,6},{8,11},{9,8},{10,9... | collective-permute-start | bytes 589832 | tf_op jit(solution)/shard_map/ppermute | solution.py:16
  30.8 10.4 %collective-permute-start.12 = (bf16[1248,128]{1,0:T(8,128)(2,1)S(1)}, bf16[1248,128]{1,0:T(8,128)(2,1)S(1)}, u32[]{:S(2)}, u32[]{:S(2)}) collective-permute-start(bf16[1248,128]{1,0:T(8,128)(2,1)S(1)} %get-tuple-element.53), channel_id=1, source_target_pairs={{0,4},{4,8},{8,12},{12,0},{1,5},{5,9},{9,13},{13,1},{2,6},{6,10},{... | collective-permute-start | bytes 958472 | tf_op jit(solution)/shard_map/ppermute | solution.py:16
  31.0 10.3 %collective-permute-start.13 = (bf16[1248,128]{1,0:T(8,128)(2,1)S(1)}, bf16[1248,128]{1,0:T(8,128)(2,1)S(1)}, u32[]{:S(2)}, u32[]{:S(2)}) collective-permute-start(bf16[1248,128]{1,0:T(8,128)(2,1)S(1)} %get-tuple-element.54), channel_id=1, source_target_pairs={{0,12},{4,0},{8,4},{12,8},{1,13},{5,1},{9,5},{13,9},{2,14},{6,2},{... | collective-permute-start | bytes 958472 | tf_op jit(solution)/shard_map/ppermute | solution.py:16
  33.0 8.2 %collective-permute-start.11 = (bf16[18,48,128]{2,1,0:T(8,128)(2,1)S(1)}, bf16[18,48,128]{2,1,0:T(8,128)(2,1)S(1)}, u32[]{:S(2)}, u32[]{:S(2)}) collective-permute-start(bf16[18,48,128]{2,1,0:T(8,128)(2,1)S(1)} %get-tuple-element.44.refs_9_), channel_id=1, source_target_pairs={{0,16},{16,0},{1,17},{17,1},{2,18},{18,2},{3,19},{19,3},{4,20},{20... | collective-permute-start | bytes 663560 | tf_op jit(solution)/shard_map/ppermute | solution.py:16
  34.6 6.7 %copy-start.6 = (s32[2,32,3]{1,0,2:T(2,128)S(1)}, s32[2,32,3]{1,0,2:T(2,128)}, u32[]{:S(2)}) copy-start(s32[2,32,3]{1,0,2:T(2,128)} %param.15) | copy-start | bytes 2308
  37.3 3.9 %collective-permute-start.14 = (bf16[2,48,128]{2,1,0:T(8,128)(2,1)S(1)}, bf16[2,48,128]{2,1,0:T(8,128)(2,1)S(1)}, u32[]{:S(2)}, u32[]{:S(2)}) collective-permute-start(bf16[2,48,128]{2,1,0:T(8,128)(2,1)S(1)} %get-tuple-element.55.refs_18_), channel_id=1, source_target_pairs={{0,8},{4,12},{8,0},{12,4},{1,9},{5,13},{9,1},{13,5},{2,10},{6,14},... | collective-permute-start | bytes 73736 | tf_op jit(solution)/shard_map/ppermute | solution.py:16

commit v4 on v3

--- a/solution.py
+++ b/solution.py
@@ -190,7 +190,7 @@
     before, after = read.faces(geo)
     mom, prev, nxt, mine = read.take(4)
     far = read.take(geo["extra_z"])
-    c_high, c_low, wide, y_high, y_low = read.take(5)
+    c_high, c_low, wide, y_high, y_low, line = read.take(6)
     for z in range(bz + 4):
         for y in range(by):
             if z < 2:
@@ -200,7 +200,6 @@
             else:
                 tile = mom[(z - 2) * by + y]
             wide[z * by + y] = tile
-    first = (bz + 4) * by
 
     def load(key):
         if key == 0:
@@ -212,7 +211,10 @@
         return far[key - 2][0]
 
     for t, tile in enumerate(assemble([(k, 0) for k in range(nz)], rhs, load)):
-        wide[first + t] = tile
+        line[t] = tile
+        at = 2 * bz * rhs + (12 + t) * rank
+        y_high[at : at + rank] = tile
+        y_low[at : at + rank] = tile
     for out, z in ((c_high, bz - 1), (c_low, 0)):
         for y in range(by):
             out[y, 0] = before[z, y]
@@ -237,14 +239,32 @@
 
 
 def third_kernel(geo, *refs):
-    nx, nz, xs, bx, by, bz, rhs, rank = (geo[k] for k in ("nx", "nz", "xs", "bx", "by", "bz", "rhs", "rank"))
+    xs, bx, by, bz, rhs, rank = (geo[k] for k in ("xs", "bx", "by", "bz", "rhs", "rank"))
     read = Reader(refs)
     prev, nxt = read.take(2)
-    sources = read.take(xs)
+    sources = [None] + read.take(xs - 1)
+    y_high, y_low = read.take(2)
+    base = 2 * (bx + 2) * rhs
+    for out, y in ((y_high, by - 1), (y_low, 0)):
+        for k, s in enumerate((prev, nxt)):
+            at = k * (bx + 2) * rhs
+            out[at : at + (bx + 2) * rhs] = s[y].reshape((bx + 2) * rhs, s.shape[3])
+        start = by - 2 if y else 0
+        for k in range(1, xs):
+            for z in range(bz + 4):
+                for yy in range(2):
+                    at = base + (((k - 1) * (bz + 4) + z) * 2 + yy) * rank
+                    out[at : at + rank] = sources[k][z * by + start + yy]
+
+
+def column_kernel(geo, *refs):
+    ny, bx, by, bz, rhs, rank = (geo[k] for k in ("ny", "bx", "by", "bz", "rhs", "rank"))
+    read = Reader(refs)
     mom, mz_prev, mz_next = read.take(3)
     y1, y2 = read.take(2), read.take(2)
-    far = read.take(geo["extra_x"])
-    y_high, y_low, one, two = read.take(4)
+    (line,) = read.take(1)
+    far = read.take(geo["extra_y"])
+    (one,) = read.take(1)
     base1 = bz * bx * rhs
     base2 = 2 * bz * rhs
     for yb in range(3):
@@ -257,36 +277,16 @@
                 else:
                     tile = tile_at(y2[yb // 2], base2 + (8 + (zb // 2) * 2 + z) * rank, rank)
                 one[(yb * 3 + zb) * 2 + z] = tile
-    base = 2 * (bx + 2) * rhs
-    first = (bz + 4) * by
-    for out, y in ((y_high, by - 1), (y_low, 0)):
-        for k, s in enumerate((prev, nxt)):
-            at = k * (bx + 2) * rhs
-            out[at : at + (bx + 2) * rhs] = s[y].reshape((bx + 2) * rhs, s.shape[3])
-        start = by - 2 if y else 0
-        for k in range(1, xs):
-            for z in range(bz + 4):
-                for yy in range(2):
-                    at = base + (((k - 1) * (bz + 4) + z) * 2 + yy) * rank
-                    out[at : at + rank] = sources[k][z * by + start + yy]
-    per = 128 // rhs
-    order = [((s, b // per), b % per) for s in range(nx) for b in range(nz)]
-
-    def load(key):
-        s, t = key
-        if s == 0:
-            return sources[0][first + t]
-        if s == 1:
-            return sources[xs - 1][first + t]
-        if s == nx - 1:
-            return sources[1][first + t]
-        return far[s - 2][t]
-
-    for t, tile in enumerate(assemble(order, rhs, load)):
-        at = base + ((xs - 1) * 2 * (bz + 4) + t) * rank
-        y_high[at : at + rank] = tile
-        y_low[at : at + rank] = tile
-        two[t] = tile
+    tiles = line.shape[0]
+    for s in range(ny):
+        for t in range(tiles):
+            if s == 0:
+                tile = line[t]
+            elif s == 1 or s == ny - 1:
+                tile = tile_at(y2[1 if s == 1 else 0], base2 + (12 + t) * rank, rank)
+            else:
+                tile = far[s - 2][t]
+            one[18 + s * tiles + t] = tile
 
 
 def near_weights(inverse, near_blocks, codes):
@@ -428,7 +428,7 @@
         coupling[level] = jnp.concatenate([coupling_in[level, e] for e in range(entries)], axis=1)
     nx, ny, nz = coarse_in.shape[:3]
     coarse[...] = jnp.concatenate(
-        [coarse_in[x, y, z] for y in range(ny) for x in range(nx) for z in range(nz)], axis=1
+        [coarse_in[x, y, z] for x in range(nx) for y in range(ny) for z in range(nz)], axis=1
     )
     turned = [transfer[c].astype(F32).T.astype(BF16) for c in range(8)]
     for c in range(8):
@@ -447,8 +447,8 @@
     read.take(2)
     beside = read.take(xs - 1)
     y1, y2, y3 = read.take(2), read.take(2), read.take(2)
-    (mine_two,) = read.take(1)
-    far_two = read.take(geo["extra_y"])
+    (one,) = read.take(1)
+    far_two = read.take(geo["extra_x"])
     out, shifts, ones = read.take(3)
     corners, planes, far_table, sems = read.take(4)
     table_copy = pltpu.make_async_copy(far_in, far_table, sems.at[bz])
@@ -486,23 +486,26 @@
             at = (15 + m) * 6 + z
             ones[at] = jnp.where(masks.odd, roll(after, width), ones[at])
 
-    start_two = base3 + (xs - 1) * 2 * (bz + 4) * rank
     per = 128 // width
+    tiles = -(-nz // per)
 
     def two_tile(s, t):
         if s == 0:
-            return mine_two[t]
-        if s == 1 or s == ny - 1:
-            return tile_at(y3[1 if s == 1 else 0], start_two + t * rank, rank)
+            return one[18 + t]
+        if s == 1:
+            return beside[-1][18 + t]
+        if s == nx - 1:
+            return beside[0][18 + t]
         return far_two[s - 2][t]
 
     lanes = lax.broadcasted_iota(jnp.int16, (rank, 128), 1)
     quarter = [(lanes >= jnp.int16(width * b)) & (lanes < jnp.int16(width * (b + 1))) for b in range(per)]
     stacked = []
-    for s in range(ny):
-        for b in range(nz * nx):
-            tile = two_tile(s, b // per)
-            stacked.append(jnp.where(quarter[b % per], tile, jnp.zeros_like(tile)))
+    for s in range(nx):
+        for y in range(ny):
+            for b in range(nz):
+                tile = two_tile(s, y * tiles + b // per)
+                stacked.append(jnp.where(quarter[b % per], tile, jnp.zeros_like(tile)))
     two = dot(coarse[...], jnp.concatenate(stacked, axis=0))
     two = two + roll(two, 2 * width)
     two = (two + roll(two, width)).astype(BF16)
@@ -594,7 +597,6 @@
     geo["extra_y"] = max(ny - 3, 0)
     per = 128 // rhs
     tiles_z = -(-nz // per)
-    tiles_x = -(-nx * nz // per)
 
     def shape(*dims, dtype=BF16):
         return jax.ShapeDtypeStruct(dims, dtype)
@@ -644,10 +646,10 @@
     )
 
     charge = shape(by, bx + 2, rhs, pts)
-    message = shape(2 * bz * rhs + 12 * rank, 128)
-    c_high, c_low, wide, y_high, y_low = run(
+    message = shape(2 * bz * rhs + (12 + tiles_z) * rank, 128)
+    c_high, c_low, wide, y_high, y_low, line = run(
         part(second_kernel),
-        (charge, charge, shape((bz + 4) * by + tiles_z, rank, 128), message, message),
+        (charge, charge, shape((bz + 4) * by, rank, 128), message, message, shape(tiles_z, rank, 128)),
         (own, *faces, mom, mz_prev, mz_next, two, *extra),
     )
     if nx == 2:
@@ -657,7 +659,7 @@
     cz_prev = from_shift(c_high, "gz", nz, -1)
     cz_next = from_shift(c_low, "gz", nz, 1)
     y2 = [from_shift(y_high, "gy", ny, -1), from_shift(y_low, "gy", ny, 1)]
-    extra = [from_shift(wide[-tiles_z:], "gx", nx, s) for s in range(2, nx - 1)]
+    extra = [from_shift(line, "gy", ny, s) for s in range(2, ny - 1)]
 
     field = shape(bz, by * bx * rhs, pts, dtype=F32)
     near = run(
@@ -673,18 +675,15 @@
         flops=2 * bx * by * bz * rhs * pts * pts * stencil,
     )
 
-    message = shape(2 * (bx + 2) * rhs + ((xs - 1) * 2 * (bz + 4) + tiles_x) * rank, 128)
-    y_high, y_low, one, two = run(
-        part(third_kernel),
-        (message, message, shape(18, rank, 128), shape(tiles_x, rank, 128)),
-        (cz_prev, cz_next, *sources, mom, mz_prev, mz_next, *y1, *y2, *extra),
-    )
+    message = shape(2 * (bx + 2) * rhs + (xs - 1) * 2 * (bz + 4) * rank, 128)
+    y_high, y_low = run(part(third_kernel), (message, message), (cz_prev, cz_next, *sources[1:]))
+    one = run(part(column_kernel), shape(18 + ny * tiles_z, rank, 128), (mom, mz_prev, mz_next, *y1, *y2, line, *extra))
     if nx == 2:
         beside = [from_shift(one, "gx", nx, 1)]
     else:
         beside = [from_shift(one, "gx", nx, -1), from_shift(one, "gx", nx, 1)]
     y3 = [from_shift(y_high, "gy", ny, -1), from_shift(y_low, "gy", ny, 1)]
-    extra = [from_shift(two, "gy", ny, s) for s in range(2, ny - 1)]
+    extra = [from_shift(one[18:], "gx", nx, s) for s in range(2, nx - 1)]
 
     windows = shape(5 * (bz + 4) * (by + 4), rank, 128)
     columns = shape(5 * 5 * 6, rank, 128)
@@ -714,7 +713,7 @@
         *y1,
         *y2,
         *y3,
-        two,
+        one,
         *extra,
     )
     potentials, _, _ = run(

time: 45.5 us -> 51.3 us (1.13)
  starting transfers between devices: 15.9 us -> 19.3 us
  waiting for transfers between devices: 18.1 us -> 20.6 us
    ppermute x15, starting transfers between devices: 15.9 us -> 19.3 us  [from_shift(): lax.ppermute(value, axis, [(i, (i - shift) % size) for i in range(size)])]
    ppermute x15, waiting for transfers between devices: 18.1 us -> 20.6 us  [from_shift(): lax.ppermute(value, axis, [(i, (i - shift) % size) for i in range(size)])]
    pallas_call x8 -> x9, Pallas kernels: 10.2 us -> 9.98 us  [run(): pl.pallas_call(kernel, out_shape=out_shape, in_specs=[spec(i) for i in ra...]
  transfers between devices with their start and end apart: 15 -> 15, of which waited for: 5 -> 6; matrix products, arithmetic and copies ran while one was open for 0% -> 0% of each run, Pallas kernels for 11% -> 10%
where the time goes in v4:
time: 51.3 us; the launch traced here: 51.2 us
  waiting for transfers between devices  20.6 us (40%)
  starting transfers between devices  19.3 us (38%)
  Pallas kernels  9.98 us (19%)
  local copies, waits for them, and re-layouts  1.04 us (2%)
    ppermute x15, waiting for transfers between devices, from_shift(): lax.ppermute(value, axis, [(i, (i - shift) % size) for i in range(size)])  20.6 us
    ppermute x15, starting transfers between devices, from_shift(): lax.ppermute(value, axis, [(i, (i - shift) % size) for i in range(size)])  19.3 us
    pallas_call x9, Pallas kernels, run(): pl.pallas_call(kernel, out_shape=out_shape, in_specs=[spec(i) for i in ra...  9.98 us
    unnamed x18, local copies, waits for them, and re-layouts  1.04 us
  transfers between devices with their start and end apart: 15, of which 6 were waited for; matrix products, arithmetic and copies ran while one was open for 0% of the time, Pallas kernels for 10%

profile of v4, /device:TPU:0, one launch (start us, length us, event | category | flops | bytes accessed | tf_op | source)
XLA Modules:
  0.0 51.2 jit_solution(4332172764708158647)
XLA Ops:
  0.0 0.0 copy-start.8
  0.0 0.0 copy-start.4
  0.0 0.0 copy-start.5
  0.0 0.0 copy-start.2
  0.0 0.7 %copy-done.8 = s32[4,4,4]{2,1,0:T(4,128)S(1)} copy-done((s32[4,4,4]{2,1,0:T(4,128)S(1)}, s32[4,4,4]{2,1,0:T(4,128)}, u32[]{:S(2)}) %copy-start.8) | copy-done | bytes 280
  0.7 0.0 copy-start.1
  0.7 0.0 copy-start.3
  0.7 0.0 copy-start
  0.7 0.0 copy-start.7
  0.7 0.1 fusion.live.refs_1_
  0.8 0.1 copy-done.4
  0.9 0.0 copy-done.5
  0.9 0.2 copy-done.2
  1.1 1.0 %shard_map.92 = (bf16[4,4,4,32,128]{4,3,2,1,0:T(8,128)(2,1)S(1)}, bf16[2,4,4,32,128]{4,3,2,1,0:T(8,128)(2,1)S(1)}, bf16[18,48,128]{2,1,0:T(8,128)(2,1)S(1)}, bf1...) custom-call(s32[8,128]{1,0:T(8,128)S(1)} %shard_map.91.token, ...), custom_call_target="tpu_custom_call" | custom-call | tf_op jit(solution)/shard_map/pallas_call | solution.py:38
  2.1 3.0 %collective-permute-start = (bf16[2,4,4,32,128]{4,3,2,1,0:T(8,128)(2,1)S(1)}, bf16[2,4,4,32,128]{4,3,2,1,0:T(8,128)(2,1)S(1)}, u32[]{:S(2)}, u32[]{:S(2)}) collective-permute-start(bf16[2,4,4,32,128]{4,3,2,1,0:T(8,128)(2,1)S(1)} %get-tuple-element.31), channel_id=1, source_target_pairs={{0,16},{16,0},{1,17},{17,1},{2,18},{18,2},{3,19},{19,3},{4,20},{20... | collective-permute-start | bytes 786440 | tf_op jit(solution)/shard_map/ppermute | solution.py:16
  5.1 1.6 %collective-permute-start.3 = (bf16[11,48,128]{2,1,0:T(8,128)(2,1)S(1)}, bf16[11,48,128]{2,1,0:T(8,128)(2,1)S(1)}, u32[]{:S(2)}, u32[]{:S(2)}) collective-permute-start(bf16[11,48,128]{2,1,0:T(8,128)(2,1)S(1)} %get-tuple-element.35), channel_id=1, source_target_pairs={{0,1},{1,2},{2,3},{3,0},{4,5},{5,6},{6,7},{7,4},{8,9},{9,10},{10,1... | collective-permute-start | bytes 405512 | tf_op jit(solution)/shard_map/ppermute | solution.py:16
  6.7 2.2 %collective-permute-start.4 = (bf16[11,48,128]{2,1,0:T(8,128)(2,1)S(1)}, bf16[11,48,128]{2,1,0:T(8,128)(2,1)S(1)}, u32[]{:S(2)}, u32[]{:S(2)}) collective-permute-start(bf16[11,48,128]{2,1,0:T(8,128)(2,1)S(1)} %get-tuple-element.36), channel_id=1, source_target_pairs={{0,3},{1,0},{2,1},{3,2},{4,7},{5,4},{6,5},{7,6},{8,11},{9,8},{10,9... | collective-permute-start | bytes 405512 | tf_op jit(solution)/shard_map/ppermute | solution.py:16
  9.0 0.8 %collective-permute-start.5 = (bf16[1,48,128]{2,1,0:T(8,128)(2,1)S(1)}, bf16[1,48,128]{2,1,0:T(8,128)(2,1)S(1)}, u32[]{:S(2)}, u32[]{:S(2)}) collective-permute-start(bf16[1,48,128]{2,1,0:T(8,128)(2,1)S(1)} %get-tuple-element.37.refs_5_), channel_id=1, source_target_pairs={{0,2},{1,3},{2,0},{3,1},{4,6},{5,7},{6,4},{7,5},{8,10},{9,11},{10,... | collective-permute-start | bytes 36872 | tf_op jit(solution)/shard_map/ppermute | solution.py:16
  9.7 5.7 %collective-permute-done.5.refs_6_ = bf16[1,48,128]{2,1,0:T(8,128)(2,1)S(1)} collective-permute-done((bf16[1,48,128]{2,1,0:T(8,128)(2,1)S(1)}, bf16[1,48,128]{2,1,0:T(8,128)(2,1)S(1)}, u32[]{:S(2)}, u32[]{:S(2)}) %collective-permute-start.5) | collective-permute-done | bytes 12320 | tf_op jit(solution)/shard_map/ppermute | solution.py:16
  15.5 0.0 collective-permute-done.3.refs_3_.refs_1_
  15.5 0.0 collective-permute-done.4.refs_4_.refs_2_
  15.5 0.0 collective-permute-done.refs_3_.refs_1_
  15.5 0.1 shard_map.94
  15.6 0.5 collective-permute-start.6
  16.1 3.4 %collective-permute-start.7 = (bf16[4,6,32,128]{3,2,1,0:T(8,128)(2,1)S(1)}, bf16[4,6,32,128]{3,2,1,0:T(8,128)(2,1)S(1)}, u32[]{:S(2)}, u32[]{:S(2)}) collective-permute-start(bf16[4,6,32,128]{3,2,1,0:T(8,128)(2,1)S(1)} %get-tuple-element.39), channel_id=1, source_target_pairs={{0,3},{1,0},{2,1},{3,2},{4,7},{5,4},{6,5},{7,6},{8,11},{9,8},{10,9... | collective-permute-start | bytes 589832 | tf_op jit(solution)/shard_map/ppermute | solution.py:16
  19.5 0.5 %collective-permute-start.10 = (bf16[32,48,128]{2,1,0:T(8,128)(2,1)S(1)}, bf16[32,48,128]{2,1,0:T(8,128)(2,1)S(1)}, u32[]{:S(2)}, u32[]{:S(2)}) collective-permute-start(bf16[32,48,128]{2,1,0:T(8,128)(2,1)S(1)} %get-tuple-element.42.refs_7_), channel_id=1, source_target_pairs={{0,16},{16,0},{1,17},{17,1},{2,18},{18,2},{3,19},{19,3},{4,20},{20... | collective-permute-start | bytes 1179656 | tf_op jit(solution)/shard_map/ppermute | solution.py:16
  20.0 0.0 collective-permute-start.1
  20.0 1.7 %collective-permute-start.2 = (bf16[992,128]{1,0:T(8,128)(2,1)S(1)}, bf16[992,128]{1,0:T(8,128)(2,1)S(1)}, u32[]{:S(2)}, u32[]{:S(2)}) collective-permute-start(bf16[992,128]{1,0:T(8,128)(2,1)S(1)} %get-tuple-element.33), channel_id=1, source_target_pairs={{0,12},{4,0},{8,4},{12,8},{1,13},{5,1},{9,5},{13,9},{2,14},{6,2},{... | collective-permute-start | bytes 761864 | tf_op jit(solution)/shard_map/ppermute | solution.py:16
  21.8 3.5 %collective-permute-done.6.refs_3_.refs_0_ = bf16[4,6,32,128]{3,2,1,0:T(8,128)(2,1)S(1)} collective-permute-done((bf16[4,6,32,128]{3,2,1,0:T(8,128)(2,1)S(1)}, bf16[4,6,32,128]{3,2,1,0:T(8,128)(2,1)S(1)}, u32[]{:S(2)}, u32[]{:S(2)}) %collective-permute-start.6) | collective-permute-done | bytes 196640 | tf_op jit(solution)/shard_map/ppermute | solution.py:16
  25.2 0.0 collective-permute-start.8
  25.2 1.1 %collective-permute-done.7.refs_4_.refs_1_ = bf16[4,6,32,128]{3,2,1,0:T(8,128)(2,1)S(1)} collective-permute-done((bf16[4,6,32,128]{3,2,1,0:T(8,128)(2,1)S(1)}, bf16[4,6,32,128]{3,2,1,0:T(8,128)(2,1)S(1)}, u32[]{:S(2)}, u32[]{:S(2)}) %collective-permute-start.7) | collective-permute-done | bytes 196640 | tf_op jit(solution)/shard_map/ppermute | solution.py:16
  26.4 0.6 %collective-permute-start.9 = (bf16[880,128]{1,0:T(8,128)(2,1)S(1)}, bf16[880,128]{1,0:T(8,128)(2,1)S(1)}, u32[]{:S(2)}, u32[]{:S(2)}) collective-permute-start(bf16[880,128]{1,0:T(8,128)(2,1)S(1)} %get-tuple-element.41), channel_id=1, source_target_pairs={{0,12},{4,0},{8,4},{12,8},{1,13},{5,1},{9,5},{13,9},{2,14},{6,2},{... | collective-permute-start | bytes 675848 | tf_op jit(solution)/shard_map/ppermute | solution.py:16
  27.0 2.3 %collective-permute-done.10.refs_8_.refs_2_ = bf16[32,48,128]{2,1,0:T(8,128)(2,1)S(1)} collective-permute-done((bf16[32,48,128]{2,1,0:T(8,128)(2,1)S(1)}, bf16[32,48,128]{2,1,0:T(8,128)(2,1)S(1)}, u32[]{:S(2)}, u32[]{:S(2)}) %collective-permute-start.10) | collective-permute-done | bytes 393248 | tf_op jit(solution)/shard_map/ppermute | solution.py:16
  29.4 0.1 collective-permute-start.13
  29.4 0.0 collective-permute-done.1.refs_4_.refs_3_.refs_12_
  29.5 1.7 %collective-permute-start.14 = (bf16[1152,128]{1,0:T(8,128)(2,1)S(1)}, bf16[1152,128]{1,0:T(8,128)(2,1)S(1)}, u32[]{:S(2)}, u32[]{:S(2)}) collective-permute-start(bf16[1152,128]{1,0:T(8,128)(2,1)S(1)} %get-tuple-element.53), channel_id=1, source_target_pairs={{0,12},{4,0},{8,4},{12,8},{1,13},{5,1},{9,5},{13,9},{2,14},{6,2},{... | collective-permute-start | bytes 884744 | tf_op jit(solution)/shard_map/ppermute | solution.py:16
  31.2 0.0 collective-permute-done.2.refs_5_.refs_4_.refs_13_
  31.2 1.5 %collective-permute-start.11 = (bf16[1,48,128]{2,1,0:T(8,128)(2,1)S(1)}, bf16[1,48,128]{2,1,0:T(8,128)(2,1)S(1)}, u32[]{:S(2)}, u32[]{:S(2)}) collective-permute-start(bf16[1,48,128]{2,1,0:T(8,128)(2,1)S(1)} %get-tuple-element.43.refs_7_), channel_id=1, source_target_pairs={{0,8},{4,12},{8,0},{12,4},{1,9},{5,13},{9,1},{13,5},{2,10},{6,14},... | collective-permute-start | bytes 36872 | tf_op jit(solution)/shard_map/ppermute | solution.py:16
  32.7 7.2 %collective-permute-done.11.refs_8_ = bf16[1,48,128]{2,1,0:T(8,128)(2,1)S(1)} collective-permute-done((bf16[1,48,128]{2,1,0:T(8,128)(2,1)S(1)}, bf16[1,48,128]{2,1,0:T(8,128)(2,1)S(1)}, u32[]{:S(2)}, u32[]{:S(2)}) %collective-permute-start.11) | collective-permute-done | bytes 12320 | tf_op jit(solution)/shard_map/ppermute | solution.py:16
  39.9 0.0 collective-permute-done.8.refs_5_.refs_14_
  39.9 0.0 collective-permute-done.9.refs_6_.refs_15_
  39.9 1.6 %collective-permute-start.12 = (bf16[22,48,128]{2,1,0:T(8,128)(2,1)S(1)}, bf16[22,48,128]{2,1,0:T(8,128)(2,1)S(1)}, u32[]{:S(2)}, u32[]{:S(2)}) collective-permute-start(bf16[22,48,128]{2,1,0:T(8,128)(2,1)S(1)} %shard_map.95.refs_9_.refs_18_), channel_id=1, source_target_pairs={{0,16},{16,0},{1,17},{17,1},{2,18},{18,2},{3,19},{19,3},{4,20},{20... | collective-permute-start | bytes 811016 | tf_op jit(solution)/shard_map/ppermute | solution.py:16
  41.5 0.0 copy-done.1
  41.5 0.0 copy-done.3
  41.5 0.4 shard_map.97
  41.9 0.0 copy-done
  41.9 0.0 copy-done.7
  41.9 0.0 copy-start.6
  41.9 2.7 %shard_map.93.refs_2_ = f32[4,512,128]{2,1,0:T(8,128)S(1)} custom-call(s32[3,27]{1,0:T(4,128)S(1)} %bitcast.3, bf16[27,128,128]{2,1,0:T(8,128)(2,1)S(1)} %copy-done, bf16[4,4,4,32,128]{4,3,2,1,0:T(8,128)(2,1)S(1)} %get-tuple-element.30.refs_2_.refs_0_, bf16[2,4,4,32,128]{4,3,2,1,0:T(8,128)(2,1)S(1)} %collective-permute-done.refs_3_.refs_1_, ...), custom_call_target="tpu_custom_call" | custom-call | flops 1811939328 | tf_op jit(solution)/shard_map/pallas_call | solution.py:38
  44.7 1.8 %shard_map.96 = (f32[4,512,128]{2,1,0:T(8,128)S(1)}, bf16[320,48,128]{2,1,0:T(8,128)(2,1)S(1)}, bf16[150,48,128]{2,1,0:T(8,128)(2,1)S(1)}, bf16[2,2,128,384]{3,2,1,0:T(8,128)(2,1)S(1)}) custom-call(s32[3,27]{1,0:T(4,128)S(1)} %bitcast.4, bf16[27,128,128]{2,1,0:T(8,128)(2,1)S(1)} %copy-done, ...), custom_call_target="tpu_custom_call", output_to_operand_aliasing={{0}: (2, {})} | custom-call | flops 603979776 | tf_op jit(solution)/shard_map/pallas_call | solution.py:38
  46.4 0.8 %collective-permute-done.12.refs_11_ = bf16[22,48,128]{2,1,0:T(8,128)(2,1)S(1)} collective-permute-done((bf16[22,48,128]{2,1,0:T(8,128)(2,1)S(1)}, bf16[22,48,128]{2,1,0:T(8,128)(2,1)S(1)}, u32[]{:S(2)}, u32[]{:S(2)}) %collective-permute-start.12) | collective-permute-done | bytes 270368 | tf_op jit(solution)/shard_map/ppermute | solution.py:16
  47.2 0.0 collective-permute-done.13.refs_16_
  47.2 0.0 collective-permute-done.14.refs_17_
  47.2 0.0 copy-done.6
  47.2 3.9 %shard_map.99 = (f32[4,4,4,32,128]{4,3,2,1,0:T(8,128)}, bf16[320,48,128]{2,1,0:T(8,128)(2,1)S(1)}, bf16[150,48,128]{2,1,0:T(8,128)(2,1)S(1)}) custom-call(s32[3,2,32]{2,1,0:T(2,128)S(1)} %bitcast.2, f32[4,4,4,128]{3,2,1,0:T(4,128)S(1)} %fusion.live.refs_1_, ...), custom_call_target="tpu_custom_call", output_to_operand_aliasing={{1}: (9, {}), {2}: (10, {})} | custom-call | tf_op jit(solution)/shard_map/pallas_call | solution.py:38
  (3 shorter events, 0.1 us)
Async XLA Ops:
  0.0 0.7 %copy-start.8 = (s32[4,4,4]{2,1,0:T(4,128)S(1)}, s32[4,4,4]{2,1,0:T(4,128)}, u32[]{:S(2)}) copy-start(s32[4,4,4]{2,1,0:T(4,128)} %param.10) | copy-start | bytes 772
  0.0 0.9 %copy-start.4 = (bf16[8,48,48]{2,1,0:T(8,128)(2,1)S(1)}, bf16[8,48,48]{2,1,0:T(8,128)(2,1)}, u32[]{:S(2)}) copy-start(bf16[8,48,48]{2,1,0:T(8,128)(2,1)} %transfer.3) | copy-start | bytes 110596
  0.0 0.9 %copy-start.5 = (bf16[48,128]{1,0:T(8,128)(2,1)S(1)}, bf16[48,128]{1,0:T(8,128)(2,1)}, u32[]{:S(2)}) copy-start(bf16[48,128]{1,0:T(8,128)(2,1)} %refs_4_.1) | copy-start | bytes 36868
  0.0 1.1 %copy-start.2 = (bf16[4,4,4,32,128]{4,3,2,1,0:T(8,128)(2,1)S(1)}, bf16[4,4,4,32,128]{4,3,2,1,0:T(8,128)(2,1)}, u32[]{:S(2)}) copy-start(bf16[4,4,4,32,128]{4,3,2,1,0:T(8,128)(2,1)} %charges.1) | copy-start | bytes 1572868
  0.7 40.8 %copy-start.1 = (bf16[2,32,48,48]{3,2,1,0:T(8,128)(2,1)S(1)}, bf16[2,32,48,48]{3,2,1,0:T(8,128)(2,1)}, u32[]{:S(2)}) copy-start(bf16[2,32,48,48]{3,2,1,0:T(8,128)(2,1)} %coupling_in.1) | copy-start | bytes 884740
  0.7 40.8 %copy-start.3 = (bf16[2,4,4,48,48]{4,3,2,1,0:T(8,128)(2,1)S(1)}, bf16[2,4,4,48,48]{4,3,2,1,0:T(8,128)(2,1)}, u32[]{:S(2)}) copy-start(bf16[2,4,4,48,48]{4,3,2,1,0:T(8,128)(2,1)} %coarse_in.1) | copy-start | bytes 442372
  0.7 41.2 %copy-start = (bf16[27,128,128]{2,1,0:T(8,128)(2,1)S(1)}, bf16[27,128,128]{2,1,0:T(8,128)(2,1)}, u32[]{:S(2)}) copy-start(bf16[27,128,128]{2,1,0:T(8,128)(2,1)} %refs_1_.3) | copy-start | bytes 2654212
  0.7 41.2 %copy-start.7 = (s32[27,3]{0,1:T(4,128)S(1)}, s32[27,3]{0,1:T(4,128)}, u32[]{:S(2)}) copy-start(s32[27,3]{0,1:T(4,128)} %param.11) | copy-start | bytes 976
  2.1 13.4 %collective-permute-start = (bf16[2,4,4,32,128]{4,3,2,1,0:T(8,128)(2,1)S(1)}, bf16[2,4,4,32,128]{4,3,2,1,0:T(8,128)(2,1)S(1)}, u32[]{:S(2)}, u32[]{:S(2)}) collective-permute-start(bf16[2,4,4,32,128]{4,3,2,1,0:T(8,128)(2,1)S(1)} %get-tuple-element.31), channel_id=1, source_target_pairs={{0,16},{16,0},{1,17},{17,1},{2,18},{18,2},{3,19},{19,3},{4,20},{20... | collective-permute-start | bytes 786440 | tf_op jit(solution)/shard_map/ppermute | solution.py:16
  5.1 10.3 %collective-permute-start.3 = (bf16[11,48,128]{2,1,0:T(8,128)(2,1)S(1)}, bf16[11,48,128]{2,1,0:T(8,128)(2,1)S(1)}, u32[]{:S(2)}, u32[]{:S(2)}) collective-permute-start(bf16[11,48,128]{2,1,0:T(8,128)(2,1)S(1)} %get-tuple-element.35), channel_id=1, source_target_pairs={{0,1},{1,2},{2,3},{3,0},{4,5},{5,6},{6,7},{7,4},{8,9},{9,10},{10,1... | collective-permute-start | bytes 405512 | tf_op jit(solution)/shard_map/ppermute | solution.py:16
  6.7 8.8 %collective-permute-start.4 = (bf16[11,48,128]{2,1,0:T(8,128)(2,1)S(1)}, bf16[11,48,128]{2,1,0:T(8,128)(2,1)S(1)}, u32[]{:S(2)}, u32[]{:S(2)}) collective-permute-start(bf16[11,48,128]{2,1,0:T(8,128)(2,1)S(1)} %get-tuple-element.36), channel_id=1, source_target_pairs={{0,3},{1,0},{2,1},{3,2},{4,7},{5,4},{6,5},{7,6},{8,11},{9,8},{10,9... | collective-permute-start | bytes 405512 | tf_op jit(solution)/shard_map/ppermute | solution.py:16
  9.0 6.5 %collective-permute-start.5 = (bf16[1,48,128]{2,1,0:T(8,128)(2,1)S(1)}, bf16[1,48,128]{2,1,0:T(8,128)(2,1)S(1)}, u32[]{:S(2)}, u32[]{:S(2)}) collective-permute-start(bf16[1,48,128]{2,1,0:T(8,128)(2,1)S(1)} %get-tuple-element.37.refs_5_), channel_id=1, source_target_pairs={{0,2},{1,3},{2,0},{3,1},{4,6},{5,7},{6,4},{7,5},{8,10},{9,11},{10,... | collective-permute-start | bytes 36872 | tf_op jit(solution)/shard_map/ppermute | solution.py:16
  15.6 9.6 %collective-permute-start.6 = (bf16[4,6,32,128]{3,2,1,0:T(8,128)(2,1)S(1)}, bf16[4,6,32,128]{3,2,1,0:T(8,128)(2,1)S(1)}, u32[]{:S(2)}, u32[]{:S(2)}) collective-permute-start(bf16[4,6,32,128]{3,2,1,0:T(8,128)(2,1)S(1)} %get-tuple-element.38), channel_id=1, source_target_pairs={{0,1},{1,2},{2,3},{3,0},{4,5},{5,6},{6,7},{7,4},{8,9},{9,10},{10,1... | collective-permute-start | bytes 589832 | tf_op jit(solution)/shard_map/ppermute | solution.py:16
  16.1 10.3 %collective-permute-start.7 = (bf16[4,6,32,128]{3,2,1,0:T(8,128)(2,1)S(1)}, bf16[4,6,32,128]{3,2,1,0:T(8,128)(2,1)S(1)}, u32[]{:S(2)}, u32[]{:S(2)}) collective-permute-start(bf16[4,6,32,128]{3,2,1,0:T(8,128)(2,1)S(1)} %get-tuple-element.39), channel_id=1, source_target_pairs={{0,3},{1,0},{2,1},{3,2},{4,7},{5,4},{6,5},{7,6},{8,11},{9,8},{10,9... | collective-permute-start | bytes 589832 | tf_op jit(solution)/shard_map/ppermute | solution.py:16
  19.5 9.8 %collective-permute-start.10 = (bf16[32,48,128]{2,1,0:T(8,128)(2,1)S(1)}, bf16[32,48,128]{2,1,0:T(8,128)(2,1)S(1)}, u32[]{:S(2)}, u32[]{:S(2)}) collective-permute-start(bf16[32,48,128]{2,1,0:T(8,128)(2,1)S(1)} %get-tuple-element.42.refs_7_), channel_id=1, source_target_pairs={{0,16},{16,0},{1,17},{17,1},{2,18},{18,2},{3,19},{19,3},{4,20},{20... | collective-permute-start | bytes 1179656 | tf_op jit(solution)/shard_map/ppermute | solution.py:16
  20.0 9.4 %collective-permute-start.1 = (bf16[992,128]{1,0:T(8,128)(2,1)S(1)}, bf16[992,128]{1,0:T(8,128)(2,1)S(1)}, u32[]{:S(2)}, u32[]{:S(2)}) collective-permute-start(bf16[992,128]{1,0:T(8,128)(2,1)S(1)} %get-tuple-element.32), channel_id=1, source_target_pairs={{0,4},{4,8},{8,12},{12,0},{1,5},{5,9},{9,13},{13,1},{2,6},{6,10},{... | collective-permute-start | bytes 761864 | tf_op jit(solution)/shard_map/ppermute | solution.py:16
  20.0 11.2 %collective-permute-start.2 = (bf16[992,128]{1,0:T(8,128)(2,1)S(1)}, bf16[992,128]{1,0:T(8,128)(2,1)S(1)}, u32[]{:S(2)}, u32[]{:S(2)}) collective-permute-start(bf16[992,128]{1,0:T(8,128)(2,1)S(1)} %get-tuple-element.33), channel_id=1, source_target_pairs={{0,12},{4,0},{8,4},{12,8},{1,13},{5,1},{9,5},{13,9},{2,14},{6,2},{... | collective-permute-start | bytes 761864 | tf_op jit(solution)/shard_map/ppermute | solution.py:16
  25.2 14.6 %collective-permute-start.8 = (bf16[880,128]{1,0:T(8,128)(2,1)S(1)}, bf16[880,128]{1,0:T(8,128)(2,1)S(1)}, u32[]{:S(2)}, u32[]{:S(2)}) collective-permute-start(bf16[880,128]{1,0:T(8,128)(2,1)S(1)} %get-tuple-element.40), channel_id=1, source_target_pairs={{0,4},{4,8},{8,12},{12,0},{1,5},{5,9},{9,13},{13,1},{2,6},{6,10},{... | collective-permute-start | bytes 675848 | tf_op jit(solution)/shard_map/ppermute | solution.py:16
  26.4 13.5 %collective-permute-start.9 = (bf16[880,128]{1,0:T(8,128)(2,1)S(1)}, bf16[880,128]{1,0:T(8,128)(2,1)S(1)}, u32[]{:S(2)}, u32[]{:S(2)}) collective-permute-start(bf16[880,128]{1,0:T(8,128)(2,1)S(1)} %get-tuple-element.41), channel_id=1, source_target_pairs={{0,12},{4,0},{8,4},{12,8},{1,13},{5,1},{9,5},{13,9},{2,14},{6,2},{... | collective-permute-start | bytes 675848 | tf_op jit(solution)/shard_map/ppermute | solution.py:16
  29.4 17.9 %collective-permute-start.13 = (bf16[1152,128]{1,0:T(8,128)(2,1)S(1)}, bf16[1152,128]{1,0:T(8,128)(2,1)S(1)}, u32[]{:S(2)}, u32[]{:S(2)}) collective-permute-start(bf16[1152,128]{1,0:T(8,128)(2,1)S(1)} %get-tuple-element.52), channel_id=1, source_target_pairs={{0,4},{4,8},{8,12},{12,0},{1,5},{5,9},{9,13},{13,1},{2,6},{6,10},{... | collective-permute-start | bytes 884744 | tf_op jit(solution)/shard_map/ppermute | solution.py:16
  29.5 17.8 %collective-permute-start.14 = (bf16[1152,128]{1,0:T(8,128)(2,1)S(1)}, bf16[1152,128]{1,0:T(8,128)(2,1)S(1)}, u32[]{:S(2)}, u32[]{:S(2)}) collective-permute-start(bf16[1152,128]{1,0:T(8,128)(2,1)S(1)} %get-tuple-element.53), channel_id=1, source_target_pairs={{0,12},{4,0},{8,4},{12,8},{1,13},{5,1},{9,5},{13,9},{2,14},{6,2},{... | collective-permute-start | bytes 884744 | tf_op jit(solution)/shard_map/ppermute | solution.py:16
  31.2 8.7 %collective-permute-start.11 = (bf16[1,48,128]{2,1,0:T(8,128)(2,1)S(1)}, bf16[1,48,128]{2,1,0:T(8,128)(2,1)S(1)}, u32[]{:S(2)}, u32[]{:S(2)}) collective-permute-start(bf16[1,48,128]{2,1,0:T(8,128)(2,1)S(1)} %get-tuple-element.43.refs_7_), channel_id=1, source_target_pairs={{0,8},{4,12},{8,0},{12,4},{1,9},{5,13},{9,1},{13,5},{2,10},{6,14},... | collective-permute-start | bytes 36872 | tf_op jit(solution)/shard_map/ppermute | solution.py:16
  39.9 7.3 %collective-permute-start.12 = (bf16[22,48,128]{2,1,0:T(8,128)(2,1)S(1)}, bf16[22,48,128]{2,1,0:T(8,128)(2,1)S(1)}, u32[]{:S(2)}, u32[]{:S(2)}) collective-permute-start(bf16[22,48,128]{2,1,0:T(8,128)(2,1)S(1)} %shard_map.95.refs_9_.refs_18_), channel_id=1, source_target_pairs={{0,16},{16,0},{1,17},{17,1},{2,18},{18,2},{3,19},{19,3},{4,20},{20... | collective-permute-start | bytes 811016 | tf_op jit(solution)/shard_map/ppermute | solution.py:16
  41.9 5.3 %copy-start.6 = (s32[2,32,3]{1,0,2:T(2,128)S(1)}, s32[2,32,3]{1,0,2:T(2,128)}, u32[]{:S(2)}) copy-start(s32[2,32,3]{1,0,2:T(2,128)} %param.15) | copy-start | bytes 2308

commit v5 on v4

--- a/solution.py
+++ b/solution.py
@@ -92,6 +92,44 @@
 
 def start_kernel(out):
     out[...] = jnp.zeros(out.shape, out.dtype)
+
+
+def lift(transfer, groups, width):
+    sums = [None, None]
+    for i in range(2):
+        for j in range(2):
+            for l in range(2):
+                cols = jnp.concatenate([g[l][2 * y + j] for g in groups for y in range(2)], axis=1)
+                part = dot(transfer[4 * i + 2 * j + l], cols)
+                sums[i] = part if sums[i] is None else sums[i] + part
+    blocks = lane_blocks(sums[0].shape[0], width)
+    tiles = []
+    for z in range(len(groups)):
+        whole = []
+        for y in range(2):
+            at = 128 * (z * 2 + y)
+            whole.append(sums[0][:, at : at + 128] + roll(sums[1][:, at : at + 128], -width))
+        packed = jnp.where(
+            blocks == 0,
+            whole[0],
+            jnp.where(
+                blocks == 1,
+                roll(whole[0], -width),
+                jnp.where(blocks == 2, roll(whole[1], 2 * width), roll(whole[1], width)),
+            ),
+        )
+        tiles.append(packed.astype(BF16))
+    return tiles
+
+
+def fold(tile, width):
+    masks = Masks(16, width)
+    rows = [tile[16 * k : 16 * (k + 1)] for k in range(3)]
+    return jnp.where(masks.first, rows[0], jnp.where(masks.lower, roll(rows[1], width), roll(rows[2], 2 * width)))
+
+
+def unfold(rows, width):
+    return jnp.concatenate([rows, roll(rows, -width), roll(rows, -2 * width)], axis=0)
 
 
 def first_kernel(token, live, charges, basis, transfer, own, faces, mom, z_high, z_low, y_high, y_low, two):
@@ -122,50 +160,27 @@
                 tile = value[:, 128 * k : 128 * (k + 1)]
                 leaf[z, y + k] = tile
                 mom[z * by + y + k] = tile
-                (z_low if z < 2 else z_high)[z % 2 * by + y + k] = tile
+                at = (z % 2 * by + y + k) * rank
+                (z_low if z < 2 else z_high)[at : at + rank] = tile
                 at = base + (z * 2 + k) * rank
                 (y_low if y == 0 else y_high)[at : at + rank] = tile
-    sums = [None, None]
-    for i in range(2):
-        for j in range(2):
-            for l in range(2):
-                cols = jnp.concatenate([leaf[2 * z + l, 2 * y + j] for z in range(2) for y in range(2)], axis=1)
-                part = dot(transfer[4 * i + 2 * j + l], cols)
-                sums[i] = part if sums[i] is None else sums[i] + part
-    blocks = lane_blocks(rank, width)
-    first = bz * by
-    one = []
+    one = lift(transfer, [[[leaf[2 * z + l, y] for y in range(by)] for l in range(2)] for z in range(2)], width)
     for z in range(2):
-        whole = []
-        for y in range(2):
-            at = 128 * (z * 2 + y)
-            whole.append(sums[0][:, at : at + 128] + roll(sums[1][:, at : at + 128], -width))
-        packed = jnp.where(
-            blocks == 0,
-            whole[0],
-            jnp.where(
-                blocks == 1,
-                roll(whole[0], -width),
-                jnp.where(blocks == 2, roll(whole[1], 2 * width), roll(whole[1], width)),
-            ),
-        ).astype(BF16)
-        one.append(packed)
-        mom[first + z] = packed
-        z_high[2 * by + z] = packed
-        z_low[2 * by + z] = packed
+        mom[bz * by + z] = one[z]
+        (z_low if z else z_high)[2 * by * rank : (2 * by + 1) * rank] = one[z]
         at = base + (2 * bz + z) * rank
-        y_high[at : at + rank] = packed
-        y_low[at : at + rank] = packed
+        y_high[at : at + rank] = one[z]
+        y_low[at : at + rank] = one[z]
     total = None
     for j in range(2):
         for i in range(2):
             part = dot(transfer[4 * i + 2 * j], one[0]) + dot(transfer[4 * i + 2 * j + 1], one[1])
             part = roll(part, -width * (2 * j + i))
             total = part if total is None else total + part
-    total = total.astype(BF16)
-    z_high[2 * by + 2] = total
-    z_low[2 * by + 2] = total
-    two[0] = total
+    total = fold(total.astype(BF16), width)
+    z_high[(2 * by + 1) * rank :] = total
+    z_low[(2 * by + 1) * rank :] = total
+    two[...] = total
 
 
 class Reader:
@@ -184,43 +199,48 @@
 
 
 def second_kernel(geo, *refs):
-    nz, bx, by, bz, rhs, rank = (geo[k] for k in ("nz", "bx", "by", "bz", "rhs", "rank"))
+    bx, by, bz, rank = (geo[k] for k in ("bx", "by", "bz", "rank"))
     read = Reader(refs)
     (own,) = read.take(1)
     before, after = read.faces(geo)
-    mom, prev, nxt, mine = read.take(4)
-    far = read.take(geo["extra_z"])
-    c_high, c_low, wide, y_high, y_low, line = read.take(6)
+    mom, prev, nxt = read.take(3)
+    c_high, c_low, wide = read.take(3)
     for z in range(bz + 4):
         for y in range(by):
             if z < 2:
-                tile = prev[z * by + y]
+                tile = tile_at(prev, (z * by + y) * rank, rank)
             elif z >= bz + 2:
-                tile = nxt[(z - bz - 2) * by + y]
+                tile = tile_at(nxt, ((z - bz - 2) * by + y) * rank, rank)
             else:
                 tile = mom[(z - 2) * by + y]
             wide[z * by + y] = tile
-
-    def load(key):
-        if key == 0:
-            return mine[0]
-        if key == 1:
-            return nxt[2 * by + 2]
-        if key == nz - 1:
-            return prev[2 * by + 2]
-        return far[key - 2][0]
-
-    for t, tile in enumerate(assemble([(k, 0) for k in range(nz)], rhs, load)):
-        line[t] = tile
-        at = 2 * bz * rhs + (12 + t) * rank
-        y_high[at : at + rank] = tile
-        y_low[at : at + rank] = tile
     for out, z in ((c_high, bz - 1), (c_low, 0)):
         for y in range(by):
             out[y, 0] = before[z, y]
             out[y, 1 : bx + 1] = own[z, y]
             out[y, bx + 1] = after[z, y]
+
+
+def sides_kernel(geo, *refs):
+    nz, _, by, bz, rhs, rank = (geo[k] for k in ("nz", "bx", "by", "bz", "rhs", "rank"))
+    read = Reader(refs)
+    before, after = read.faces(geo)
+    transfer, prev, nxt, mine = read.take(4)
+    far = read.take(geo["extra_z"])
+    y_high, y_low, line, halo = read.take(4)
+
+    def leaf(s, z, y):
+        return tile_at(s, (z * by + y) * rank, rank)
+
+    near = lift(transfer, [[[leaf(s, l, y) for y in range(by)] for l in range(2)] for s in (prev, nxt)], rhs)
+    sent = [tile_at(s, 2 * by * rank, rank) for s in (prev, nxt)]
+    level = [sent[0], near[0], near[1], sent[1]]
     base = 2 * bz * rhs
+    for z in range(4):
+        halo[z] = level[z]
+        at = base + (8 + z) * rank
+        y_high[at : at + rank] = level[z]
+        y_low[at : at + rank] = level[z]
     for out, y in ((y_high, by - 1), (y_low, 0)):
         for k, s in enumerate((before, after)):
             for z in range(bz):
@@ -228,14 +248,24 @@
                 out[at : at + rhs] = s[z, y]
         start = by - 2 if y else 0
         for zh in range(4):
-            s = prev if zh < 2 else nxt
             for yy in range(2):
                 at = base + (zh * 2 + yy) * rank
-                out[at : at + rank] = s[zh % 2 * by + start + yy]
-        for side, s in enumerate((prev, nxt)):
-            for z in range(2):
-                at = base + (8 + side * 2 + z) * rank
-                out[at : at + rank] = s[2 * by + z]
+                out[at : at + rank] = leaf(prev if zh < 2 else nxt, zh % 2, start + yy)
+
+    def load(key):
+        if key == 0:
+            return unfold(mine[...], rhs)
+        if key == 1:
+            return unfold(nxt[(2 * by + 1) * rank :, :], rhs)
+        if key == nz - 1:
+            return unfold(prev[(2 * by + 1) * rank :, :], rhs)
+        return unfold(far[key - 2][...], rhs)
+
+    for t, tile in enumerate(assemble([(k, 0) for k in range(nz)], rhs, load)):
+        line[t] = tile
+        at = base + (12 + t) * rank
+        y_high[at : at + rank] = tile
+        y_low[at : at + rank] = tile
 
 
 def third_kernel(geo, *refs):
@@ -257,26 +287,35 @@
                     out[at : at + rank] = sources[k][z * by + start + yy]
 
 
+def sent_index(yb, z):
+    left_out = [(1, k) for k in range(1, 5)]
+    order = [(b, k) for b in range(3) for k in range(6) if (b, k) not in left_out]
+    return order.index((yb, z)) if (yb, z) in order else None
+
+
 def column_kernel(geo, *refs):
     ny, bx, by, bz, rhs, rank = (geo[k] for k in ("ny", "bx", "by", "bz", "rhs", "rank"))
     read = Reader(refs)
-    mom, mz_prev, mz_next = read.take(3)
+    mom, halo = read.take(2)
     y1, y2 = read.take(2), read.take(2)
     (line,) = read.take(1)
     far = read.take(geo["extra_y"])
-    (one,) = read.take(1)
+    one, send = read.take(2)
     base1 = bz * bx * rhs
     base2 = 2 * bz * rhs
     for yb in range(3):
-        for zb in range(3):
-            for z in range(2):
-                if yb == 1:
-                    tile = mom[bz * by + z] if zb == 1 else (mz_prev if zb == 0 else mz_next)[2 * by + z]
-                elif zb == 1:
-                    tile = tile_at(y1[yb // 2], base1 + (2 * bz + z) * rank, rank)
-                else:
-                    tile = tile_at(y2[yb // 2], base2 + (8 + (zb // 2) * 2 + z) * rank, rank)
-                one[(yb * 3 + zb) * 2 + z] = tile
+        for z in range(6):
+            inside = z in (2, 3)
+            if yb == 1:
+                tile = mom[bz * by + z - 2] if inside else halo[z if z < 2 else z - 2]
+            elif inside:
+                tile = tile_at(y1[yb // 2], base1 + (2 * bz + z - 2) * rank, rank)
+            else:
+                tile = tile_at(y2[yb // 2], base2 + (8 + (z if z < 2 else z - 2)) * rank, rank)
+            one[yb * 6 + z] = tile
+            at = sent_index(yb, z)
+            if at is not None:
+                send[at] = tile
     tiles = line.shape[0]
     for s in range(ny):
         for t in range(tiles):
@@ -286,7 +325,7 @@
                 tile = tile_at(y2[1 if s == 1 else 0], base2 + (12 + t) * rank, rank)
             else:
                 tile = far[s - 2][t]
-            one[18 + s * tiles + t] = tile
+            send[14 + s * tiles + t] = tile
 
 
 def near_weights(inverse, near_blocks, codes):
@@ -371,11 +410,12 @@
     read = Reader(refs)
     table, near_blocks = read.take(2)
     read.take(1)
+    (transfer,) = read.take(1)
     cz_prev, cz_next = read.take(2)
     y2 = read.take(2)
     sources = read.take(xs)
     (one,) = read.take(1)
-    out, shifts, ones, corner_weights, wide, inverse = read.take(6)
+    out, shifts, ones, corner_weights, lifted, wide, inverse = read.take(7)
     pts = wide.shape[3]
     find_inverse(table, inverse, near_blocks.shape[0])
     rows = (bx + 2) * rhs
@@ -411,6 +451,12 @@
             tiles = [s[z * by + y] for s in sources]
             at = z * (by + 4) + y + 2
             store_windows(shifts, at, (bz + 4) * (by + 4), masks, rhs, tiles[0], tiles[1], tiles[-1])
+    for k in range(1, xs):
+        groups = [
+            [[sources[k][(2 * z + l) * by + y] for y in range(by)] for l in range(2)] for z in range(bz // 2 + 2)
+        ]
+        for z, tile in enumerate(lift(transfer, groups, rhs)):
+            lifted[(k - 1) * 4 + z] = tile
     for z in range(6):
         for m, mid in enumerate(windows_y(masks, rhs, [one[yb * 6 + z] for yb in range(3)])):
             ones[(10 + m) * 6 + z] = mid
@@ -447,7 +493,7 @@
     read.take(2)
     beside = read.take(xs - 1)
     y1, y2, y3 = read.take(2), read.take(2), read.take(2)
-    (one,) = read.take(1)
+    lifted, send = read.take(2)
     far_two = read.take(geo["extra_x"])
     out, shifts, ones = read.take(3)
     corners, planes, far_table, sems = read.take(4)
@@ -475,8 +521,12 @@
                 at = (z + 2) * (by + 4) + yy + side * (by + 2)
                 store_windows(shifts, at, (bz + 4) * (by + 4), masks, width, tiles[0], tiles[1], tiles[-1])
 
+    def one_tile(k, yb, z):
+        at = sent_index(yb, z)
+        return lifted[k * 4 + z - 1] if at is None else beside[k][at]
+
     for z in range(6):
-        sides = [windows_y(masks, width, [s[yb * 6 + z] for yb in range(3)]) for s in beside]
+        sides = [windows_y(masks, width, [one_tile(k, yb, z) for yb in range(3)]) for k in range(xs - 1)]
         for m in range(5):
             before, after = sides[0][m], sides[-1][m]
             ones[m * 6 + z] = before
@@ -491,11 +541,11 @@
 
     def two_tile(s, t):
         if s == 0:
-            return one[18 + t]
+            return send[14 + t]
         if s == 1:
-            return beside[-1][18 + t]
+            return beside[-1][14 + t]
         if s == nx - 1:
-            return beside[0][18 + t]
+            return beside[0][14 + t]
         return far_two[s - 2][t]
 
     lanes = lax.broadcasted_iota(jnp.int16, (rank, 128), 1)
@@ -609,7 +659,8 @@
     far_table = far_offsets.transpose(2, 0, 1)
 
     token = run(start_kernel, shape(8, 128, dtype=jnp.int32), (), flops=10**10)
-    side = shape(2 * by + 3, rank, 128)
+    assert rank == 48
+    side = shape((2 * by + 1) * rank + 16, 128)
     message = shape(bz * bx * rhs + (bz * 2 + 2) * rank, 128)
     own, faces, mom, z_high, z_low, y_high, y_low, two = run(
         first_kernel,
@@ -621,7 +672,7 @@
             side,
             message,
             message,
-            shape(1, rank, 128),
+            shape(16, 128),
         ),
         (token, live, charges, leaf_basis, transfer),
     )
@@ -646,11 +697,14 @@
     )
 
     charge = shape(by, bx + 2, rhs, pts)
+    c_high, c_low, wide = run(
+        part(second_kernel), (charge, charge, shape((bz + 4) * by, rank, 128)), (own, *faces, mom, mz_prev, mz_next)
+    )
     message = shape(2 * bz * rhs + (12 + tiles_z) * rank, 128)
-    c_high, c_low, wide, y_high, y_low, line = run(
-        part(second_kernel),
-        (charge, charge, shape((bz + 4) * by, rank, 128), message, message, shape(tiles_z, rank, 128)),
-        (own, *faces, mom, mz_prev, mz_next, two, *extra),
+    y_high, y_low, line, halo = run(
+        part(sides_kernel),
+        (message, message, shape(tiles_z, rank, 128), shape(4, rank, 128)),
+        (*faces, transfer, mz_prev, mz_next, two, *extra),
     )
     if nx == 2:
         sources = [wide, from_shift(wide, "gx", nx, 1)]
@@ -677,20 +731,24 @@
 
     message = shape(2 * (bx + 2) * rhs + (xs - 1) * 2 * (bz + 4) * rank, 128)
     y_high, y_low = run(part(third_kernel), (message, message), (cz_prev, cz_next, *sources[1:]))
-    one = run(part(column_kernel), shape(18 + ny * tiles_z, rank, 128), (mom, mz_prev, mz_next, *y1, *y2, line, *extra))
+    one, send = run(
+        part(column_kernel),
+        (shape(18, rank, 128), shape(14 + ny * tiles_z, rank, 128)),
+        (mom, halo, *y1, *y2, line, *extra),
+    )
     if nx == 2:
-        beside = [from_shift(one, "gx", nx, 1)]
+        beside = [from_shift(send, "gx", nx, 1)]
     else:
-        beside = [from_shift(one, "gx", nx, -1), from_shift(one, "gx", nx, 1)]
+        beside = [from_shift(send, "gx", nx, -1), from_shift(send, "gx", nx, 1)]
     y3 = [from_shift(y_high, "gy", ny, -1), from_shift(y_low, "gy", ny, 1)]
-    extra = [from_shift(one[18:], "gx", nx, s) for s in range(2, nx - 1)]
+    extra = [from_shift(send[14:], "gx", nx, s) for s in range(2, nx - 1)]
 
     windows = shape(5 * (bz + 4) * (by + 4), rank, 128)
     columns = shape(5 * 5 * 6, rank, 128)
-    near, shifts, ones, corner_weights = run(
+    near, shifts, ones, corner_weights, lifted = run(
         part(near_kernel),
-        (field, windows, columns, shape(2, 2, pts, 3 * pts)),
-        (near_table, near_blocks, near, cz_prev, cz_next, *y2, *sources, one),
+        (field, windows, columns, shape(2, 2, pts, 3 * pts), shape((xs - 1) * 4, rank, 128)),
+        (near_table, near_blocks, near, transfer, cz_prev, cz_next, *y2, *sources, one),
         smem=(0,),
         aliases={2: 0},
         scratch=[
@@ -713,7 +771,8 @@
         *y1,
         *y2,
         *y3,
-        one,
+        lifted,
+        send,
         *extra,
     )
     potentials, _, _ = run(

time: 51.3 us -> 53.2 us (1.037)
  waiting for transfers between devices: 20.6 us -> 22.5 us
  Pallas kernels: 9.98 us -> 10.8 us
  starting transfers between devices: 19.3 us -> 18.5 us
    ppermute x15, waiting for transfers between devices: 20.6 us -> 22.5 us  [from_shift(): lax.ppermute(value, axis, [(i, (i - shift) % size) for i in range(size)])]
    pallas_call x9 -> x10, Pallas kernels: 9.98 us -> 10.8 us  [run(): pl.pallas_call(kernel, out_shape=out_shape, in_specs=[spec(i) for i in ra...]
    ppermute x15, starting transfers between devices: 19.3 us -> 18.5 us  [from_shift(): lax.ppermute(value, axis, [(i, (i - shift) % size) for i in range(size)])]
  transfers between devices with their start and end apart: 15 -> 15, of which waited for: 6 -> 5; matrix products, arithmetic and copies ran while one was open for 0% -> 0% of each run, Pallas kernels for 10% -> 11%
where the time goes in v5:
time: 53.2 us; the launch traced here: 53.1 us
  waiting for transfers between devices  22.5 us (42%)
  starting transfers between devices  18.5 us (35%)
  Pallas kernels  10.8 us (20%)
  local copies, waits for them, and re-layouts  1.03 us (2%)
    ppermute x15, waiting for transfers between devices, from_shift(): lax.ppermute(value, axis, [(i, (i - shift) % size) for i in range(size)])  22.5 us
    ppermute x15, starting transfers between devices, from_shift(): lax.ppermute(value, axis, [(i, (i - shift) % size) for i in range(size)])  18.5 us
    pallas_call x10, Pallas kernels, run(): pl.pallas_call(kernel, out_shape=out_shape, in_specs=[spec(i) for i in ra...  10.8 us
  transfers between devices with their start and end apart: 15, of which 5 were waited for; matrix products, arithmetic and copies ran while one was open for 0% of the time, Pallas kernels for 11%

profile of v5, /device:TPU:0, one launch (start us, length us, event | category | flops | bytes accessed | tf_op | source)
XLA Modules:
  0.0 53.1 jit_solution(14580189692433700494)
XLA Ops:
  0.0 0.0 copy-start.8
  0.0 0.0 copy-start
  0.0 0.0 copy-start.5
  0.0 0.0 copy-start.3
  0.0 0.0 copy-start.4
  0.0 0.0 copy-start.2
  0.0 0.7 %copy-done.8 = s32[4,4,4]{2,1,0:T(4,128)S(1)} copy-done((s32[4,4,4]{2,1,0:T(4,128)S(1)}, s32[4,4,4]{2,1,0:T(4,128)}, u32[]{:S(2)}) %copy-start.8) | copy-done | bytes 280
  0.7 0.0 copy-start.1
  0.7 0.0 copy-start.7
  0.7 0.1 fusion.live.refs_1_
  0.8 0.1 copy-done
  0.9 0.0 copy-done.5
  0.9 0.2 copy-done.3
  1.1 1.0 %shard_map.92 = (bf16[4,4,4,32,128]{4,3,2,1,0:T(8,128)(2,1)S(1)}, bf16[2,4,4,32,128]{4,3,2,1,0:T(8,128)(2,1)S(1)}, bf16[18,48,128]{2,1,0:T(8,128)(2,1)S(1)}, bf1...) custom-call(s32[8,128]{1,0:T(8,128)S(1)} %shard_map.91.token, ...), custom_call_target="tpu_custom_call" | custom-call | tf_op jit(solution)/shard_map/pallas_call | solution.py:38
  2.2 3.0 %collective-permute-start = (bf16[2,4,4,32,128]{4,3,2,1,0:T(8,128)(2,1)S(1)}, bf16[2,4,4,32,128]{4,3,2,1,0:T(8,128)(2,1)S(1)}, u32[]{:S(2)}, u32[]{:S(2)}) collective-permute-start(bf16[2,4,4,32,128]{4,3,2,1,0:T(8,128)(2,1)S(1)} %get-tuple-element.35), channel_id=1, source_target_pairs={{0,16},{16,0},{1,17},{17,1},{2,18},{18,2},{3,19},{19,3},{4,20},{20... | collective-permute-start | bytes 786440 | tf_op jit(solution)/shard_map/ppermute | solution.py:16
  5.1 1.6 %collective-permute-start.3 = (bf16[448,128]{1,0:T(8,128)(2,1)S(1)}, bf16[448,128]{1,0:T(8,128)(2,1)S(1)}, u32[]{:S(2)}, u32[]{:S(2)}) collective-permute-start(bf16[448,128]{1,0:T(8,128)(2,1)S(1)} %get-tuple-element.39), channel_id=1, source_target_pairs={{0,1},{1,2},{2,3},{3,0},{4,5},{5,6},{6,7},{7,4},{8,9},{9,10},{10,1... | collective-permute-start | bytes 344072 | tf_op jit(solution)/shard_map/ppermute | solution.py:16
  6.7 2.2 %collective-permute-start.4 = (bf16[448,128]{1,0:T(8,128)(2,1)S(1)}, bf16[448,128]{1,0:T(8,128)(2,1)S(1)}, u32[]{:S(2)}, u32[]{:S(2)}) collective-permute-start(bf16[448,128]{1,0:T(8,128)(2,1)S(1)} %get-tuple-element.40), channel_id=1, source_target_pairs={{0,3},{1,0},{2,1},{3,2},{4,7},{5,4},{6,5},{7,6},{8,11},{9,8},{10,9... | collective-permute-start | bytes 344072 | tf_op jit(solution)/shard_map/ppermute | solution.py:16
  9.0 3.9 %collective-permute-done.3.refs_3_.refs_2_ = bf16[448,128]{1,0:T(8,128)(2,1)S(1)} collective-permute-done((bf16[448,128]{1,0:T(8,128)(2,1)S(1)}, bf16[448,128]{1,0:T(8,128)(2,1)S(1)}, u32[]{:S(2)}, u32[]{:S(2)}) %collective-permute-start.3) | collective-permute-done | bytes 114720 | tf_op jit(solution)/shard_map/ppermute | solution.py:16
  12.9 0.6 %collective-permute-done.4.refs_4_.refs_3_ = bf16[448,128]{1,0:T(8,128)(2,1)S(1)} collective-permute-done((bf16[448,128]{1,0:T(8,128)(2,1)S(1)}, bf16[448,128]{1,0:T(8,128)(2,1)S(1)}, u32[]{:S(2)}, u32[]{:S(2)}) %collective-permute-start.4) | collective-permute-done | bytes 114720 | tf_op jit(solution)/shard_map/ppermute | solution.py:16
  13.5 0.0 collective-permute-done.refs_3_.refs_1_.refs_0_
  13.5 0.1 shard_map.94
  13.6 0.6 %collective-permute-start.10 = (bf16[32,48,128]{2,1,0:T(8,128)(2,1)S(1)}, bf16[32,48,128]{2,1,0:T(8,128)(2,1)S(1)}, u32[]{:S(2)}, u32[]{:S(2)}) collective-permute-start(bf16[32,48,128]{2,1,0:T(8,128)(2,1)S(1)} %get-tuple-element.46.refs_8_), channel_id=1, source_target_pairs={{0,16},{16,0},{1,17},{17,1},{2,18},{18,2},{3,19},{19,3},{4,20},{20... | collective-permute-start | bytes 1179656 | tf_op jit(solution)/shard_map/ppermute | solution.py:16
  14.2 1.1 %collective-permute-start.5 = (bf16[4,6,32,128]{3,2,1,0:T(8,128)(2,1)S(1)}, bf16[4,6,32,128]{3,2,1,0:T(8,128)(2,1)S(1)}, u32[]{:S(2)}, u32[]{:S(2)}) collective-permute-start(bf16[4,6,32,128]{3,2,1,0:T(8,128)(2,1)S(1)} %get-tuple-element.41), channel_id=1, source_target_pairs={{0,1},{1,2},{2,3},{3,0},{4,5},{5,6},{6,7},{7,4},{8,9},{9,10},{10,1... | collective-permute-start | bytes 589832 | tf_op jit(solution)/shard_map/ppermute | solution.py:16
  15.3 2.7 %collective-permute-start.6 = (bf16[4,6,32,128]{3,2,1,0:T(8,128)(2,1)S(1)}, bf16[4,6,32,128]{3,2,1,0:T(8,128)(2,1)S(1)}, u32[]{:S(2)}, u32[]{:S(2)}) collective-permute-start(bf16[4,6,32,128]{3,2,1,0:T(8,128)(2,1)S(1)} %get-tuple-element.42), channel_id=1, source_target_pairs={{0,3},{1,0},{2,1},{3,2},{4,7},{5,4},{6,5},{7,6},{8,11},{9,8},{10,9... | collective-permute-start | bytes 589832 | tf_op jit(solution)/shard_map/ppermute | solution.py:16
  18.0 0.0 collective-permute-start.1
  18.0 0.0 collective-permute-start.7
  18.0 7.6 %collective-permute-done.7.refs_5_ = bf16[16,128]{1,0:T(8,128)(2,1)S(1)} collective-permute-done((bf16[16,128]{1,0:T(8,128)(2,1)S(1)}, bf16[16,128]{1,0:T(8,128)(2,1)S(1)}, u32[]{:S(2)}, u32[]{:S(2)}) %collective-permute-start.7) | collective-permute-done | bytes 4128 | tf_op jit(solution)/shard_map/ppermute | solution.py:16
  25.6 0.0 collective-permute-start.2
  25.6 0.4 shard_map.95
  26.0 0.0 collective-permute-done.5.refs_4_.refs_0_
  26.0 0.6 %collective-permute-start.8 = (bf16[880,128]{1,0:T(8,128)(2,1)S(1)}, bf16[880,128]{1,0:T(8,128)(2,1)S(1)}, u32[]{:S(2)}, u32[]{:S(2)}) collective-permute-start(bf16[880,128]{1,0:T(8,128)(2,1)S(1)} %get-tuple-element.44), channel_id=1, source_target_pairs={{0,4},{4,8},{8,12},{12,0},{1,5},{5,9},{9,13},{13,1},{2,6},{6,10},{... | collective-permute-start | bytes 675848 | tf_op jit(solution)/shard_map/ppermute | solution.py:16
  26.5 0.0 collective-permute-done.6.refs_5_.refs_1_
  26.5 1.2 %collective-permute-start.9 = (bf16[880,128]{1,0:T(8,128)(2,1)S(1)}, bf16[880,128]{1,0:T(8,128)(2,1)S(1)}, u32[]{:S(2)}, u32[]{:S(2)}) collective-permute-start(bf16[880,128]{1,0:T(8,128)(2,1)S(1)} %get-tuple-element.45), channel_id=1, source_target_pairs={{0,12},{4,0},{8,4},{12,8},{1,13},{5,1},{9,5},{13,9},{2,14},{6,2},{... | collective-permute-start | bytes 675848 | tf_op jit(solution)/shard_map/ppermute | solution.py:16
  27.8 0.0 collective-permute-done.10.refs_9_.refs_2_
  27.8 0.1 collective-permute-start.13
  27.9 0.0 collective-permute-done.1.refs_4_.refs_2_.refs_12_
  27.9 1.7 %collective-permute-start.14 = (bf16[1152,128]{1,0:T(8,128)(2,1)S(1)}, bf16[1152,128]{1,0:T(8,128)(2,1)S(1)}, u32[]{:S(2)}, u32[]{:S(2)}) collective-permute-start(bf16[1152,128]{1,0:T(8,128)(2,1)S(1)} %get-tuple-element.60), channel_id=1, source_target_pairs={{0,12},{4,0},{8,4},{12,8},{1,13},{5,1},{9,5},{13,9},{2,14},{6,2},{... | collective-permute-start | bytes 884744 | tf_op jit(solution)/shard_map/ppermute | solution.py:16
  29.6 1.1 %collective-permute-done.2.refs_5_.refs_3_.refs_13_ = bf16[992,128]{1,0:T(8,128)(2,1)S(1)} collective-permute-done((bf16[992,128]{1,0:T(8,128)(2,1)S(1)}, bf16[992,128]{1,0:T(8,128)(2,1)S(1)}, u32[]{:S(2)}, u32[]{:S(2)}) %collective-permute-start.2) | collective-permute-done | bytes 253984 | tf_op jit(solution)/shard_map/ppermute | solution.py:16
  30.8 2.3 %collective-permute-start.11 = (bf16[1,48,128]{2,1,0:T(8,128)(2,1)S(1)}, bf16[1,48,128]{2,1,0:T(8,128)(2,1)S(1)}, u32[]{:S(2)}, u32[]{:S(2)}) collective-permute-start(bf16[1,48,128]{2,1,0:T(8,128)(2,1)S(1)} %get-tuple-element.48.refs_6_), channel_id=1, source_target_pairs={{0,8},{4,12},{8,0},{12,4},{1,9},{5,13},{9,1},{13,5},{2,10},{6,14},... | collective-permute-start | bytes 36872 | tf_op jit(solution)/shard_map/ppermute | solution.py:16
  33.0 0.0 copy-done.4
  33.0 0.0 copy-done.2
  33.0 0.4 shard_map.98
  33.5 9.2 %collective-permute-done.11.refs_7_ = bf16[1,48,128]{2,1,0:T(8,128)(2,1)S(1)} collective-permute-done((bf16[1,48,128]{2,1,0:T(8,128)(2,1)S(1)}, bf16[1,48,128]{2,1,0:T(8,128)(2,1)S(1)}, u32[]{:S(2)}, u32[]{:S(2)}) %collective-permute-start.11) | collective-permute-done | bytes 12320 | tf_op jit(solution)/shard_map/ppermute | solution.py:16
  42.7 0.0 collective-permute-done.8.refs_4_.refs_6_.refs_14_
  42.7 0.0 collective-permute-done.9.refs_5_.refs_7_.refs_15_
  42.7 0.1 shard_map.96
  42.7 1.4 %collective-permute-start.12 = (bf16[18,48,128]{2,1,0:T(8,128)(2,1)S(1)}, bf16[18,48,128]{2,1,0:T(8,128)(2,1)S(1)}, u32[]{:S(2)}, u32[]{:S(2)}) collective-permute-start(bf16[18,48,128]{2,1,0:T(8,128)(2,1)S(1)} %get-tuple-element.58.refs_19_), channel_id=1, source_target_pairs={{0,16},{16,0},{1,17},{17,1},{2,18},{18,2},{3,19},{19,3},{4,20},{20... | collective-permute-start | bytes 663560 | tf_op jit(solution)/shard_map/ppermute | solution.py:16
  44.2 0.0 copy-done.1
  44.2 0.0 copy-done.7
  44.2 0.0 copy-start.6
  44.2 2.7 %shard_map.93.refs_2_ = f32[4,512,128]{2,1,0:T(8,128)S(1)} custom-call(s32[3,27]{1,0:T(4,128)S(1)} %bitcast.3, bf16[27,128,128]{2,1,0:T(8,128)(2,1)S(1)} %copy-done.1, bf16[4,4,4,32,128]{4,3,2,1,0:T(8,128)(2,1)S(1)} %get-tuple-element.34.refs_2_.refs_0_, bf16[2,4,4,32,128]{4,3,2,1,0:T(8,128)(2,1)S(1)} %collective-permute-done.refs_3_.refs_1_.refs_0_, ...), custom_call_target="tpu_custom_call" | custom-call | flops 1811939328 | tf_op jit(solution)/shard_map/pallas_call | solution.py:38
  46.9 2.0 %shard_map.97 = (f32[4,512,128]{2,1,0:T(8,128)S(1)}, bf16[320,48,128]{2,1,0:T(8,128)(2,1)S(1)}, bf16[150,48,128]{2,1,0:T(8,128)(2,1)S(1)}, bf16[2,2,128,384]{3,2,1,0:T(8,128)(2,1)S(1)}, bf16[4,48,128]{2,1,0:T(8,128)(2,1)S(1)}) custom-call(s32[3,27]{1,0:T(4,128)S(1)} %bitcast.4, bf16[27,128,128]{2,1,0:T(8,128)(2,1)S(1)} %copy-done.1, ...), custom_call_target="tpu_custom_call", output_to_operand_aliasing={{0}: (2, {})} | custom-call | flops 603979776 | tf_op jit(solution)/shard_map/pallas_call | solution.py:38
  48.9 0.0 collective-permute-done.12.refs_11_
  48.9 0.0 collective-permute-done.13.refs_16_
  48.9 0.0 collective-permute-done.14.refs_17_
  49.0 0.0 copy-done.6
  49.0 4.1 %shard_map.100 = (f32[4,4,4,32,128]{4,3,2,1,0:T(8,128)}, bf16[320,48,128]{2,1,0:T(8,128)(2,1)S(1)}, bf16[150,48,128]{2,1,0:T(8,128)(2,1)S(1)}) custom-call(s32[3,2,32]{2,1,0:T(2,128)S(1)} %bitcast.2, f32[4,4,4,128]{3,2,1,0:T(4,128)S(1)} %fusion.live.refs_1_, ...), custom_call_target="tpu_custom_call", output_to_operand_aliasing={{1}: (9, {}), {2}: (10, {})} | custom-call | tf_op jit(solution)/shard_map/pallas_call | solution.py:38
  (2 shorter events, 0.0 us)
Async XLA Ops:
  0.0 0.7 %copy-start.8 = (s32[4,4,4]{2,1,0:T(4,128)S(1)}, s32[4,4,4]{2,1,0:T(4,128)}, u32[]{:S(2)}) copy-start(s32[4,4,4]{2,1,0:T(4,128)} %param.10) | copy-start | bytes 772
  0.0 0.9 %copy-start = (bf16[8,48,48]{2,1,0:T(8,128)(2,1)S(1)}, bf16[8,48,48]{2,1,0:T(8,128)(2,1)}, u32[]{:S(2)}) copy-start(bf16[8,48,48]{2,1,0:T(8,128)(2,1)} %transfer.3) | copy-start | bytes 110596
  0.0 0.9 %copy-start.5 = (bf16[48,128]{1,0:T(8,128)(2,1)S(1)}, bf16[48,128]{1,0:T(8,128)(2,1)}, u32[]{:S(2)}) copy-start(bf16[48,128]{1,0:T(8,128)(2,1)} %refs_4_.1) | copy-start | bytes 36868
  0.0 1.1 %copy-start.3 = (bf16[4,4,4,32,128]{4,3,2,1,0:T(8,128)(2,1)S(1)}, bf16[4,4,4,32,128]{4,3,2,1,0:T(8,128)(2,1)}, u32[]{:S(2)}) copy-start(bf16[4,4,4,32,128]{4,3,2,1,0:T(8,128)(2,1)} %charges.1) | copy-start | bytes 1572868
  0.0 33.0 %copy-start.4 = (bf16[2,4,4,48,48]{4,3,2,1,0:T(8,128)(2,1)S(1)}, bf16[2,4,4,48,48]{4,3,2,1,0:T(8,128)(2,1)}, u32[]{:S(2)}) copy-start(bf16[2,4,4,48,48]{4,3,2,1,0:T(8,128)(2,1)} %coarse_in.1) | copy-start | bytes 442372
  0.0 33.0 %copy-start.2 = (bf16[2,32,48,48]{3,2,1,0:T(8,128)(2,1)S(1)}, bf16[2,32,48,48]{3,2,1,0:T(8,128)(2,1)}, u32[]{:S(2)}) copy-start(bf16[2,32,48,48]{3,2,1,0:T(8,128)(2,1)} %coupling_in.1) | copy-start | bytes 884740
  0.7 43.5 %copy-start.1 = (bf16[27,128,128]{2,1,0:T(8,128)(2,1)S(1)}, bf16[27,128,128]{2,1,0:T(8,128)(2,1)}, u32[]{:S(2)}) copy-start(bf16[27,128,128]{2,1,0:T(8,128)(2,1)} %refs_1_.5) | copy-start | bytes 2654212
  0.7 43.5 %copy-start.7 = (s32[27,3]{0,1:T(4,128)S(1)}, s32[27,3]{0,1:T(4,128)}, u32[]{:S(2)}) copy-start(s32[27,3]{0,1:T(4,128)} %param.11) | copy-start | bytes 976
  2.2 11.3 %collective-permute-start = (bf16[2,4,4,32,128]{4,3,2,1,0:T(8,128)(2,1)S(1)}, bf16[2,4,4,32,128]{4,3,2,1,0:T(8,128)(2,1)S(1)}, u32[]{:S(2)}, u32[]{:S(2)}) collective-permute-start(bf16[2,4,4,32,128]{4,3,2,1,0:T(8,128)(2,1)S(1)} %get-tuple-element.35), channel_id=1, source_target_pairs={{0,16},{16,0},{1,17},{17,1},{2,18},{18,2},{3,19},{19,3},{4,20},{20... | collective-permute-start | bytes 786440 | tf_op jit(solution)/shard_map/ppermute | solution.py:16
  5.1 7.7 %collective-permute-start.3 = (bf16[448,128]{1,0:T(8,128)(2,1)S(1)}, bf16[448,128]{1,0:T(8,128)(2,1)S(1)}, u32[]{:S(2)}, u32[]{:S(2)}) collective-permute-start(bf16[448,128]{1,0:T(8,128)(2,1)S(1)} %get-tuple-element.39), channel_id=1, source_target_pairs={{0,1},{1,2},{2,3},{3,0},{4,5},{5,6},{6,7},{7,4},{8,9},{9,10},{10,1... | collective-permute-start | bytes 344072 | tf_op jit(solution)/shard_map/ppermute | solution.py:16
  6.7 6.8 %collective-permute-start.4 = (bf16[448,128]{1,0:T(8,128)(2,1)S(1)}, bf16[448,128]{1,0:T(8,128)(2,1)S(1)}, u32[]{:S(2)}, u32[]{:S(2)}) collective-permute-start(bf16[448,128]{1,0:T(8,128)(2,1)S(1)} %get-tuple-element.40), channel_id=1, source_target_pairs={{0,3},{1,0},{2,1},{3,2},{4,7},{5,4},{6,5},{7,6},{8,11},{9,8},{10,9... | collective-permute-start | bytes 344072 | tf_op jit(solution)/shard_map/ppermute | solution.py:16
  13.6 14.2 %collective-permute-start.10 = (bf16[32,48,128]{2,1,0:T(8,128)(2,1)S(1)}, bf16[32,48,128]{2,1,0:T(8,128)(2,1)S(1)}, u32[]{:S(2)}, u32[]{:S(2)}) collective-permute-start(bf16[32,48,128]{2,1,0:T(8,128)(2,1)S(1)} %get-tuple-element.46.refs_8_), channel_id=1, source_target_pairs={{0,16},{16,0},{1,17},{17,1},{2,18},{18,2},{3,19},{19,3},{4,20},{20... | collective-permute-start | bytes 1179656 | tf_op jit(solution)/shard_map/ppermute | solution.py:16
  14.2 11.8 %collective-permute-start.5 = (bf16[4,6,32,128]{3,2,1,0:T(8,128)(2,1)S(1)}, bf16[4,6,32,128]{3,2,1,0:T(8,128)(2,1)S(1)}, u32[]{:S(2)}, u32[]{:S(2)}) collective-permute-start(bf16[4,6,32,128]{3,2,1,0:T(8,128)(2,1)S(1)} %get-tuple-element.41), channel_id=1, source_target_pairs={{0,1},{1,2},{2,3},{3,0},{4,5},{5,6},{6,7},{7,4},{8,9},{9,10},{10,1... | collective-permute-start | bytes 589832 | tf_op jit(solution)/shard_map/ppermute | solution.py:16
  15.3 11.3 %collective-permute-start.6 = (bf16[4,6,32,128]{3,2,1,0:T(8,128)(2,1)S(1)}, bf16[4,6,32,128]{3,2,1,0:T(8,128)(2,1)S(1)}, u32[]{:S(2)}, u32[]{:S(2)}) collective-permute-start(bf16[4,6,32,128]{3,2,1,0:T(8,128)(2,1)S(1)} %get-tuple-element.42), channel_id=1, source_target_pairs={{0,3},{1,0},{2,1},{3,2},{4,7},{5,4},{6,5},{7,6},{8,11},{9,8},{10,9... | collective-permute-start | bytes 589832 | tf_op jit(solution)/shard_map/ppermute | solution.py:16
  18.0 9.9 %collective-permute-start.1 = (bf16[992,128]{1,0:T(8,128)(2,1)S(1)}, bf16[992,128]{1,0:T(8,128)(2,1)S(1)}, u32[]{:S(2)}, u32[]{:S(2)}) collective-permute-start(bf16[992,128]{1,0:T(8,128)(2,1)S(1)} %get-tuple-element.36), channel_id=1, source_target_pairs={{0,4},{4,8},{8,12},{12,0},{1,5},{5,9},{9,13},{13,1},{2,6},{6,10},{... | collective-permute-start | bytes 761864 | tf_op jit(solution)/shard_map/ppermute | solution.py:16
  18.0 7.6 %collective-permute-start.7 = (bf16[16,128]{1,0:T(8,128)(2,1)S(1)}, bf16[16,128]{1,0:T(8,128)(2,1)S(1)}, u32[]{:S(2)}, u32[]{:S(2)}) collective-permute-start(bf16[16,128]{1,0:T(8,128)(2,1)S(1)} %get-tuple-element.43.refs_4_), channel_id=1, source_target_pairs={{0,2},{1,3},{2,0},{3,1},{4,6},{5,7},{6,4},{7,5},{8,10},{9,11},{10,... | collective-permute-start | bytes 12296 | tf_op jit(solution)/shard_map/ppermute | solution.py:16
  25.6 5.2 %collective-permute-start.2 = (bf16[992,128]{1,0:T(8,128)(2,1)S(1)}, bf16[992,128]{1,0:T(8,128)(2,1)S(1)}, u32[]{:S(2)}, u32[]{:S(2)}) collective-permute-start(bf16[992,128]{1,0:T(8,128)(2,1)S(1)} %get-tuple-element.37), channel_id=1, source_target_pairs={{0,12},{4,0},{8,4},{12,8},{1,13},{5,1},{9,5},{13,9},{2,14},{6,2},{... | collective-permute-start | bytes 761864 | tf_op jit(solution)/shard_map/ppermute | solution.py:16
  26.0 16.7 %collective-permute-start.8 = (bf16[880,128]{1,0:T(8,128)(2,1)S(1)}, bf16[880,128]{1,0:T(8,128)(2,1)S(1)}, u32[]{:S(2)}, u32[]{:S(2)}) collective-permute-start(bf16[880,128]{1,0:T(8,128)(2,1)S(1)} %get-tuple-element.44), channel_id=1, source_target_pairs={{0,4},{4,8},{8,12},{12,0},{1,5},{5,9},{9,13},{13,1},{2,6},{6,10},{... | collective-permute-start | bytes 675848 | tf_op jit(solution)/shard_map/ppermute | solution.py:16
  26.5 16.1 %collective-permute-start.9 = (bf16[880,128]{1,0:T(8,128)(2,1)S(1)}, bf16[880,128]{1,0:T(8,128)(2,1)S(1)}, u32[]{:S(2)}, u32[]{:S(2)}) collective-permute-start(bf16[880,128]{1,0:T(8,128)(2,1)S(1)} %get-tuple-element.45), channel_id=1, source_target_pairs={{0,12},{4,0},{8,4},{12,8},{1,13},{5,1},{9,5},{13,9},{2,14},{6,2},{... | collective-permute-start | bytes 675848 | tf_op jit(solution)/shard_map/ppermute | solution.py:16
  27.8 21.1 %collective-permute-start.13 = (bf16[1152,128]{1,0:T(8,128)(2,1)S(1)}, bf16[1152,128]{1,0:T(8,128)(2,1)S(1)}, u32[]{:S(2)}, u32[]{:S(2)}) collective-permute-start(bf16[1152,128]{1,0:T(8,128)(2,1)S(1)} %get-tuple-element.59), channel_id=1, source_target_pairs={{0,4},{4,8},{8,12},{12,0},{1,5},{5,9},{9,13},{13,1},{2,6},{6,10},{... | collective-permute-start | bytes 884744 | tf_op jit(solution)/shard_map/ppermute | solution.py:16
  27.9 21.0 %collective-permute-start.14 = (bf16[1152,128]{1,0:T(8,128)(2,1)S(1)}, bf16[1152,128]{1,0:T(8,128)(2,1)S(1)}, u32[]{:S(2)}, u32[]{:S(2)}) collective-permute-start(bf16[1152,128]{1,0:T(8,128)(2,1)S(1)} %get-tuple-element.60), channel_id=1, source_target_pairs={{0,12},{4,0},{8,4},{12,8},{1,13},{5,1},{9,5},{13,9},{2,14},{6,2},{... | collective-permute-start | bytes 884744 | tf_op jit(solution)/shard_map/ppermute | solution.py:16
  30.8 11.9 %collective-permute-start.11 = (bf16[1,48,128]{2,1,0:T(8,128)(2,1)S(1)}, bf16[1,48,128]{2,1,0:T(8,128)(2,1)S(1)}, u32[]{:S(2)}, u32[]{:S(2)}) collective-permute-start(bf16[1,48,128]{2,1,0:T(8,128)(2,1)S(1)} %get-tuple-element.48.refs_6_), channel_id=1, source_target_pairs={{0,8},{4,12},{8,0},{12,4},{1,9},{5,13},{9,1},{13,5},{2,10},{6,14},... | collective-permute-start | bytes 36872 | tf_op jit(solution)/shard_map/ppermute | solution.py:16
  42.7 6.2 %collective-permute-start.12 = (bf16[18,48,128]{2,1,0:T(8,128)(2,1)S(1)}, bf16[18,48,128]{2,1,0:T(8,128)(2,1)S(1)}, u32[]{:S(2)}, u32[]{:S(2)}) collective-permute-start(bf16[18,48,128]{2,1,0:T(8,128)(2,1)S(1)} %get-tuple-element.58.refs_19_), channel_id=1, source_target_pairs={{0,16},{16,0},{1,17},{17,1},{2,18},{18,2},{3,19},{19,3},{4,20},{20... | collective-permute-start | bytes 663560 | tf_op jit(solution)/shard_map/ppermute | solution.py:16
  44.2 4.8 %copy-start.6 = (s32[2,32,3]{1,0,2:T(2,128)S(1)}, s32[2,32,3]{1,0,2:T(2,128)}, u32[]{:S(2)}) copy-start(s32[2,32,3]{1,0,2:T(2,128)} %param.15) | copy-start | bytes 2308

commit v6 on v5

--- a/solution.py
+++ b/solution.py
@@ -132,7 +132,17 @@
     return jnp.concatenate([rows, roll(rows, -width), roll(rows, -2 * width)], axis=0)
 
 
-def first_kernel(token, live, charges, basis, transfer, own, faces, mom, z_high, z_low, y_high, y_low, two):
+def top(transfer, low, high, width):
+    total = None
+    for j in range(2):
+        for i in range(2):
+            part = dot(transfer[4 * i + 2 * j], low) + dot(transfer[4 * i + 2 * j + 1], high)
+            part = roll(part, -width * (2 * j + i))
+            total = part if total is None else total + part
+    return total.astype(BF16)
+
+
+def first_kernel(token, live, charges, basis, transfer, own, faces, mom, z_high, z_low):
     bx, by, bz, rhs, pts = charges.shape
     rank = basis.shape[0]
     width = rhs
@@ -145,12 +155,6 @@
                     faces[0, z, y] = value
                 if x == bx - 1:
                     faces[1, z, y] = value
-                at = (z * bx + x) * rhs
-                if y == 0:
-                    y_low[at : at + rhs] = value
-                if y == by - 1:
-                    y_high[at : at + rhs] = value
-    base = bz * bx * rhs
     leaf = {}
     for z in range(bz):
         for y in range(0, by, 2):
@@ -162,25 +166,28 @@
                 mom[z * by + y + k] = tile
                 at = (z % 2 * by + y + k) * rank
                 (z_low if z < 2 else z_high)[at : at + rank] = tile
-                at = base + (z * 2 + k) * rank
-                (y_low if y == 0 else y_high)[at : at + rank] = tile
     one = lift(transfer, [[[leaf[2 * z + l, y] for y in range(by)] for l in range(2)] for z in range(2)], width)
     for z in range(2):
         mom[bz * by + z] = one[z]
-        (z_low if z else z_high)[2 * by * rank : (2 * by + 1) * rank] = one[z]
-        at = base + (2 * bz + z) * rank
-        y_high[at : at + rank] = one[z]
-        y_low[at : at + rank] = one[z]
-    total = None
-    for j in range(2):
-        for i in range(2):
-            part = dot(transfer[4 * i + 2 * j], one[0]) + dot(transfer[4 * i + 2 * j + 1], one[1])
-            part = roll(part, -width * (2 * j + i))
-            total = part if total is None else total + part
-    total = fold(total.astype(BF16), width)
-    z_high[(2 * by + 1) * rank :] = total
-    z_low[(2 * by + 1) * rank :] = total
-    two[...] = total
+        (z_low if z else z_high)[2 * by * rank :] = one[z]
+
+
+def rest_kernel(own, mom, transfer, y_high, y_low, two):
+    bz, by, bx, rhs, pts = own.shape
+    rank = mom.shape[1]
+    rows = bx * rhs
+    base = bz * rows
+    for out, y in ((y_high, by - 1), (y_low, 0)):
+        start = by - 2 if y else 0
+        for z in range(bz):
+            out[z * rows : (z + 1) * rows] = own[z, y].reshape(rows, pts)
+            for k in range(2):
+                at = base + (z * 2 + k) * rank
+                out[at : at + rank] = mom[z * by + start + k]
+        for z in range(2):
+            at = base + (2 * bz + z) * rank
+            out[at : at + rank] = mom[bz * by + z]
+    two[...] = fold(top(transfer, mom[bz * by], mom[bz * by + 1], rhs), rhs)
 
 
 class Reader:
@@ -253,13 +260,11 @@
                 out[at : at + rank] = leaf(prev if zh < 2 else nxt, zh % 2, start + yy)
 
     def load(key):
-        if key == 0:
-            return unfold(mine[...], rhs)
         if key == 1:
-            return unfold(nxt[(2 * by + 1) * rank :, :], rhs)
+            return top(transfer, level[2], level[3], rhs)
         if key == nz - 1:
-            return unfold(prev[(2 * by + 1) * rank :, :], rhs)
-        return unfold(far[key - 2][...], rhs)
+            return top(transfer, level[0], level[1], rhs)
+        return unfold(mine[...] if key == 0 else far[key - 2][...], rhs)
 
     for t, tile in enumerate(assemble([(k, 0) for k in range(nz)], rhs, load)):
         line[t] = tile
@@ -660,9 +665,9 @@
 
     token = run(start_kernel, shape(8, 128, dtype=jnp.int32), (), flops=10**10)
     assert rank == 48
-    side = shape((2 * by + 1) * rank + 16, 128)
+    side = shape((2 * by + 1) * rank, 128)
     message = shape(bz * bx * rhs + (bz * 2 + 2) * rank, 128)
-    own, faces, mom, z_high, z_low, y_high, y_low, two = run(
+    own, faces, mom, z_high, z_low = run(
         first_kernel,
         (
             shape(bz, by, bx, rhs, pts),
@@ -670,12 +675,10 @@
             shape(bz * by + 2, rank, 128),
             side,
             side,
-            message,
-            message,
-            shape(16, 128),
         ),
         (token, live, charges, leaf_basis, transfer),
     )
+    y_high, y_low, two = run(rest_kernel, (message, message, shape(16, 128)), (own, mom, transfer))
     mz_prev = from_shift(z_high, "gz", nz, -1)
     mz_next = from_shift(z_low, "gz", nz, 1)
     if nx == 2:

time: 53.2 us -> 52.8 us (level)
  waiting for transfers between devices: 22.5 us -> 21.9 us
    ppermute x15, waiting for transfers between devices: 22.5 us -> 21.9 us  [from_shift(): lax.ppermute(value, axis, [(i, (i - shift) % size) for i in range(size)])]
    pallas_call x10 -> x11, Pallas kernels: 10.8 us -> 11.3 us  [run(): pl.pallas_call(kernel, out_shape=out_shape, in_specs=[spec(i) for i in ra...]
  transfers between devices with their start and end apart: 15 -> 15, of which waited for: 5 -> 5; matrix products, arithmetic and copies ran while one was open for 0% -> 0% of each run, Pallas kernels for 11% -> 12%
where the time goes in v6:
time: 52.8 us; the launch traced here: 52.6 us
  waiting for transfers between devices  21.9 us (41%)
  starting transfers between devices  18.2 us (34%)
  Pallas kernels  11.3 us (21%)
  local copies, waits for them, and re-layouts  1.04 us (2%)
    ppermute x15, waiting for transfers between devices, from_shift(): lax.ppermute(value, axis, [(i, (i - shift) % size) for i in range(size)])  21.9 us
    ppermute x15, starting transfers between devices, from_shift(): lax.ppermute(value, axis, [(i, (i - shift) % size) for i in range(size)])  18.2 us
    pallas_call x11, Pallas kernels, run(): pl.pallas_call(kernel, out_shape=out_shape, in_specs=[spec(i) for i in ra...  11.3 us
  transfers between devices with their start and end apart: 15, of which 5 were waited for; matrix products, arithmetic and copies ran while one was open for 0% of the time, Pallas kernels for 12%

profile of v6, /device:TPU:0, one launch (start us, length us, event | category | flops | bytes accessed | tf_op | source)
XLA Modules:
  0.0 52.6 jit_solution(1708907894905351406)
XLA Ops:
  0.0 0.0 copy-start.8
  0.0 0.0 copy-start
  0.0 0.0 copy-start.5
  0.0 0.0 copy-start.3
  0.0 0.7 %copy-done.8 = s32[4,4,4]{2,1,0:T(4,128)S(1)} copy-done((s32[4,4,4]{2,1,0:T(4,128)S(1)}, s32[4,4,4]{2,1,0:T(4,128)}, u32[]{:S(2)}) %copy-start.8) | copy-done | bytes 280
  0.7 0.0 copy-start.2
  0.7 0.0 copy-start.4
  0.7 0.0 copy-start.1
  0.7 0.0 copy-start.7
  0.7 0.1 fusion.live.refs_1_
  0.8 0.1 copy-done
  0.9 0.0 copy-done.5
  0.9 0.2 copy-done.3
  1.1 0.7 %shard_map.92 = (bf16[4,4,4,32,128]{4,3,2,1,0:T(8,128)(2,1)S(1)}, bf16[2,4,4,32,128]{4,3,2,1,0:T(8,128)(2,1)S(1)}, bf16[18,48,128]{2,1,0:T(8,128)(2,1)S(1)}, bf1...) custom-call(s32[8,128]{1,0:T(8,128)S(1)} %shard_map.91.token, f32[4,4,4,128]{3,2,1,0:T(4,128)S(1)} %fusion.live.refs_1_, ...), custom_call_target="tpu_custom_call" | custom-call | tf_op jit(solution)/shard_map/pallas_call | solution.py:38
  1.8 3.0 %collective-permute-start = (bf16[2,4,4,32,128]{4,3,2,1,0:T(8,128)(2,1)S(1)}, bf16[2,4,4,32,128]{4,3,2,1,0:T(8,128)(2,1)S(1)}, u32[]{:S(2)}, u32[]{:S(2)}) collective-permute-start(bf16[2,4,4,32,128]{4,3,2,1,0:T(8,128)(2,1)S(1)} %get-tuple-element.35), channel_id=1, source_target_pairs={{0,16},{16,0},{1,17},{17,1},{2,18},{18,2},{3,19},{19,3},{4,20},{20... | collective-permute-start | bytes 786440 | tf_op jit(solution)/shard_map/ppermute | solution.py:16
  4.9 1.6 %collective-permute-start.3 = (bf16[432,128]{1,0:T(8,128)(2,1)S(1)}, bf16[432,128]{1,0:T(8,128)(2,1)S(1)}, u32[]{:S(2)}, u32[]{:S(2)}) collective-permute-start(bf16[432,128]{1,0:T(8,128)(2,1)S(1)} %get-tuple-element.39), channel_id=1, source_target_pairs={{0,1},{1,2},{2,3},{3,0},{4,5},{5,6},{6,7},{7,4},{8,9},{9,10},{10,1... | collective-permute-start | bytes 331784 | tf_op jit(solution)/shard_map/ppermute | solution.py:16
  6.4 2.2 %collective-permute-start.4 = (bf16[432,128]{1,0:T(8,128)(2,1)S(1)}, bf16[432,128]{1,0:T(8,128)(2,1)S(1)}, u32[]{:S(2)}, u32[]{:S(2)}) collective-permute-start(bf16[432,128]{1,0:T(8,128)(2,1)S(1)} %get-tuple-element.40), channel_id=1, source_target_pairs={{0,3},{1,0},{2,1},{3,2},{4,7},{5,4},{6,5},{7,6},{8,11},{9,8},{10,9... | collective-permute-start | bytes 331784 | tf_op jit(solution)/shard_map/ppermute | solution.py:16
  8.7 3.8 %collective-permute-done.3.refs_3_.refs_2_ = bf16[432,128]{1,0:T(8,128)(2,1)S(1)} collective-permute-done((bf16[432,128]{1,0:T(8,128)(2,1)S(1)}, bf16[432,128]{1,0:T(8,128)(2,1)S(1)}, u32[]{:S(2)}, u32[]{:S(2)}) %collective-permute-start.3) | collective-permute-done | bytes 110624 | tf_op jit(solution)/shard_map/ppermute | solution.py:16
  12.5 0.6 %collective-permute-done.4.refs_4_.refs_3_ = bf16[432,128]{1,0:T(8,128)(2,1)S(1)} collective-permute-done((bf16[432,128]{1,0:T(8,128)(2,1)S(1)}, bf16[432,128]{1,0:T(8,128)(2,1)S(1)}, u32[]{:S(2)}, u32[]{:S(2)}) %collective-permute-start.4) | collective-permute-done | bytes 110624 | tf_op jit(solution)/shard_map/ppermute | solution.py:16
  13.1 0.0 collective-permute-done.refs_3_.refs_1_.refs_0_
  13.1 0.1 shard_map.95
  13.1 0.6 %collective-permute-start.10 = (bf16[32,48,128]{2,1,0:T(8,128)(2,1)S(1)}, bf16[32,48,128]{2,1,0:T(8,128)(2,1)S(1)}, u32[]{:S(2)}, u32[]{:S(2)}) collective-permute-start(bf16[32,48,128]{2,1,0:T(8,128)(2,1)S(1)} %get-tuple-element.46.refs_8_), channel_id=1, source_target_pairs={{0,16},{16,0},{1,17},{17,1},{2,18},{18,2},{3,19},{19,3},{4,20},{20... | collective-permute-start | bytes 1179656 | tf_op jit(solution)/shard_map/ppermute | solution.py:16
  13.7 1.1 %collective-permute-start.5 = (bf16[4,6,32,128]{3,2,1,0:T(8,128)(2,1)S(1)}, bf16[4,6,32,128]{3,2,1,0:T(8,128)(2,1)S(1)}, u32[]{:S(2)}, u32[]{:S(2)}) collective-permute-start(bf16[4,6,32,128]{3,2,1,0:T(8,128)(2,1)S(1)} %get-tuple-element.41), channel_id=1, source_target_pairs={{0,1},{1,2},{2,3},{3,0},{4,5},{5,6},{6,7},{7,4},{8,9},{9,10},{10,1... | collective-permute-start | bytes 589832 | tf_op jit(solution)/shard_map/ppermute | solution.py:16
  14.8 2.7 %collective-permute-start.6 = (bf16[4,6,32,128]{3,2,1,0:T(8,128)(2,1)S(1)}, bf16[4,6,32,128]{3,2,1,0:T(8,128)(2,1)S(1)}, u32[]{:S(2)}, u32[]{:S(2)}) collective-permute-start(bf16[4,6,32,128]{3,2,1,0:T(8,128)(2,1)S(1)} %get-tuple-element.42), channel_id=1, source_target_pairs={{0,3},{1,0},{2,1},{3,2},{4,7},{5,4},{6,5},{7,6},{8,11},{9,8},{10,9... | collective-permute-start | bytes 589832 | tf_op jit(solution)/shard_map/ppermute | solution.py:16
  17.5 0.3 shard_map.93
  17.9 0.0 collective-permute-start.1
  17.9 0.2 collective-permute-start.7
  18.1 7.1 %collective-permute-done.7.refs_5_ = bf16[16,128]{1,0:T(8,128)(2,1)S(1)} collective-permute-done((bf16[16,128]{1,0:T(8,128)(2,1)S(1)}, bf16[16,128]{1,0:T(8,128)(2,1)S(1)}, u32[]{:S(2)}, u32[]{:S(2)}) %collective-permute-start.7) | collective-permute-done | bytes 4128 | tf_op jit(solution)/shard_map/ppermute | solution.py:16
  25.2 0.3 collective-permute-start.2
  25.5 0.8 %shard_map.96 = (bf16[880,128]{1,0:T(8,128)(2,1)S(1)}, bf16[880,128]{1,0:T(8,128)(2,1)S(1)}, bf16[1,48,128]{2,1,0:T(8,128)(2,1)S(1)}, bf16[4,48,128]{2,1,0:T(8,128)(2,1)S(1)}) custom-call(bf16[2,4,4,32,128]{4,3,2,1,0:T(8,128)(2,1)S(1)} %collective-permute-done.refs_3_.refs_1_.refs_0_, bf16[8,48,48]{2,1,0:T(8,128)(2,1)S(1)} %copy-done, ...), custom_call_target="tpu_custom_call" | custom-call | tf_op jit(solution)/shard_map/pallas_call | solution.py:38
  26.3 0.0 collective-permute-done.5.refs_4_.refs_0_
  26.3 0.2 collective-permute-start.8
  26.6 0.0 collective-permute-done.6.refs_5_.refs_1_
  26.6 1.6 %collective-permute-start.9 = (bf16[880,128]{1,0:T(8,128)(2,1)S(1)}, bf16[880,128]{1,0:T(8,128)(2,1)S(1)}, u32[]{:S(2)}, u32[]{:S(2)}) collective-permute-start(bf16[880,128]{1,0:T(8,128)(2,1)S(1)} %get-tuple-element.45), channel_id=1, source_target_pairs={{0,12},{4,0},{8,4},{12,8},{1,13},{5,1},{9,5},{13,9},{2,14},{6,2},{... | collective-permute-start | bytes 675848 | tf_op jit(solution)/shard_map/ppermute | solution.py:16
  28.1 0.0 collective-permute-done.10.refs_9_.refs_2_
  28.2 0.1 collective-permute-start.13
  28.2 0.0 collective-permute-done.1.refs_4_.refs_2_.refs_12_
  28.3 1.7 %collective-permute-start.14 = (bf16[1152,128]{1,0:T(8,128)(2,1)S(1)}, bf16[1152,128]{1,0:T(8,128)(2,1)S(1)}, u32[]{:S(2)}, u32[]{:S(2)}) collective-permute-start(bf16[1152,128]{1,0:T(8,128)(2,1)S(1)} %get-tuple-element.60), channel_id=1, source_target_pairs={{0,12},{4,0},{8,4},{12,8},{1,13},{5,1},{9,5},{13,9},{2,14},{6,2},{... | collective-permute-start | bytes 884744 | tf_op jit(solution)/shard_map/ppermute | solution.py:16
  30.0 0.5 %collective-permute-done.2.refs_5_.refs_3_.refs_13_ = bf16[992,128]{1,0:T(8,128)(2,1)S(1)} collective-permute-done((bf16[992,128]{1,0:T(8,128)(2,1)S(1)}, bf16[992,128]{1,0:T(8,128)(2,1)S(1)}, u32[]{:S(2)}, u32[]{:S(2)}) %collective-permute-start.2) | collective-permute-done | bytes 253984 | tf_op jit(solution)/shard_map/ppermute | solution.py:16
  30.5 1.6 %collective-permute-start.11 = (bf16[1,48,128]{2,1,0:T(8,128)(2,1)S(1)}, bf16[1,48,128]{2,1,0:T(8,128)(2,1)S(1)}, u32[]{:S(2)}, u32[]{:S(2)}) collective-permute-start(bf16[1,48,128]{2,1,0:T(8,128)(2,1)S(1)} %get-tuple-element.48.refs_6_), channel_id=1, source_target_pairs={{0,8},{4,12},{8,0},{12,4},{1,9},{5,13},{9,1},{13,5},{2,10},{6,14},... | collective-permute-start | bytes 36872 | tf_op jit(solution)/shard_map/ppermute | solution.py:16
  32.1 0.0 copy-done.2
  32.2 0.0 copy-done.4
  32.2 0.4 shard_map.99
  32.6 9.8 %collective-permute-done.11.refs_7_ = bf16[1,48,128]{2,1,0:T(8,128)(2,1)S(1)} collective-permute-done((bf16[1,48,128]{2,1,0:T(8,128)(2,1)S(1)}, bf16[1,48,128]{2,1,0:T(8,128)(2,1)S(1)}, u32[]{:S(2)}, u32[]{:S(2)}) %collective-permute-start.11) | collective-permute-done | bytes 12320 | tf_op jit(solution)/shard_map/ppermute | solution.py:16
  42.4 0.0 collective-permute-done.8.refs_4_.refs_6_.refs_14_
  42.4 0.0 collective-permute-done.9.refs_5_.refs_7_.refs_15_
  42.4 0.1 shard_map.97
  42.5 1.2 %collective-permute-start.12 = (bf16[18,48,128]{2,1,0:T(8,128)(2,1)S(1)}, bf16[18,48,128]{2,1,0:T(8,128)(2,1)S(1)}, u32[]{:S(2)}, u32[]{:S(2)}) collective-permute-start(bf16[18,48,128]{2,1,0:T(8,128)(2,1)S(1)} %get-tuple-element.58.refs_19_), channel_id=1, source_target_pairs={{0,16},{16,0},{1,17},{17,1},{2,18},{18,2},{3,19},{19,3},{4,20},{20... | collective-permute-start | bytes 663560 | tf_op jit(solution)/shard_map/ppermute | solution.py:16
  43.7 0.0 copy-done.1
  43.7 0.0 copy-done.7
  43.7 0.0 copy-start.6
  43.7 2.7 %shard_map.94.refs_2_ = f32[4,512,128]{2,1,0:T(8,128)S(1)} custom-call(s32[3,27]{1,0:T(4,128)S(1)} %bitcast.3, bf16[27,128,128]{2,1,0:T(8,128)(2,1)S(1)} %copy-done.1, bf16[4,4,4,32,128]{4,3,2,1,0:T(8,128)(2,1)S(1)} %get-tuple-element.34.own.refs_2_.refs_0_, bf16[2,4,4,32,128]{4,3,2,1,0:T(8,128)(2,1)S(1)} %collective-permute-done.refs_3_.refs_1_.refs_0_, ...), custom_call_target="tpu_custom_call" | custom-call | flops 1811939328 | tf_op jit(solution)/shard_map/pallas_call | solution.py:38
  46.4 2.0 %shard_map.98 = (f32[4,512,128]{2,1,0:T(8,128)S(1)}, bf16[320,48,128]{2,1,0:T(8,128)(2,1)S(1)}, bf16[150,48,128]{2,1,0:T(8,128)(2,1)S(1)}, bf16[2,2,128,384]{3,2,1,0:T(8,128)(2,1)S(1)}, bf16[4,48,128]{2,1,0:T(8,128)(2,1)S(1)}) custom-call(s32[3,27]{1,0:T(4,128)S(1)} %bitcast.4, bf16[27,128,128]{2,1,0:T(8,128)(2,1)S(1)} %copy-done.1, ...), custom_call_target="tpu_custom_call", output_to_operand_aliasing={{0}: (2, {})} | custom-call | flops 603979776 | tf_op jit(solution)/shard_map/pallas_call | solution.py:38
  48.5 0.0 collective-permute-done.12.refs_11_
  48.5 0.0 collective-permute-done.13.refs_16_
  48.5 0.0 collective-permute-done.14.refs_17_
  48.5 0.0 copy-done.6
  48.5 4.1 %shard_map.101 = (f32[4,4,4,32,128]{4,3,2,1,0:T(8,128)}, bf16[320,48,128]{2,1,0:T(8,128)(2,1)S(1)}, bf16[150,48,128]{2,1,0:T(8,128)(2,1)S(1)}) custom-call(s32[3,2,32]{2,1,0:T(2,128)S(1)} %bitcast.2, f32[4,4,4,128]{3,2,1,0:T(4,128)S(1)} %fusion.live.refs_1_, ...), custom_call_target="tpu_custom_call", output_to_operand_aliasing={{1}: (9, {}), {2}: (10, {})} | custom-call | tf_op jit(solution)/shard_map/pallas_call | solution.py:38
  (2 shorter events, 0.0 us)
Async XLA Ops:
  0.0 0.7 %copy-start.8 = (s32[4,4,4]{2,1,0:T(4,128)S(1)}, s32[4,4,4]{2,1,0:T(4,128)}, u32[]{:S(2)}) copy-start(s32[4,4,4]{2,1,0:T(4,128)} %param.10) | copy-start | bytes 772
  0.0 0.9 %copy-start = (bf16[8,48,48]{2,1,0:T(8,128)(2,1)S(1)}, bf16[8,48,48]{2,1,0:T(8,128)(2,1)}, u32[]{:S(2)}) copy-start(bf16[8,48,48]{2,1,0:T(8,128)(2,1)} %transfer.5) | copy-start | bytes 110596
  0.0 0.9 %copy-start.5 = (bf16[48,128]{1,0:T(8,128)(2,1)S(1)}, bf16[48,128]{1,0:T(8,128)(2,1)}, u32[]{:S(2)}) copy-start(bf16[48,128]{1,0:T(8,128)(2,1)} %refs_4_.1) | copy-start | bytes 36868
  0.0 1.1 %copy-start.3 = (bf16[4,4,4,32,128]{4,3,2,1,0:T(8,128)(2,1)S(1)}, bf16[4,4,4,32,128]{4,3,2,1,0:T(8,128)(2,1)}, u32[]{:S(2)}) copy-start(bf16[4,4,4,32,128]{4,3,2,1,0:T(8,128)(2,1)} %charges.1) | copy-start | bytes 1572868
  0.7 31.5 %copy-start.2 = (bf16[2,32,48,48]{3,2,1,0:T(8,128)(2,1)S(1)}, bf16[2,32,48,48]{3,2,1,0:T(8,128)(2,1)}, u32[]{:S(2)}) copy-start(bf16[2,32,48,48]{3,2,1,0:T(8,128)(2,1)} %coupling_in.1) | copy-start | bytes 884740
  0.7 31.5 %copy-start.4 = (bf16[2,4,4,48,48]{4,3,2,1,0:T(8,128)(2,1)S(1)}, bf16[2,4,4,48,48]{4,3,2,1,0:T(8,128)(2,1)}, u32[]{:S(2)}) copy-start(bf16[2,4,4,48,48]{4,3,2,1,0:T(8,128)(2,1)} %coarse_in.1) | copy-start | bytes 442372
  0.7 43.0 %copy-start.1 = (bf16[27,128,128]{2,1,0:T(8,128)(2,1)S(1)}, bf16[27,128,128]{2,1,0:T(8,128)(2,1)}, u32[]{:S(2)}) copy-start(bf16[27,128,128]{2,1,0:T(8,128)(2,1)} %refs_1_.5) | copy-start | bytes 2654212
  0.7 43.0 %copy-start.7 = (s32[27,3]{0,1:T(4,128)S(1)}, s32[27,3]{0,1:T(4,128)}, u32[]{:S(2)}) copy-start(s32[27,3]{0,1:T(4,128)} %param.11) | copy-start | bytes 976
  1.8 11.2 %collective-permute-start = (bf16[2,4,4,32,128]{4,3,2,1,0:T(8,128)(2,1)S(1)}, bf16[2,4,4,32,128]{4,3,2,1,0:T(8,128)(2,1)S(1)}, u32[]{:S(2)}, u32[]{:S(2)}) collective-permute-start(bf16[2,4,4,32,128]{4,3,2,1,0:T(8,128)(2,1)S(1)} %get-tuple-element.35), channel_id=1, source_target_pairs={{0,16},{16,0},{1,17},{17,1},{2,18},{18,2},{3,19},{19,3},{4,20},{20... | collective-permute-start | bytes 786440 | tf_op jit(solution)/shard_map/ppermute | solution.py:16
  4.9 7.6 %collective-permute-start.3 = (bf16[432,128]{1,0:T(8,128)(2,1)S(1)}, bf16[432,128]{1,0:T(8,128)(2,1)S(1)}, u32[]{:S(2)}, u32[]{:S(2)}) collective-permute-start(bf16[432,128]{1,0:T(8,128)(2,1)S(1)} %get-tuple-element.39), channel_id=1, source_target_pairs={{0,1},{1,2},{2,3},{3,0},{4,5},{5,6},{6,7},{7,4},{8,9},{9,10},{10,1... | collective-permute-start | bytes 331784 | tf_op jit(solution)/shard_map/ppermute | solution.py:16
  6.4 6.6 %collective-permute-start.4 = (bf16[432,128]{1,0:T(8,128)(2,1)S(1)}, bf16[432,128]{1,0:T(8,128)(2,1)S(1)}, u32[]{:S(2)}, u32[]{:S(2)}) collective-permute-start(bf16[432,128]{1,0:T(8,128)(2,1)S(1)} %get-tuple-element.40), channel_id=1, source_target_pairs={{0,3},{1,0},{2,1},{3,2},{4,7},{5,4},{6,5},{7,6},{8,11},{9,8},{10,9... | collective-permute-start | bytes 331784 | tf_op jit(solution)/shard_map/ppermute | solution.py:16
  13.1 15.0 %collective-permute-start.10 = (bf16[32,48,128]{2,1,0:T(8,128)(2,1)S(1)}, bf16[32,48,128]{2,1,0:T(8,128)(2,1)S(1)}, u32[]{:S(2)}, u32[]{:S(2)}) collective-permute-start(bf16[32,48,128]{2,1,0:T(8,128)(2,1)S(1)} %get-tuple-element.46.refs_8_), channel_id=1, source_target_pairs={{0,16},{16,0},{1,17},{17,1},{2,18},{18,2},{3,19},{19,3},{4,20},{20... | collective-permute-start | bytes 1179656 | tf_op jit(solution)/shard_map/ppermute | solution.py:16
  13.7 12.6 %collective-permute-start.5 = (bf16[4,6,32,128]{3,2,1,0:T(8,128)(2,1)S(1)}, bf16[4,6,32,128]{3,2,1,0:T(8,128)(2,1)S(1)}, u32[]{:S(2)}, u32[]{:S(2)}) collective-permute-start(bf16[4,6,32,128]{3,2,1,0:T(8,128)(2,1)S(1)} %get-tuple-element.41), channel_id=1, source_target_pairs={{0,1},{1,2},{2,3},{3,0},{4,5},{5,6},{6,7},{7,4},{8,9},{9,10},{10,1... | collective-permute-start | bytes 589832 | tf_op jit(solution)/shard_map/ppermute | solution.py:16
  14.8 11.7 %collective-permute-start.6 = (bf16[4,6,32,128]{3,2,1,0:T(8,128)(2,1)S(1)}, bf16[4,6,32,128]{3,2,1,0:T(8,128)(2,1)S(1)}, u32[]{:S(2)}, u32[]{:S(2)}) collective-permute-start(bf16[4,6,32,128]{3,2,1,0:T(8,128)(2,1)S(1)} %get-tuple-element.42), channel_id=1, source_target_pairs={{0,3},{1,0},{2,1},{3,2},{4,7},{5,4},{6,5},{7,6},{8,11},{9,8},{10,9... | collective-permute-start | bytes 589832 | tf_op jit(solution)/shard_map/ppermute | solution.py:16
  17.9 10.4 %collective-permute-start.1 = (bf16[992,128]{1,0:T(8,128)(2,1)S(1)}, bf16[992,128]{1,0:T(8,128)(2,1)S(1)}, u32[]{:S(2)}, u32[]{:S(2)}) collective-permute-start(bf16[992,128]{1,0:T(8,128)(2,1)S(1)} %get-tuple-element.37), channel_id=1, source_target_pairs={{0,4},{4,8},{8,12},{12,0},{1,5},{5,9},{9,13},{13,1},{2,6},{6,10},{... | collective-permute-start | bytes 761864 | tf_op jit(solution)/shard_map/ppermute | solution.py:16
  17.9 7.3 %collective-permute-start.7 = (bf16[16,128]{1,0:T(8,128)(2,1)S(1)}, bf16[16,128]{1,0:T(8,128)(2,1)S(1)}, u32[]{:S(2)}, u32[]{:S(2)}) collective-permute-start(bf16[16,128]{1,0:T(8,128)(2,1)S(1)} %get-tuple-element.43.refs_4_), channel_id=1, source_target_pairs={{0,2},{1,3},{2,0},{3,1},{4,6},{5,7},{6,4},{7,5},{8,10},{9,11},{10,... | collective-permute-start | bytes 12296 | tf_op jit(solution)/shard_map/ppermute | solution.py:16
  25.2 5.3 %collective-permute-start.2 = (bf16[992,128]{1,0:T(8,128)(2,1)S(1)}, bf16[992,128]{1,0:T(8,128)(2,1)S(1)}, u32[]{:S(2)}, u32[]{:S(2)}) collective-permute-start(bf16[992,128]{1,0:T(8,128)(2,1)S(1)} %get-tuple-element.38), channel_id=1, source_target_pairs={{0,12},{4,0},{8,4},{12,8},{1,13},{5,1},{9,5},{13,9},{2,14},{6,2},{... | collective-permute-start | bytes 761864 | tf_op jit(solution)/shard_map/ppermute | solution.py:16
  26.3 16.1 %collective-permute-start.8 = (bf16[880,128]{1,0:T(8,128)(2,1)S(1)}, bf16[880,128]{1,0:T(8,128)(2,1)S(1)}, u32[]{:S(2)}, u32[]{:S(2)}) collective-permute-start(bf16[880,128]{1,0:T(8,128)(2,1)S(1)} %get-tuple-element.44), channel_id=1, source_target_pairs={{0,4},{4,8},{8,12},{12,0},{1,5},{5,9},{9,13},{13,1},{2,6},{6,10},{... | collective-permute-start | bytes 675848 | tf_op jit(solution)/shard_map/ppermute | solution.py:16
  26.6 15.8 %collective-permute-start.9 = (bf16[880,128]{1,0:T(8,128)(2,1)S(1)}, bf16[880,128]{1,0:T(8,128)(2,1)S(1)}, u32[]{:S(2)}, u32[]{:S(2)}) collective-permute-start(bf16[880,128]{1,0:T(8,128)(2,1)S(1)} %get-tuple-element.45), channel_id=1, source_target_pairs={{0,12},{4,0},{8,4},{12,8},{1,13},{5,1},{9,5},{13,9},{2,14},{6,2},{... | collective-permute-start | bytes 675848 | tf_op jit(solution)/shard_map/ppermute | solution.py:16
  28.2 20.3 %collective-permute-start.13 = (bf16[1152,128]{1,0:T(8,128)(2,1)S(1)}, bf16[1152,128]{1,0:T(8,128)(2,1)S(1)}, u32[]{:S(2)}, u32[]{:S(2)}) collective-permute-start(bf16[1152,128]{1,0:T(8,128)(2,1)S(1)} %get-tuple-element.59), channel_id=1, source_target_pairs={{0,4},{4,8},{8,12},{12,0},{1,5},{5,9},{9,13},{13,1},{2,6},{6,10},{... | collective-permute-start | bytes 884744 | tf_op jit(solution)/shard_map/ppermute | solution.py:16
  28.3 20.2 %collective-permute-start.14 = (bf16[1152,128]{1,0:T(8,128)(2,1)S(1)}, bf16[1152,128]{1,0:T(8,128)(2,1)S(1)}, u32[]{:S(2)}, u32[]{:S(2)}) collective-permute-start(bf16[1152,128]{1,0:T(8,128)(2,1)S(1)} %get-tuple-element.60), channel_id=1, source_target_pairs={{0,12},{4,0},{8,4},{12,8},{1,13},{5,1},{9,5},{13,9},{2,14},{6,2},{... | collective-permute-start | bytes 884744 | tf_op jit(solution)/shard_map/ppermute | solution.py:16
  30.5 11.9 %collective-permute-start.11 = (bf16[1,48,128]{2,1,0:T(8,128)(2,1)S(1)}, bf16[1,48,128]{2,1,0:T(8,128)(2,1)S(1)}, u32[]{:S(2)}, u32[]{:S(2)}) collective-permute-start(bf16[1,48,128]{2,1,0:T(8,128)(2,1)S(1)} %get-tuple-element.48.refs_6_), channel_id=1, source_target_pairs={{0,8},{4,12},{8,0},{12,4},{1,9},{5,13},{9,1},{13,5},{2,10},{6,14},... | collective-permute-start | bytes 36872 | tf_op jit(solution)/shard_map/ppermute | solution.py:16
  42.5 6.0 %collective-permute-start.12 = (bf16[18,48,128]{2,1,0:T(8,128)(2,1)S(1)}, bf16[18,48,128]{2,1,0:T(8,128)(2,1)S(1)}, u32[]{:S(2)}, u32[]{:S(2)}) collective-permute-start(bf16[18,48,128]{2,1,0:T(8,128)(2,1)S(1)} %get-tuple-element.58.refs_19_), channel_id=1, source_target_pairs={{0,16},{16,0},{1,17},{17,1},{2,18},{18,2},{3,19},{19,3},{4,20},{20... | collective-permute-start | bytes 663560 | tf_op jit(solution)/shard_map/ppermute | solution.py:16
  43.7 4.8 %copy-start.6 = (s32[2,32,3]{1,0,2:T(2,128)S(1)}, s32[2,32,3]{1,0,2:T(2,128)}, u32[]{:S(2)}) copy-start(s32[2,32,3]{1,0,2:T(2,128)} %param.15) | copy-start | bytes 2308
